TPU v7x, 32 devices: a whole 2x2x4 slice. The times are simulated.
32 devices in a mesh: groups: 2 (over x), lon: 16 (over z, y, core).
Axes of the slice: x: 2, y: 2, z: 4, core: 2. Of those that a mesh axis runs over, the one named last changes fastest.
Arguments:
- tracers: bfloat16 [2048, 64, 256], P(('groups', 'lon')), parts along dimension 0, may hold values from -6 to 6
- wind_fields: bfloat16 [2048, 64, 128], P(('groups', 'lon')), parts along dimension 0, may hold values from -3 to 3
- departures: int32 [32, 16, 2], P(('groups', 'lon')), parts along dimension 0, may hold values from -4 to 3, as said below
Outputs:
- advected: bfloat16 [2048, 64, 256], P(('groups', 'lon')), parts along dimension 0
There are 2 independent parts, one for each index of `groups`. A program takes and returns all parts, laid end to end along the dimension named above; each array names one. Nothing has to cross between parts.
Inputs may be any that keep to these rules, and one draw needn't show every extreme that they name: `departures`: entry 0 lies in -4..3 and entry 1 in -1..1 with q - entry 1 a valid band; in every sector exactly 4 bands share one value of entry 0, and no value is shared by more.
All inputs are finite; a program needn't handle non-finite values.
Results may differ from a plain program's by a relative error of at most 0.001.
Values may be sent and summed in bfloat16 or wider, within the bound.
No kernel may reach another device: no remote copies, remote signals or barrier semaphores. Data moves between devices by JAX's collectives and lax.ppermute only.
A program may use at most 128 MiB of HBM per device.

v0:
```python
import jax
import jax.numpy as jnp
from jax import lax
from jax.sharding import PartitionSpec as P

CAP = 4
TRAJ = 3


CLIP_BOUND = 0.95


def with_halo(block, sides, width):
    for axis, dim in sides:
        count = lax.axis_size(axis)
        forward = [(i, i + 1) for i in range(count - 1)]
        forward.append((count - 1, 0))
        backward = [(target, source) for source, target in forward]
        low = lax.ppermute(
            lax.slice_in_dim(block, block.shape[dim] - width, None, axis=dim), axis, forward
        )
        high = lax.ppermute(lax.slice_in_dim(block, 0, width, axis=dim), axis, backward)
        block = jnp.concatenate([low, block, high], axis=dim)
    return block


def shifted(block, axis, distance):
    devices = range(lax.axis_size(axis))
    route = [((i - distance) % len(devices), i) for i in devices]
    return lax.ppermute(block, axis, route)


def linear_kernel(distance):
    return jnp.maximum(1.0 - jnp.abs(distance), 0.0)


def cubic_kernel(distance):
    magnitude = jnp.abs(distance)
    inner_part = 0.5 * (1.0 - magnitude) * (2.0 - magnitude) * (1.0 + magnitude)
    outer_part = -(magnitude - 1.0) * (2.0 - magnitude) * (3.0 - magnitude) / 6.0
    return jnp.where(magnitude < 1.0, inner_part, jnp.where(magnitude < 2.0, outer_part, 0.0))


def advect_tile(source_tile, arrival_wind):
    columns = source_tile.shape[0] - 4
    band_rows = source_tile.shape[1] - 4
    levels = arrival_wind.shape[-1] // 2
    tracer_ch = source_tile.shape[-1] - 4 * levels
    per_level = tracer_ch // levels
    wind_data = source_tile[:, :, tracer_ch:].astype(jnp.float32)
    extrapolated = 2.0 * wind_data[:, :, : 2 * levels] - wind_data[:, :, 2 * levels :]
    wind_here = arrival_wind.astype(jnp.float32)
    displace = jnp.clip(wind_here, -CLIP_BOUND, CLIP_BOUND)
    for iteration in range(TRAJ):
        lon_shift = displace[:, :, :levels]
        lat_shift = displace[:, :, levels:]
        accumulated = jnp.zeros_like(wind_here)
        for lat_step in (-1, 0, 1):
            lat_weight = linear_kernel(lat_step + lat_shift)
            for lon_step in (-1, 0, 1):
                weight = linear_kernel(lon_step + lon_shift) * lat_weight
                window = extrapolated[
                    2 + lon_step : 2 + lon_step + columns,
                    2 + lat_step : 2 + lat_step + band_rows,
                    :,
                ]
                accumulated = accumulated + jnp.concatenate([weight, weight], -1) * window
        displace = jnp.clip(0.5 * (wind_here + accumulated), -CLIP_BOUND, CLIP_BOUND)
    lon_shift = displace[:, :, :levels]
    lat_shift = displace[:, :, levels:]
    result = jnp.zeros((columns, band_rows, tracer_ch), jnp.float32)
    for lat_step in range(-2, 3):
        lat_dist = lat_step + lat_shift
        lat_weight = cubic_kernel(lat_dist)
        inner_rows = jnp.abs(lat_dist) < 1.0
        for lon_step in range(-2, 3):
            lon_dist = lon_step + lon_shift
            lon_weight = jnp.where(inner_rows, cubic_kernel(lon_dist), linear_kernel(lon_dist))
            weight = jnp.repeat(lon_weight * lat_weight, per_level, axis=-1)
            window = source_tile[
                2 + lon_step : 2 + lon_step + columns,
                2 + lat_step : 2 + lat_step + band_rows,
                :tracer_ch,
            ]
            result = result + weight * window.astype(jnp.float32)
    return result.astype(jnp.bfloat16)


def slot_bands(table_row, offset, capacity):
    matches = (table_row[:, 0] == offset).astype(jnp.int32)
    ordinal = jnp.cumsum(matches) - 1
    slot_index = jnp.arange(capacity, dtype=jnp.int32)
    picked = matches[None, :] * (ordinal[None, :] == slot_index[:, None]).astype(jnp.int32)
    band_ids = jnp.arange(table_row.shape[0], dtype=jnp.int32)
    return jnp.sum(picked * band_ids[None, :], axis=1)


def source_tiles(padded, table_row, offset, capacity, band_rows):
    chosen = slot_bands(table_row, offset, capacity)
    starts = (chosen - table_row[chosen, 1]) * band_rows

    def cut_tile(start_row):
        return lax.dynamic_slice_in_dim(padded, start_row, band_rows + 4, 1)

    return jax.vmap(cut_tile)(starts)


def on_device(tracers, wind_fields, departures):
    levels = wind_fields.shape[-1] // 4
    tracer_ch = tracers.shape[-1]
    columns = tracers.shape[0]
    band_count = departures.shape[1]
    band_rows = tracers.shape[1] // band_count
    capacity = CAP
    combined = jnp.concatenate([tracers, wind_fields], -1)
    combined = with_halo(combined, (("lon", 0),), 2)
    padded = jnp.concatenate(
        [combined[:, :1], combined[:, :1], combined, combined[:, -1:], combined[:, -1:]], 1
    )
    own_row = departures[0]
    table_rows = []
    for offset in range(-4, 4):
        if offset == 0:
            table_rows.append(own_row)
        else:
            table_rows.append(shifted(departures, "lon", -offset)[0])
    lon_tiles = own_row[:, 0]
    band_ids = jnp.arange(band_count, dtype=jnp.int32)
    earlier = (lon_tiles[:, None] == lon_tiles[None, :]) & (band_ids[None, :] < band_ids[:, None])
    position = (lon_tiles + 4) * capacity + jnp.sum(earlier.astype(jnp.int32), axis=1)
    arrival_all = wind_fields[:, :, : 2 * levels].reshape(
        columns, band_count, band_rows, 2 * levels
    )
    received = []
    for offset in range(-4, 4):
        outgoing = source_tiles(padded, table_rows[4 + offset], offset, capacity, band_rows)
        received.append(shifted(outgoing, "lon", offset))
    gathered = jnp.concatenate(received, 0)

    def advect_band(band_index):
        return advect_tile(gathered[position[band_index]], arrival_all[:, band_index])

    moved = lax.map(advect_band, band_ids)
    moved = jnp.transpose(moved, (1, 0, 2, 3))
    return moved.reshape(columns, band_count * band_rows, tracer_ch)


def solution(mesh):
    placed = (
        P(("groups", "lon"), None, None),
        P(("groups", "lon"), None, None),
        P(("groups", "lon"), None, None),
    )
    return jax.shard_map(
        on_device,
        mesh=mesh,
        in_specs=placed,
        out_specs=P(("groups", "lon"), None, None),
        check_vma=False,
    )
```

profile of v0, /device:TPU:0, one launch (start us, length us, event | category | flops | bytes accessed | tf_op | source)
XLA Modules:
  0.0 439.0 jit_solution(14753818186789090102)
XLA Ops:
  0.0 3.1 collective-permute-start.2
  6.0 3.7 collective-permute-start.11
  11.1 2.8 copy_dynamic-update-slice_fusion
  21.9 3.0 collective-permute-start.1
  27.1 1.9 pad_maximum_fusion
  30.3 3.1 constant_dynamic-update-slice_fusion.1
  34.6 3.0 gather_fusion.1
  39.0 3.0 gather_fusion.3
  44.0 3.0 gather_fusion.5
  48.4 2.4 collective-permute-start.7
  52.9 3.0 gather_fusion.7
  59.1 3.0 gather_fusion.9
  63.5 13.5 %collective-permute-start.10 = (bf16[4,68,8,384]{3,2,1,0:T(8,128)(2,1)}, bf16[4,68,8,384]{3,2,1,0:T(8,128)(2,1)}, u32[]{:S(2)}, u32[]{:S(2)}) collective-permute-start(bf16[4,68,8,384]{3,2,1,0:T(8,128)(2,1)} %copy.64), channel_id=1, source_target_pairs={{0,0},{1,1},{2,2},{3,3},{4,4},{5,5},{6,6},{7,7},{8,8},{9,9},{10,10... | collective-permute-start | bytes 5013512 | tf_op jit(solution)/shard_map/ppermute | solution.py:30
  77.0 3.0 gather_fusion.11
  82.3 3.0 gather_fusion.13
  86.7 25.3 %collective-permute-done.5 = bf16[4,68,8,384]{3,2,1,0:T(8,128)(2,1)} collective-permute-done((bf16[4,68,8,384]{3,2,1,0:T(8,128)(2,1)}, bf16[4,68,8,384]{3,2,1,0:T(8,128)(2,1)}, u32[]{:S(2)}, u32[]{:S(2)}) %collective-permute-start.5) | collective-permute-done | bytes 1671200 | tf_op jit(solution)/shard_map/ppermute | solution.py:30
  112.0 2.1 collective-permute-start.14
  114.2 3.0 gather_fusion.15
  118.6 28.6 %collective-permute-done.7 = bf16[4,68,8,384]{3,2,1,0:T(8,128)(2,1)} collective-permute-done((bf16[4,68,8,384]{3,2,1,0:T(8,128)(2,1)}, bf16[4,68,8,384]{3,2,1,0:T(8,128)(2,1)}, u32[]{:S(2)}, u32[]{:S(2)}) %collective-permute-start.7) | collective-permute-done | bytes 1671200 | tf_op jit(solution)/shard_map/ppermute | solution.py:30
  147.2 22.0 %collective-permute-start.16 = (bf16[4,68,8,384]{3,2,1,0:T(8,128)(2,1)}, bf16[4,68,8,384]{3,2,1,0:T(8,128)(2,1)S(1)}, u32[]{:S(2)}, u32[]{:S(2)}) collective-permute-start(bf16[4,68,8,384]{3,2,1,0:T(8,128)(2,1)} %copy.70), channel_id=1, source_target_pairs={{13,0},{14,1},{15,2},{0,3},{1,4},{2,5},{3,6},{4,7},{5,8},{6,9},{7,... | collective-permute-start | bytes 5013512 | tf_op jit(solution)/shard_map/ppermute | solution.py:30
  169.3 1.6 copy.80
  171.1 2.8 constant_dynamic-update-slice_fusion.9
  173.9 2.8 constant_dynamic-update-slice_fusion.8
  176.7 2.8 constant_dynamic-update-slice_fusion.7
  179.5 2.8 constant_dynamic-update-slice_fusion.6
  182.3 2.8 constant_dynamic-update-slice_fusion.5
  185.1 2.9 constant_dynamic-update-slice_fusion.4
  188.0 14.2 %collective-permute-done.14 = bf16[4,68,8,384]{3,2,1,0:T(8,128)(2,1)} collective-permute-done((bf16[4,68,8,384]{3,2,1,0:T(8,128)(2,1)}, bf16[4,68,8,384]{3,2,1,0:T(8,128)(2,1)}, u32[]{:S(2)}, u32[]{:S(2)}) %collective-permute-start.14) | collective-permute-done | bytes 1671200 | tf_op jit(solution)/shard_map/ppermute | solution.py:30
  202.2 2.8 constant_dynamic-update-slice_fusion.3
  205.0 18.3 %collective-permute-done.16 = bf16[4,68,8,384]{3,2,1,0:T(8,128)(2,1)S(1)} collective-permute-done((bf16[4,68,8,384]{3,2,1,0:T(8,128)(2,1)}, bf16[4,68,8,384]{3,2,1,0:T(8,128)(2,1)S(1)}, u32[]{:S(2)}, u32[]{:S(2)}) %collective-permute-start.16) | collective-permute-done | bytes 1671200 | tf_op jit(solution)/shard_map/ppermute | solution.py:30
  224.7 208.6 %while.13 = (s32[]{:T(128)}, bf16[16,64,4,256]{1,3,2,0:T(8,128)(2,1)}, s32[16]{0:T(128)S(1)}, bf16[64,16,4,64]{3,0,2,1:T(8,128)(2,1)}, s32[16]{0:T(128)S(1)}, /*...) while((s32[]{:T(128)}, bf16[16,64,4,256]{1,3,2,0:T(8,128)(2,1)}, ...), condition=%wide.region_18.19_spmd, body=%wide.region_17.18_spmd.sunk | while | flops 11304968 | bytes 12288713 | solution.py:143
  234.9 2.8 bitcast_dynamic-update-slice_fusion.2
  248.0 2.8 bitcast_dynamic-update-slice_fusion.2
  261.0 2.8 bitcast_dynamic-update-slice_fusion.2
  274.0 2.8 bitcast_dynamic-update-slice_fusion.2
  287.1 2.8 bitcast_dynamic-update-slice_fusion.2
  300.1 2.8 bitcast_dynamic-update-slice_fusion.2
  313.2 2.8 bitcast_dynamic-update-slice_fusion.2
  326.2 2.8 bitcast_dynamic-update-slice_fusion.2
  339.2 2.8 bitcast_dynamic-update-slice_fusion.2
  352.3 2.8 bitcast_dynamic-update-slice_fusion.2
  365.3 2.8 bitcast_dynamic-update-slice_fusion.2
  378.4 2.8 bitcast_dynamic-update-slice_fusion.2
  391.4 2.8 bitcast_dynamic-update-slice_fusion.2
  404.4 2.8 bitcast_dynamic-update-slice_fusion.2
  417.5 2.8 bitcast_dynamic-update-slice_fusion.2
  430.5 2.8 bitcast_dynamic-update-slice_fusion.2
  433.3 5.6 %copy.74 = bf16[64,64,256]{2,1,0:T(8,128)(2,1)} copy(bf16[64,64,256]{0,2,1:T(8,128)(2,1)} %bitcast.80) | data formatting | bytes 4194304 | tf_op jit(solution)/shard_map/reshape | solution.py:145
  (421 shorter events, 135.3 us)
Async XLA Ops:
  0.0 15.9 %copy-start = (s32[1,16,2]{1,2,0:T(2,128)S(1)}, s32[1,16,2]{1,2,0:T(2,128)}, u32[]{:S(2)}) copy-start(s32[1,16,2]{1,2,0:T(2,128)} %param.7) | copy-start | bytes 388
  0.0 13.9 %copy-start.1 = (bf16[64,64,128]{2,1,0:T(8,128)(2,1)S(1)}, bf16[64,64,128]{2,1,0:T(8,128)(2,1)}, u32[]{:S(2)}) copy-start(bf16[64,64,128]{2,1,0:T(8,128)(2,1)} %param.6) | copy-start | bytes 3145732
  0.0 16.6 %collective-permute-start.2 = (s32[1,16,2]{1,2,0:T(2,128)}, s32[1,16,2]{1,2,0:T(2,128)S(1)}, u32[]{:S(2)}, u32[]{:S(2)}) collective-permute-start(s32[1,16,2]{1,2,0:T(2,128)} %param.7), channel_id=1, source_target_pairs={{12,0},{13,1},{14,2},{15,3},{0,4},{1,5},{2,6},{3,7},{4,8},{5,9},{6... | collective-permute-start | bytes 392 | tf_op jit(solution)/shard_map/ppermute | solution.py:30
  3.1 15.1 %collective-permute-start.4 = (s32[1,16,2]{1,2,0:T(2,128)}, s32[1,16,2]{1,2,0:T(2,128)S(1)}, u32[]{:S(2)}, u32[]{:S(2)}) collective-permute-start(s32[1,16,2]{1,2,0:T(2,128)} %param.7), channel_id=1, source_target_pairs={{13,0},{14,1},{15,2},{0,3},{1,4},{2,5},{3,6},{4,7},{5,8},{6,9},{7,... | collective-permute-start | bytes 392 | tf_op jit(solution)/shard_map/ppermute | solution.py:30
  3.7 15.6 %collective-permute-start.6 = (s32[1,16,2]{1,2,0:T(2,128)}, s32[1,16,2]{1,2,0:T(2,128)S(1)}, u32[]{:S(2)}, u32[]{:S(2)}) collective-permute-start(s32[1,16,2]{1,2,0:T(2,128)} %param.7), channel_id=1, source_target_pairs={{14,0},{15,1},{0,2},{1,3},{2,4},{3,5},{4,6},{5,7},{6,8},{7,9},{8,1... | collective-permute-start | bytes 392 | tf_op jit(solution)/shard_map/ppermute | solution.py:30
  5.3 16.6 %collective-permute-start.8 = (s32[1,16,2]{1,2,0:T(2,128)}, s32[1,16,2]{1,2,0:T(2,128)S(1)}, u32[]{:S(2)}, u32[]{:S(2)}) collective-permute-start(s32[1,16,2]{1,2,0:T(2,128)} %param.7), channel_id=1, source_target_pairs={{15,0},{0,1},{1,2},{2,3},{3,4},{4,5},{5,6},{6,7},{7,8},{8,9},{9,10... | collective-permute-start | bytes 392 | tf_op jit(solution)/shard_map/ppermute | solution.py:30
  6.0 19.3 %collective-permute-start.11 = (s32[1,16,2]{1,2,0:T(2,128)}, s32[1,16,2]{1,2,0:T(2,128)S(1)}, u32[]{:S(2)}, u32[]{:S(2)}) collective-permute-start(s32[1,16,2]{1,2,0:T(2,128)} %param.7), channel_id=1, source_target_pairs={{1,0},{2,1},{3,2},{4,3},{5,4},{6,5},{7,6},{8,7},{9,8},{10,9},{11,1... | collective-permute-start | bytes 392 | tf_op jit(solution)/shard_map/ppermute | solution.py:30
  16.6 8.9 %collective-permute-start.13 = (s32[1,16,2]{1,2,0:T(2,128)S(1)}, s32[1,16,2]{1,2,0:T(2,128)S(1)}, u32[]{:S(2)}, u32[]{:S(2)}) collective-permute-start(s32[1,16,2]{1,2,0:T(2,128)S(1)} %copy-done), channel_id=1, source_target_pairs={{2,0},{3,1},{4,2},{5,3},{6,4},{7,5},{8,6},{9,7},{10,8},{11,9},{12,... | collective-permute-start | bytes 392 | tf_op jit(solution)/shard_map/ppermute | solution.py:30
  18.2 34.6 %collective-permute-start.15 = (s32[1,16,2]{1,2,0:T(2,128)S(1)}, s32[1,16,2]{1,2,0:T(2,128)S(1)}, u32[]{:S(2)}, u32[]{:S(2)}) collective-permute-start(s32[1,16,2]{1,2,0:T(2,128)S(1)} %copy-done), channel_id=1, source_target_pairs={{3,0},{4,1},{5,2},{6,3},{7,4},{8,5},{9,6},{10,7},{11,8},{12,9},{13... | collective-permute-start | bytes 392 | tf_op jit(solution)/shard_map/ppermute | solution.py:30
  19.3 7.1 %collective-permute-start = (bf16[2,64,384]{2,0,1:T(2,128)(2,1)}, bf16[2,64,384]{2,0,1:T(2,128)(2,1)S(1)}, u32[]{:S(2)}, u32[]{:S(2)}) collective-permute-start(bf16[2,64,384]{2,0,1:T(2,128)(2,1)} %get-tuple-element.218), channel_id=1, source_target_pairs={{0,1},{1,2},{2,3},{3,4},{4,5},{5,6},{6,7},{7,8},{8,9},{9,10},{10,1... | collective-permute-start | bytes 294920 | tf_op jit(solution)/shard_map/ppermute | solution.py:19
  21.9 5.2 %collective-permute-start.1 = (bf16[2,64,384]{2,0,1:T(2,128)(2,1)S(1)}, bf16[2,64,384]{2,0,1:T(2,128)(2,1)S(1)}, u32[]{:S(2)}, u32[]{:S(2)}) collective-permute-start(bf16[2,64,384]{2,0,1:T(2,128)(2,1)S(1)} %get-tuple-element.219), channel_id=1, source_target_pairs={{1,0},{2,1},{3,2},{4,3},{5,4},{6,5},{7,6},{8,7},{9,8},{10,9},{11,1... | collective-permute-start | bytes 294920 | tf_op jit(solution)/shard_map/ppermute | solution.py:22
  39.0 42.6 %collective-permute-start.3 = (bf16[4,68,8,384]{3,2,1,0:T(8,128)(2,1)}, bf16[4,68,8,384]{3,2,1,0:T(8,128)(2,1)S(1)}, u32[]{:S(2)}, u32[]{:S(2)}) collective-permute-start(bf16[4,68,8,384]{3,2,1,0:T(8,128)(2,1)} %copy.56), channel_id=1, source_target_pairs={{4,0},{5,1},{6,2},{7,3},{8,4},{9,5},{10,6},{11,7},{12,8},{13,9},{1... | collective-permute-start | bytes 5013512 | tf_op jit(solution)/shard_map/ppermute | solution.py:30
  43.4 68.6 %collective-permute-start.5 = (bf16[4,68,8,384]{3,2,1,0:T(8,128)(2,1)}, bf16[4,68,8,384]{3,2,1,0:T(8,128)(2,1)}, u32[]{:S(2)}, u32[]{:S(2)}) collective-permute-start(bf16[4,68,8,384]{3,2,1,0:T(8,128)(2,1)} %copy.58), channel_id=1, source_target_pairs={{3,0},{4,1},{5,2},{6,3},{7,4},{8,5},{9,6},{10,7},{11,8},{12,9},{13... | collective-permute-start | bytes 5013512 | tf_op jit(solution)/shard_map/ppermute | solution.py:30
  48.4 98.8 %collective-permute-start.7 = (bf16[4,68,8,384]{3,2,1,0:T(8,128)(2,1)}, bf16[4,68,8,384]{3,2,1,0:T(8,128)(2,1)}, u32[]{:S(2)}, u32[]{:S(2)}) collective-permute-start(bf16[4,68,8,384]{3,2,1,0:T(8,128)(2,1)} %copy.60), channel_id=1, source_target_pairs={{2,0},{3,1},{4,2},{5,3},{6,4},{7,5},{8,6},{9,7},{10,8},{11,9},{12,... | collective-permute-start | bytes 5013512 | tf_op jit(solution)/shard_map/ppermute | solution.py:30
  57.3 122.2 %collective-permute-start.9 = (bf16[4,68,8,384]{3,2,1,0:T(8,128)(2,1)}, bf16[4,68,8,384]{3,2,1,0:T(8,128)(2,1)}, u32[]{:S(2)}, u32[]{:S(2)}) collective-permute-start(bf16[4,68,8,384]{3,2,1,0:T(8,128)(2,1)} %copy.62), channel_id=1, source_target_pairs={{1,0},{2,1},{3,2},{4,3},{5,4},{6,5},{7,6},{8,7},{9,8},{10,9},{11,1... | collective-permute-start | bytes 5013512 | tf_op jit(solution)/shard_map/ppermute | solution.py:30
  63.5 118.8 %collective-permute-start.10 = (bf16[4,68,8,384]{3,2,1,0:T(8,128)(2,1)}, bf16[4,68,8,384]{3,2,1,0:T(8,128)(2,1)}, u32[]{:S(2)}, u32[]{:S(2)}) collective-permute-start(bf16[4,68,8,384]{3,2,1,0:T(8,128)(2,1)} %copy.64), channel_id=1, source_target_pairs={{0,0},{1,1},{2,2},{3,3},{4,4},{5,5},{6,6},{7,7},{8,8},{9,9},{10,10... | collective-permute-start | bytes 5013512 | tf_op jit(solution)/shard_map/ppermute | solution.py:30
  81.5 5.2 %copy-start.3 = (bf16[4,68,8,384]{3,2,1,0:T(8,128)(2,1)}, bf16[4,68,8,384]{3,2,1,0:T(8,128)(2,1)S(1)}, u32[]{:S(2)}) copy-start(bf16[4,68,8,384]{3,2,1,0:T(8,128)(2,1)S(1)} %collective-permute-done.3) | copy-start | bytes 5013508
  81.5 103.6 %collective-permute-start.12 = (bf16[4,68,8,384]{3,2,1,0:T(8,128)(2,1)}, bf16[4,68,8,384]{3,2,1,0:T(8,128)(2,1)}, u32[]{:S(2)}, u32[]{:S(2)}) collective-permute-start(bf16[4,68,8,384]{3,2,1,0:T(8,128)(2,1)} %copy.66), channel_id=1, source_target_pairs={{15,0},{0,1},{1,2},{2,3},{3,4},{4,5},{5,6},{6,7},{7,8},{8,9},{9,10... | collective-permute-start | bytes 5013512 | tf_op jit(solution)/shard_map/ppermute | solution.py:30
  86.7 82.5 %copy-start.2 = (bf16[64,64,128]{2,1,0:T(8,128)(2,1)S(1)}, bf16[64,64,128]{2,1,0:T(8,128)(2,1)}, u32[]{:S(2)}) copy-start(bf16[64,64,128]{2,1,0:T(8,128)(2,1)} %param.6) | copy-start | bytes 3145732
  112.0 90.2 %collective-permute-start.14 = (bf16[4,68,8,384]{3,2,1,0:T(8,128)(2,1)}, bf16[4,68,8,384]{3,2,1,0:T(8,128)(2,1)}, u32[]{:S(2)}, u32[]{:S(2)}) collective-permute-start(bf16[4,68,8,384]{3,2,1,0:T(8,128)(2,1)} %copy.68), channel_id=1, source_target_pairs={{14,0},{15,1},{0,2},{1,3},{2,4},{3,5},{4,6},{5,7},{6,8},{7,9},{8,1... | collective-permute-start | bytes 5013512 | tf_op jit(solution)/shard_map/ppermute | solution.py:30
  147.2 76.0 %collective-permute-start.16 = (bf16[4,68,8,384]{3,2,1,0:T(8,128)(2,1)}, bf16[4,68,8,384]{3,2,1,0:T(8,128)(2,1)S(1)}, u32[]{:S(2)}, u32[]{:S(2)}) collective-permute-start(bf16[4,68,8,384]{3,2,1,0:T(8,128)(2,1)} %copy.70), channel_id=1, source_target_pairs={{13,0},{14,1},{15,2},{0,3},{1,4},{2,5},{3,6},{4,7},{5,8},{6,9},{7,... | collective-permute-start | bytes 5013512 | tf_op jit(solution)/shard_map/ppermute | solution.py:30
where the time goes:
time: 443 us; the launch traced here: 439 us
  local copies, waits for them, and re-layouts  135 us (30%)
  other arithmetic  95.1 us (21%)
  waiting for transfers between devices  87.6 us (20%)
  loops' own time  63.9 us (14%)
  starting transfers between devices  57.2 us (13%)
    ppermute x15, waiting for transfers between devices, shifted(): return lax.ppermute(block, axis, route)  86.4 us
    another operation x1, loops' own time, on_device(): moved = lax.map(advect_band, band_ids)  63.9 us
    ppermute x15, starting transfers between devices, shifted(): return lax.ppermute(block, axis, route)  52.6 us
    dynamic_update_slice x16, other arithmetic, on_device(): moved = lax.map(advect_band, band_ids)  44.7 us
    gather x16, local copies, waits for them, and re-layouts, cut_tile(): return lax.dynamic_slice_in_dim(padded, start_row, band_rows + 4, 1)  35.3 us
    unnamed x21, local copies, waits for them, and re-layouts  26 us
    dynamic_slice x32, local copies, waits for them, and re-layouts, advect_band(): gathered[position[band_index]]  24.6 us
    min x48, other arithmetic, advect_tile(): jnp.clip(0.5 * (wind_here + accumulated), -CLIP_BOUND, CLIP_BOUND)  18.1 us
  transfers between devices with their start and end apart: 17, of which 6 were waited for; matrix products, arithmetic and copies ran while one was open for 18% of the time, Pallas kernels for 0%

commit v1 on v0

v1 whole, which is shorter than its diff:
```python
import functools

import jax
import jax.numpy as jnp
from jax import lax
from jax.experimental import pallas as pl
from jax.experimental.pallas import tpu as pltpu
from jax.sharding import PartitionSpec as P

CAP = 4
TRAJ = 3
FIRST = -4
LAST = 4
RIM = 2
LANES = 128
META = 16
CLIP_BOUND = 0.95
F32 = jnp.float32
BF16 = jnp.bfloat16


def shifted(block, axis, distance):
    count = lax.axis_size(axis)
    route = [((i - distance) % count, i) for i in range(count)]
    return lax.ppermute(block, axis, route)


def fill_slots(dep_ref, slot_ref, count_ref, bands):
    for offset in range(LAST - FIRST):
        count_ref[offset] = 0
        for slot in range(CAP):
            slot_ref[offset * CAP + slot] = -1

    def place(band, carry):
        offset = dep_ref[0, band, 0] - FIRST
        ordinal = count_ref[offset]
        slot_ref[offset * CAP + ordinal] = band
        count_ref[offset] = ordinal + 1
        return carry

    lax.fori_loop(0, bands, place, 0)


def wind_kernel(sizes, dep_ref, wind_ref, perm_ref, *rest):
    columns, rows, groups, inner, bands, band_rows = sizes
    outs = rest[: LAST - FIRST]
    wide_ref, here_ref, slot_ref, count_ref = rest[LAST - FIRST :]

    def widen(column, carry):
        wide_ref[pl.ds(column * rows, rows), :] = wind_ref[column].astype(F32)
        return carry

    lax.fori_loop(0, columns, widen, 0)
    fill_slots(dep_ref, slot_ref, count_ref, bands)
    perm = perm_ref[:, : 2 * LANES]

    def eight_rows(block, carry):
        parts = []
        for row in range(8):
            parts.append(
                jnp.concatenate(
                    [
                        wide_ref[pl.ds(g * inner * rows + block * 8 + row, inner, stride=rows), :]
                        for g in range(groups)
                    ],
                    axis=1,
                )
            )
        left = jnp.concatenate(parts, axis=0).astype(BF16)
        moved = jnp.dot(left, perm, preferred_element_type=F32)
        for comp in range(2):
            here_ref[comp, pl.ds(block * 8, 8)] = (
                moved[:, comp * LANES : (comp + 1) * LANES].reshape(8, inner, LANES).astype(BF16)
            )
        return carry

    lax.fori_loop(0, rows // 8, eight_rows, 0)
    lane = lax.broadcasted_iota(jnp.int32, (META, LANES), 1)
    size = band_rows * inner
    for offset in range(LAST - FIRST):
        meta = jnp.full((META, LANES), -1.0, F32)
        for slot in range(CAP):
            band = slot_ref[offset * CAP + slot]
            safe = jnp.maximum(band, 0)
            source = jnp.where(band >= 0, safe - dep_ref[0, safe, 1], -1)
            meta = jnp.where(lane == slot, source.astype(F32), meta)
            for comp in range(2):
                outs[offset][pl.ds((slot * 2 + comp) * size, size), :] = here_ref[
                    comp, pl.ds(safe * band_rows, band_rows)
                ].reshape(size, LANES)
        outs[offset][pl.ds(CAP * 2 * size, META), :] = meta.astype(BF16)


def prepare_kernel(
    sizes,
    tracers_ref,
    wind_ref,
    low_t_ref,
    high_t_ref,
    low_w_ref,
    high_w_ref,
    perm_ref,
    perm_w_ref,
    out_t_ref,
    out_e_ref,
    wide_t_ref,
    wide_w_ref,
    stage_t_ref,
    stage_e_ref,
    edge_t_ref,
    edge_e_ref,
    sem_ref,
    edge_sem_ref,
):
    columns, rows, groups, inner, padded_inner, per_level = sizes
    halves = tracers_ref.shape[-1] // LANES
    blocks = rows // 8

    def put(column, t_value, w_value):
        at = pl.ds(column * rows, rows)
        for half in range(halves):
            wide_t_ref[half, at, :] = t_value[:, half * LANES : (half + 1) * LANES].astype(F32)
        wide_w_ref[at, :] = w_value.astype(F32)

    def own(column, carry):
        put(column + RIM, tracers_ref[column], wind_ref[column])
        return carry

    lax.fori_loop(0, columns, own, 0)
    for column in range(RIM):
        put(column, low_t_ref[column], low_w_ref[column])
        put(columns + RIM + column, high_t_ref[column], high_w_ref[column])
    for column in range(columns + 2 * RIM, (groups - 1) * inner + padded_inner):
        at = pl.ds(column * rows, rows)
        for half in range(halves):
            wide_t_ref[half, at, :] = jnp.zeros((rows, LANES), F32)
        wide_w_ref[at, :] = jnp.zeros((rows, LANES), F32)

    def copies(block, slot):
        at = pl.ds(RIM + block * 8, 8)
        return (
            pltpu.make_async_copy(stage_t_ref.at[slot], out_t_ref.at[:, at], sem_ref.at[slot, 0]),
            pltpu.make_async_copy(stage_e_ref.at[slot], out_e_ref.at[:, at], sem_ref.at[slot, 1]),
        )

    def edge_copies(side):
        at = pl.ds(side * (rows + RIM), RIM)
        return (
            pltpu.make_async_copy(
                edge_t_ref.at[side], out_t_ref.at[:, at], edge_sem_ref.at[side, 0]
            ),
            pltpu.make_async_copy(
                edge_e_ref.at[side], out_e_ref.at[:, at], edge_sem_ref.at[side, 1]
            ),
        )

    def eight_rows(block, carry):
        slot = lax.rem(block, 2)

        @pl.when(block >= 2)
        def _():
            for copy in copies(block - 2, slot):
                copy.wait()

        parts_t = []
        parts_w = []
        for row in range(8):
            pieces_t = []
            pieces_w = []
            for g in range(groups):
                at = pl.ds(g * inner * rows + block * 8 + row, padded_inner, stride=rows)
                for half in range(halves):
                    pieces_t.append(wide_t_ref[half, at, :])
                pieces_w.append(wide_w_ref[at, :])
            parts_t.append(jnp.concatenate(pieces_t, axis=1))
            parts_w.append(jnp.concatenate(pieces_w, axis=1))
        left_t = jnp.concatenate(parts_t, axis=0).astype(BF16)
        left_w = jnp.concatenate(parts_w, axis=0).astype(BF16)
        moved_w = jnp.dot(left_w, perm_w_ref[...], preferred_element_type=F32)
        for comp in range(2):
            now = moved_w[:, comp * LANES : (comp + 1) * LANES]
            before = moved_w[:, (comp + 2) * LANES : (comp + 3) * LANES]
            stage_e_ref[slot, comp] = (2.0 * now - before).reshape(8, padded_inner, LANES)
        moved_t = lax.dot_general(
            left_t, perm_ref[...], (((1,), (1,)), ((), ())), preferred_element_type=F32
        )
        for tracer in range(per_level):
            stage_t_ref[slot, tracer] = moved_t[:, tracer * LANES : (tracer + 1) * LANES].reshape(
                8, padded_inner, LANES
            )
        for copy in copies(block, slot):
            copy.start()

        for side, which, row in ((0, 0, 0), (1, blocks - 1, 7)):

            @pl.when(block == which)
            def _():
                for repeat in range(RIM):
                    for tracer in range(per_level):
                        edge_t_ref[side, tracer, repeat] = stage_t_ref[slot, tracer, row]
                    for comp in range(2):
                        edge_e_ref[side, comp, repeat] = stage_e_ref[slot, comp, row]
                for copy in edge_copies(side):
                    copy.start()

        return carry

    lax.fori_loop(0, blocks, eight_rows, 0)
    for block in range(max(blocks - 2, 0), blocks):
        for copy in copies(block, block % 2):
            copy.wait()
    for side in range(2):
        for copy in edge_copies(side):
            copy.wait()


def cubic_weights(shift):
    e = jnp.abs(shift)
    positive = shift > 0.0
    one_less = 1.0 - e
    one_more = 1.0 + e
    two_less = 2.0 - e
    center = 0.5 * one_less * two_less * one_more
    near = 0.5 * e * two_less * one_more
    across = e * one_less * (-1.0 / 6.0)
    beyond = across * two_less
    far = across * one_more
    zero = jnp.zeros_like(e)
    return (
        jnp.where(positive, far, zero),
        jnp.where(positive, near, beyond),
        center,
        jnp.where(positive, beyond, near),
        jnp.where(positive, zero, far),
    ), positive


def linear_weights(shift):
    return jnp.maximum(shift, 0.0), 1.0 - jnp.abs(shift), jnp.maximum(-shift, 0.0)


def clipped(value):
    return jnp.clip(value, -CLIP_BOUND, CLIP_BOUND)


def advect_kernel(
    sizes,
    msg_ref,
    fields_ref,
    extra_ref,
    perm_hbm_ref,
    out_ref,
    t_ref,
    e_ref,
    perm_ref,
    result_ref,
    source_ref,
    sem_ref,
    perm_sem_ref,
):
    inner, band_rows, per_level = sizes
    size = band_rows * inner
    perm_copy = pltpu.make_async_copy(perm_hbm_ref, perm_ref, perm_sem_ref)
    perm_copy.start()
    meta = msg_ref[pl.ds(CAP * 2 * size, META), :].astype(F32)
    lane = lax.broadcasted_iota(jnp.int32, (META, LANES), 1)

    def copies(slot, source):
        at = pl.ds(source * band_rows, band_rows + 2 * RIM)
        return (
            pltpu.make_async_copy(extra_ref.at[:, at], e_ref.at[slot], sem_ref.at[slot, 0]),
            pltpu.make_async_copy(fields_ref.at[:, at], t_ref.at[slot], sem_ref.at[slot, 1]),
        )

    for slot in range(CAP):
        source = jnp.max(jnp.where(lane == slot, meta, -1.0)).astype(jnp.int32)
        source_ref[slot] = source

        @pl.when(source >= 0)
        def _():
            for copy in copies(slot, source):
                copy.start()

    def one_slot(slot, carry):
        source = source_ref[slot]

        @pl.when(source < 0)
        def _():
            result_ref[pl.ds(slot * size, size), :] = jnp.zeros((size, per_level * LANES), F32)

        @pl.when(source >= 0)
        def _():
            for copy in copies(slot, source):
                copy.wait()

            def one_row(row, inner_carry):
                here = [
                    msg_ref[pl.ds((slot * 2 + comp) * size + row * inner, inner), :].astype(F32)
                    for comp in range(2)
                ]
                for eight in range(inner // 8):
                    base = eight * 8
                    wind = [h[base : base + 8] for h in here]
                    window = [
                        [
                            [
                                e_ref[slot, comp, row + RIM + b, pl.ds(base + RIM + a, 8), :]
                                for a in (-1, 0, 1)
                            ]
                            for b in (-1, 0, 1)
                        ]
                        for comp in range(2)
                    ]
                    shift = [clipped(w) for w in wind]
                    for _ in range(TRAJ):
                        lon = linear_weights(shift[0])
                        lat = linear_weights(shift[1])
                        moved = []
                        for comp in range(2):
                            total = None
                            for b in range(3):
                                line = (
                                    lon[0] * window[comp][b][0]
                                    + lon[1] * window[comp][b][1]
                                    + lon[2] * window[comp][b][2]
                                )
                                line = lat[b] * line
                                total = line if total is None else total + line
                            moved.append(clipped(0.5 * (wind[comp] + total)))
                        shift = moved
                    lon_cubic, _ = cubic_weights(shift[0])
                    lat_cubic, north = cubic_weights(shift[1])
                    low, mid, high = linear_weights(shift[0])
                    zero = jnp.zeros_like(low)
                    lon_linear = (zero, low, mid, high, zero)
                    taps = []
                    for b in range(-2, 3):
                        for a in range(-2, 3):
                            if abs(b) == 2:
                                if abs(a) == 2:
                                    continue
                                weight = lon_linear[a + 2]
                            elif b == 0:
                                weight = lon_cubic[a + 2]
                            elif b == -1:
                                weight = jnp.where(north, lon_cubic[a + 2], lon_linear[a + 2])
                            else:
                                weight = jnp.where(north, lon_linear[a + 2], lon_cubic[a + 2])
                            taps.append((a, b, weight * lat_cubic[b + 2]))
                    for tracer in range(per_level):
                        total = None
                        for a, b, weight in taps:
                            term = weight * t_ref[
                                slot, tracer, row + RIM + b, pl.ds(base + RIM + a, 8), :
                            ]
                            total = term if total is None else total + term
                        result_ref[
                            pl.ds(slot * size + row * inner + base, 8),
                            tracer * LANES : (tracer + 1) * LANES,
                        ] = total
                return inner_carry

            lax.fori_loop(0, band_rows, one_row, 0)

        return carry

    lax.fori_loop(0, CAP, one_slot, 0)
    perm_copy.wait()
    out_ref[...] = jnp.dot(
        result_ref[...].astype(BF16), perm_ref[...], preferred_element_type=F32
    ).astype(BF16)


def gather_kernel(sizes, dep_ref, *rest):
    columns, rows, groups, inner, bands, band_rows = sizes
    ins = rest[: LAST - FIRST]
    out_ref, wide_ref, slot_ref, count_ref = rest[LAST - FIRST :]
    halves = out_ref.shape[-1] // LANES
    size = band_rows * inner
    fill_slots(dep_ref, slot_ref, count_ref, bands)
    for offset in range(LAST - FIRST):

        def one_slot(slot, carry):
            band = slot_ref[offset * CAP + slot]

            @pl.when(band >= 0)
            def _():
                for row in range(band_rows):
                    value = ins[offset][pl.ds(slot * size + row * inner, inner), :].astype(F32)
                    for g in range(groups):
                        at = pl.ds(g * inner * rows + band * band_rows + row, inner, stride=rows)
                        for half in range(halves):
                            first = (g * halves + half) * LANES
                            wide_ref[half, at, :] = value[:, first : first + LANES]

            return carry

        lax.fori_loop(0, CAP, one_slot, 0)

    def narrow(column, carry):
        at = pl.ds(column * rows, rows)
        for half in range(halves):
            out_ref[column, :, half * LANES : (half + 1) * LANES] = wide_ref[half, at, :].astype(
                BF16
            )
        return carry

    lax.fori_loop(0, columns, narrow, 0)


def one_hot(target, width):
    return (target[:, None] == jnp.arange(width, dtype=jnp.int32)[None, :]).astype(BF16)


def on_device(tracers, wind_fields, departures):
    columns, rows, tracer_ch = tracers.shape
    wind_ch = wind_fields.shape[-1]
    levels = wind_ch // 4
    per_level = tracer_ch // levels
    bands = departures.shape[1]
    band_rows = rows // bands
    groups = LANES // levels
    inner = columns // groups
    padded_inner = -(-(inner + 2 * RIM) // 8) * 8
    size = band_rows * inner
    offsets = LAST - FIRST
    wide = per_level * LANES

    index = jnp.arange(wide, dtype=jnp.int32)
    tracer, group, level = index // LANES, (index // levels) % groups, index % levels
    perm = one_hot(group * tracer_ch + level * per_level + tracer, wide)
    index = jnp.arange(groups * wind_ch, dtype=jnp.int32)
    group, kind, level = index // wind_ch, (index // levels) % 4, index % levels
    perm_w = one_hot(kind * LANES + group * levels + level, 4 * LANES)

    low_t = shifted(tracers[columns - RIM :], "lon", 1)
    high_t = shifted(tracers[:RIM], "lon", -1)
    low_w = shifted(wind_fields[columns - RIM :], "lon", 1)
    high_w = shifted(wind_fields[:RIM], "lon", -1)

    vmem = pl.BlockSpec(memory_space=pltpu.VMEM)
    smem = pl.BlockSpec(memory_space=pltpu.SMEM)
    anywhere = pl.BlockSpec(memory_space=pl.ANY)
    msg_shape = jax.ShapeDtypeStruct((CAP * 2 * size + META, LANES), BF16)
    tables = [pltpu.SMEM((offsets * CAP,), jnp.int32), pltpu.SMEM((offsets,), jnp.int32)]
    messages = pl.pallas_call(
        functools.partial(wind_kernel, (columns, rows, groups, inner, bands, band_rows)),
        out_shape=[msg_shape] * offsets,
        in_specs=[smem, vmem, vmem],
        out_specs=[vmem] * offsets,
        scratch_shapes=[
            pltpu.VMEM((columns * rows, LANES), F32),
            pltpu.VMEM((2, rows, inner, LANES), BF16),
        ]
        + tables,
        cost_estimate=pl.CostEstimate(flops=4_000_000, bytes_accessed=3_000_000, transcendentals=0),
        name="winds",
    )(departures, wind_fields, perm_w)

    arrived = [
        msg if FIRST + n == 0 else shifted(msg, "lon", -(FIRST + n))
        for n, msg in enumerate(messages)
    ]

    all_columns = (groups - 1) * inner + padded_inner
    fields, extra = pl.pallas_call(
        functools.partial(
            prepare_kernel, (columns, rows, groups, inner, padded_inner, per_level)
        ),
        out_shape=[
            jax.ShapeDtypeStruct((per_level, rows + 2 * RIM, padded_inner, LANES), F32),
            jax.ShapeDtypeStruct((2, rows + 2 * RIM, padded_inner, LANES), F32),
        ],
        in_specs=[vmem] * 8,
        out_specs=[anywhere] * 2,
        scratch_shapes=[
            pltpu.VMEM((tracer_ch // LANES, all_columns * rows, LANES), F32),
            pltpu.VMEM((all_columns * rows, LANES), F32),
            pltpu.VMEM((2, per_level, 8, padded_inner, LANES), F32),
            pltpu.VMEM((2, 2, 8, padded_inner, LANES), F32),
            pltpu.VMEM((2, per_level, RIM, padded_inner, LANES), F32),
            pltpu.VMEM((2, 2, RIM, padded_inner, LANES), F32),
            pltpu.SemaphoreType.DMA((2, 2)),
            pltpu.SemaphoreType.DMA((2, 2)),
        ],
        cost_estimate=pl.CostEstimate(
            flops=16_000_000, bytes_accessed=12_000_000, transcendentals=0
        ),
        name="prepare",
    )(tracers, wind_fields, low_t, high_t, low_w, high_w, perm, perm_w)

    advect = pl.pallas_call(
        functools.partial(advect_kernel, (inner, band_rows, per_level)),
        out_shape=jax.ShapeDtypeStruct((CAP * size, wide), BF16),
        in_specs=[vmem, anywhere, anywhere, anywhere],
        out_specs=vmem,
        scratch_shapes=[
            pltpu.VMEM((CAP, per_level, band_rows + 2 * RIM, padded_inner, LANES), F32),
            pltpu.VMEM((CAP, 2, band_rows + 2 * RIM, padded_inner, LANES), F32),
            pltpu.VMEM((wide, wide), BF16),
            pltpu.VMEM((CAP * size, wide), F32),
            pltpu.SMEM((CAP,), jnp.int32),
            pltpu.SemaphoreType.DMA((CAP, 2)),
            pltpu.SemaphoreType.DMA,
        ],
        cost_estimate=pl.CostEstimate(
            flops=16_000_000, bytes_accessed=6_000_000, transcendentals=0
        ),
        name="advect",
    )
    received = []
    for n in range(offsets):
        result = advect(arrived[n], fields, extra, perm)
        received.append(result if FIRST + n == 0 else shifted(result, "lon", FIRST + n))

    return pl.pallas_call(
        functools.partial(gather_kernel, (columns, rows, groups, inner, bands, band_rows)),
        out_shape=jax.ShapeDtypeStruct((columns, rows, tracer_ch), BF16),
        in_specs=[smem] + [vmem] * offsets,
        out_specs=vmem,
        scratch_shapes=[pltpu.VMEM((tracer_ch // LANES, columns * rows, LANES), F32)] + tables,
        cost_estimate=pl.CostEstimate(flops=2_000_000, bytes_accessed=6_000_000, transcendentals=0),
        name="gather",
    )(departures, *received)


def solution(mesh):
    placed = (
        P(("groups", "lon"), None, None),
        P(("groups", "lon"), None, None),
        P(("groups", "lon"), None, None),
    )
    return jax.shard_map(
        on_device,
        mesh=mesh,
        in_specs=placed,
        out_specs=P(("groups", "lon"), None, None),
        check_vma=False,
    )
```

time: 443 us -> 148 us (0.33)
  the two profiles are of different devices: /device:TPU:0 before, /device:TPU:1 now
where the time goes in v1:
time: 148 us; the launch traced here: 150 us
  Pallas kernels  79 us (53%)
  starting transfers between devices  32.3 us (22%)
  waiting for transfers between devices  29.7 us (20%)
  local copies, waits for them, and re-layouts  6.25 us (4%)
  other arithmetic  2.72 us (2%)
    pallas_call x8, Pallas kernels, on_device(): result = advect(arrived[n], fields, extra, perm)  49.5 us
    ppermute x18, starting transfers between devices, shifted(): return lax.ppermute(block, axis, route)  32.3 us
    ppermute x18, waiting for transfers between devices, shifted(): return lax.ppermute(block, axis, route)  29.7 us
    pallas_call x1, Pallas kernels, on_device(): pl.pallas_call(functools.partial(prepare_kernel, (columns, rows, groups,...  15.1 us
    pallas_call x1, Pallas kernels, on_device(): pl.pallas_call(functools.partial(gather_kernel, (columns, rows, groups, i...  8.74 us
    pallas_call x1, Pallas kernels, on_device(): pl.pallas_call(functools.partial(wind_kernel, (columns, rows, groups, inn...  5.69 us
    unnamed x45, local copies, waits for them, and re-layouts  4.59 us
  transfers between devices with their start and end apart: 18, of which 4 were waited for; matrix products, arithmetic and copies ran while one was open for 3% of the time, Pallas kernels for 47%

profile of v1, /device:TPU:1, one launch (start us, length us, event | category | flops | bytes accessed | tf_op | source)
XLA Modules:
  0.0 150.3 jit_solution(13208398473692322959)
XLA Ops:
  0.0 0.8 fusion.30
  0.8 0.0 collective-permute-start.4
  0.8 2.7 %collective-permute-start.3 = (bf16[2,64,128]{2,1,0:T(8,128)(2,1)S(1)}, bf16[2,64,128]{2,1,0:T(8,128)(2,1)S(1)}, u32[]{:S(2)}, u32[]{:S(2)}) collective-permute-start(bf16[2,64,128]{2,1,0:T(8,128)(2,1)S(1)} %get-tuple-element.28), channel_id=1, source_target_pairs={{15,0},{0,1},{1,2},{2,3},{3,4},{4,5},{5,6},{6,7},{7,8},{8,9},{9,10... | collective-permute-start | bytes 98312 | tf_op jit(solution)/shard_map/ppermute | solution.py:25
  3.5 0.9 fusion.29
  4.3 2.9 %collective-permute-start.2 = (bf16[2,64,256]{2,1,0:T(8,128)(2,1)S(1)}, bf16[2,64,256]{2,1,0:T(8,128)(2,1)S(1)}, u32[]{:S(2)}, u32[]{:S(2)}) collective-permute-start(bf16[2,64,256]{2,1,0:T(8,128)(2,1)S(1)} %get-tuple-element.25), channel_id=1, source_target_pairs={{1,0},{2,1},{3,2},{4,3},{5,4},{6,5},{7,6},{8,7},{9,8},{10,9},{11,1... | collective-permute-start | bytes 196616 | tf_op jit(solution)/shard_map/ppermute | solution.py:25
  7.2 0.0 collective-permute-start.1
  7.2 1.4 copy.5.dep_ref
  8.6 1.0 fusion.1.perm_ref.perm_w_ref
  9.6 5.7 %winds.1 = (bf16[528,128]{1,0:T(8,128)(2,1)}, bf16[528,128]{1,0:T(8,128)(2,1)}, bf16[528,128]{1,0:T(8,128)(2,1)}, bf16[528,128]{1,0:T(8,128)(2,1)}, bf16[528,128...) custom-call(s32[1,16,2]{2,1,0:T(8,128)} %copy.5.dep_ref, ...), custom_call_target="tpu_custom_call" | custom-call | flops 4000000 | bytes 3000000 | tf_op jit(solution)/shard_map/winds/pallas_call | solution.py:446
  15.3 0.2 collective-permute-start
  15.5 2.1 %collective-permute-start.6 = (bf16[528,128]{1,0:T(8,128)(2,1)}, bf16[528,128]{1,0:T(8,128)(2,1)S(1)}, u32[]{:S(2)}, u32[]{:S(2)}) collective-permute-start(bf16[528,128]{1,0:T(8,128)(2,1)} %get-tuple-element.18), channel_id=1, source_target_pairs={{13,0},{14,1},{15,2},{0,3},{1,4},{2,5},{3,6},{4,7},{5,8},{6,9},{7,... | collective-permute-start | bytes 405512 | tf_op jit(solution)/shard_map/ppermute | solution.py:25
  17.6 1.7 %fusion.perm_ref.perm_hbm_ref = bf16[1024,1024]{1,0:T(8,128)(2,1)} fusion(s32[1024]{0:T(1024)S(1)} %fusion.15), kind=kLoop, calls=%fused_computation.1 | loop fusion | flops 2097152 | bytes 2101248 | tf_op jit(solution)/shard_map/convert_element_type | solution.py:412
  19.3 0.0 collective-permute-done.3.low_w_ref
  19.3 0.0 collective-permute-done.1.low_t_ref
  19.3 0.6 copy-done.16
  19.9 0.0 copy-done.13
  19.9 0.6 copy-done.14
  20.5 15.1 %prepare.1 = (f32[8,68,24,128]{3,2,1,0:T(8,128)}, f32[2,68,24,128]{3,2,1,0:T(8,128)}) custom-call(bf16[64,64,256]{2,1,0:T(8,128)(2,1)} %tracers_ref.1, bf16[64,64,128]{2,1,0:T(8,128)(2,1)} %wind_ref.3, bf16[2,64,256]{2,1,0:T(8,128)(2,1)} %copy-done.14, bf16[2,64,256]{2,1,0:T(8,128)(2,1)} %copy-done.13, bf16[2,64,128]{2,1,0:T(8,128)(2,1)} %copy-done.16, ...), custom_call_target="tpu_custom_call" | custom-call | flops 16000000 | bytes 12000000 | tf_op jit(solution)/shard_map/prepare/pallas_call | solution.py:466
  35.6 0.0 collective-permute-done.msg_ref
  35.6 0.6 copy-done.7
  36.3 7.2 %advect.8 = bf16[256,1024]{1,0:T(8,128)(2,1)} custom-call(bf16[528,128]{1,0:T(8,128)(2,1)} %copy-done.7, f32[8,68,24,128]{3,2,1,0:T(8,128)} %get-tuple-element.16.fields_ref, f32[2,68,24,128]{3,2,1,0:T(8,128)} %get-tuple-element.17.extra_ref, bf16[1024,1024]{1,0:T(8,128)(2,1)} %fusion.perm_ref.perm_hbm_ref), custom_call_target="tpu_custom_call" | custom-call | flops 16000000 | bytes 6000000 | tf_op jit(solution)/shard_map/advect/pallas_call | solution.py:513
  43.5 5.4 %collective-permute-start.5 = (bf16[256,1024]{1,0:T(8,128)(2,1)}, bf16[256,1024]{1,0:T(8,128)(2,1)S(1)}, u32[]{:S(2)}, u32[]{:S(2)}) collective-permute-start(bf16[256,1024]{1,0:T(8,128)(2,1)} %advect.8), channel_id=1, source_target_pairs={{4,0},{5,1},{6,2},{7,3},{8,4},{9,5},{10,6},{11,7},{12,8},{13,9},{1... | collective-permute-start | bytes 1572872 | tf_op jit(solution)/shard_map/ppermute | solution.py:25
  49.0 0.7 copy-done.6
  49.6 5.8 %advect.9 = bf16[256,1024]{1,0:T(8,128)(2,1)} custom-call(bf16[528,128]{1,0:T(8,128)(2,1)} %copy-done.6, f32[8,68,24,128]{3,2,1,0:T(8,128)} %get-tuple-element.16.fields_ref, f32[2,68,24,128]{3,2,1,0:T(8,128)} %get-tuple-element.17.extra_ref, bf16[1024,1024]{1,0:T(8,128)(2,1)} %fusion.perm_ref.perm_hbm_ref), custom_call_target="tpu_custom_call" | custom-call | flops 16000000 | bytes 6000000 | tf_op jit(solution)/shard_map/advect/pallas_call | solution.py:513
  55.5 0.1 collective-permute-start.7
  55.5 1.1 collective-permute-start.8
  56.7 3.6 %collective-permute-start.16 = (bf16[528,128]{1,0:T(8,128)(2,1)S(1)}, bf16[528,128]{1,0:T(8,128)(2,1)S(1)}, u32[]{:S(2)}, u32[]{:S(2)}) collective-permute-start(bf16[528,128]{1,0:T(8,128)(2,1)S(1)} %copy-done.20), channel_id=1, source_target_pairs={{3,0},{4,1},{5,2},{6,3},{7,4},{8,5},{9,6},{10,7},{11,8},{12,9},{13... | collective-permute-start | bytes 405512 | tf_op jit(solution)/shard_map/ppermute | solution.py:25
  60.3 0.1 collective-permute-start.10
  60.3 4.2 %collective-permute-done.8.msg_ref = bf16[528,128]{1,0:T(8,128)(2,1)S(1)} collective-permute-done((bf16[528,128]{1,0:T(8,128)(2,1)S(1)}, bf16[528,128]{1,0:T(8,128)(2,1)S(1)}, u32[]{:S(2)}, u32[]{:S(2)}) %collective-permute-start.8) | collective-permute-done | bytes 135200 | tf_op jit(solution)/shard_map/ppermute | solution.py:25
  64.6 6.8 %collective-permute-start.12 = (bf16[528,128]{1,0:T(8,128)(2,1)S(1)}, bf16[528,128]{1,0:T(8,128)(2,1)S(1)}, u32[]{:S(2)}, u32[]{:S(2)}) collective-permute-start(bf16[528,128]{1,0:T(8,128)(2,1)S(1)} %copy-done.18), channel_id=1, source_target_pairs={{1,0},{2,1},{3,2},{4,3},{5,4},{6,5},{7,6},{8,7},{9,8},{10,9},{11,1... | collective-permute-start | bytes 405512 | tf_op jit(solution)/shard_map/ppermute | solution.py:25
  71.4 3.0 %collective-permute-done.16.msg_ref = bf16[528,128]{1,0:T(8,128)(2,1)S(1)} collective-permute-done((bf16[528,128]{1,0:T(8,128)(2,1)S(1)}, bf16[528,128]{1,0:T(8,128)(2,1)S(1)}, u32[]{:S(2)}, u32[]{:S(2)}) %collective-permute-start.16) | collective-permute-done | bytes 135200 | tf_op jit(solution)/shard_map/ppermute | solution.py:25
  74.4 0.0 collective-permute-start.14
  74.4 0.7 copy-done.12
  75.1 7.2 %advect.15 = bf16[256,1024]{1,0:T(8,128)(2,1)} custom-call(bf16[528,128]{1,0:T(8,128)(2,1)} %copy-done.12, f32[8,68,24,128]{3,2,1,0:T(8,128)} %get-tuple-element.16.fields_ref, f32[2,68,24,128]{3,2,1,0:T(8,128)} %get-tuple-element.17.extra_ref, bf16[1024,1024]{1,0:T(8,128)(2,1)} %fusion.perm_ref.perm_hbm_ref), custom_call_target="tpu_custom_call" | custom-call | flops 16000000 | bytes 6000000 | tf_op jit(solution)/shard_map/advect/pallas_call | solution.py:513
  82.3 5.8 %advect.10 = bf16[256,1024]{1,0:T(8,128)(2,1)} custom-call(bf16[528,128]{1,0:T(8,128)(2,1)} %copy-done.11, f32[8,68,24,128]{3,2,1,0:T(8,128)} %get-tuple-element.16.fields_ref, f32[2,68,24,128]{3,2,1,0:T(8,128)} %get-tuple-element.17.extra_ref, bf16[1024,1024]{1,0:T(8,128)(2,1)} %fusion.perm_ref.perm_hbm_ref), custom_call_target="tpu_custom_call" | custom-call | flops 16000000 | bytes 6000000 | tf_op jit(solution)/shard_map/advect/pallas_call | solution.py:513
  88.1 3.7 %collective-permute-start.9 = (bf16[256,1024]{1,0:T(8,128)(2,1)}, bf16[256,1024]{1,0:T(8,128)(2,1)S(1)}, u32[]{:S(2)}, u32[]{:S(2)}) collective-permute-start(bf16[256,1024]{1,0:T(8,128)(2,1)} %advect.10), channel_id=1, source_target_pairs={{2,0},{3,1},{4,2},{5,3},{6,4},{7,5},{8,6},{9,7},{10,8},{11,9},{12,... | collective-permute-start | bytes 1572872 | tf_op jit(solution)/shard_map/ppermute | solution.py:25
  91.8 5.2 %advect.11 = bf16[256,1024]{1,0:T(8,128)(2,1)} custom-call(bf16[528,128]{1,0:T(8,128)(2,1)} %copy-done.10, f32[8,68,24,128]{3,2,1,0:T(8,128)} %get-tuple-element.16.fields_ref, f32[2,68,24,128]{3,2,1,0:T(8,128)} %get-tuple-element.17.extra_ref, bf16[1024,1024]{1,0:T(8,128)(2,1)} %fusion.perm_ref.perm_hbm_ref), custom_call_target="tpu_custom_call" | custom-call | flops 16000000 | bytes 6000000 | tf_op jit(solution)/shard_map/advect/pallas_call | solution.py:513
  97.0 0.0 collective-permute-done.12.msg_ref
  97.0 2.7 %collective-permute-start.11 = (bf16[256,1024]{1,0:T(8,128)(2,1)}, bf16[256,1024]{1,0:T(8,128)(2,1)S(1)}, u32[]{:S(2)}, u32[]{:S(2)}) collective-permute-start(bf16[256,1024]{1,0:T(8,128)(2,1)} %advect.11), channel_id=1, source_target_pairs={{1,0},{2,1},{3,2},{4,3},{5,4},{6,5},{7,6},{8,7},{9,8},{10,9},{11,1... | collective-permute-start | bytes 1572872 | tf_op jit(solution)/shard_map/ppermute | solution.py:25
  99.7 5.8 %advect.13 = bf16[256,1024]{1,0:T(8,128)(2,1)} custom-call(bf16[528,128]{1,0:T(8,128)(2,1)} %copy-done.9, f32[8,68,24,128]{3,2,1,0:T(8,128)} %get-tuple-element.16.fields_ref, f32[2,68,24,128]{3,2,1,0:T(8,128)} %get-tuple-element.17.extra_ref, bf16[1024,1024]{1,0:T(8,128)(2,1)} %fusion.perm_ref.perm_hbm_ref), custom_call_target="tpu_custom_call" | custom-call | flops 16000000 | bytes 6000000 | tf_op jit(solution)/shard_map/advect/pallas_call | solution.py:513
  105.5 0.9 collective-permute-start.13
  106.4 7.2 %advect.14 = bf16[256,1024]{1,0:T(8,128)(2,1)} custom-call(bf16[528,128]{1,0:T(8,128)(2,1)} %copy-done.8, f32[8,68,24,128]{3,2,1,0:T(8,128)} %get-tuple-element.16.fields_ref, f32[2,68,24,128]{3,2,1,0:T(8,128)} %get-tuple-element.17.extra_ref, bf16[1024,1024]{1,0:T(8,128)(2,1)} %fusion.perm_ref.perm_hbm_ref), custom_call_target="tpu_custom_call" | custom-call | flops 16000000 | bytes 6000000 | tf_op jit(solution)/shard_map/advect/pallas_call | solution.py:513
  113.6 0.1 collective-permute-start.15
  113.7 0.1 collective-permute-start.17
  113.8 5.3 %advect.12.rest_4_ = bf16[256,1024]{1,0:T(8,128)(2,1)} custom-call(bf16[528,128]{1,0:T(8,128)(2,1)} %get-tuple-element.21.msg_ref, f32[8,68,24,128]{3,2,1,0:T(8,128)} %get-tuple-element.16.fields_ref, f32[2,68,24,128]{3,2,1,0:T(8,128)} %get-tuple-element.17.extra_ref, bf16[1024,1024]{1,0:T(8,128)(2,1)} %fusion.perm_ref.perm_hbm_ref), custom_call_target="tpu_custom_call" | custom-call | flops 16000000 | bytes 6000000 | tf_op jit(solution)/shard_map/advect/pallas_call | solution.py:513
  119.2 10.7 %collective-permute-done.15.rest_6_ = bf16[256,1024]{1,0:T(8,128)(2,1)} collective-permute-done((bf16[256,1024]{1,0:T(8,128)(2,1)}, bf16[256,1024]{1,0:T(8,128)(2,1)}, u32[]{:S(2)}, u32[]{:S(2)}) %collective-permute-start.15) | collective-permute-done | bytes 524320 | tf_op jit(solution)/shard_map/ppermute | solution.py:25
  130.0 11.6 %collective-permute-done.17.rest_7_ = bf16[256,1024]{1,0:T(8,128)(2,1)} collective-permute-done((bf16[256,1024]{1,0:T(8,128)(2,1)S(1)}, bf16[256,1024]{1,0:T(8,128)(2,1)}, u32[]{:S(2)}, u32[]{:S(2)}) %collective-permute-start.17) | collective-permute-done | bytes 524320 | tf_op jit(solution)/shard_map/ppermute | solution.py:25
  141.6 8.7 %gather.1 = bf16[64,64,256]{2,1,0:T(8,128)(2,1)} custom-call(s32[1,16,2]{2,1,0:T(8,128)} %copy.5.dep_ref, bf16[256,1024]{1,0:T(8,128)(2,1)} %copy-done, bf16[256,1024]{1,0:T(8,128)(2,1)} %copy-done.1, bf16[256,1024]{1,0:T(8,128)(2,1)} %copy-done.3, bf16[256,1024]{1,0:T(8,128)(2,1)} %copy-done.4, bf16[256,1024]{1,0:T(8,128)(2,1)} %advect.12.rest_4_, ...), custom_call_target="tpu_custom_call" | custom-call | flops 2000000 | bytes 6000000 | tf_op jit(solution)/shard_map/gather/pallas_call | solution.py:516
  (50 shorter events, 0.1 us)
Async XLA Ops:
  0.8 14.7 %collective-permute-start.4 = (bf16[2,64,128]{2,1,0:T(8,128)(2,1)S(1)}, bf16[2,64,128]{2,1,0:T(8,128)(2,1)S(1)}, u32[]{:S(2)}, u32[]{:S(2)}) collective-permute-start(bf16[2,64,128]{2,1,0:T(8,128)(2,1)S(1)} %get-tuple-element.27), channel_id=1, source_target_pairs={{1,0},{2,1},{3,2},{4,3},{5,4},{6,5},{7,6},{8,7},{9,8},{10,9},{11,1... | collective-permute-start | bytes 98312 | tf_op jit(solution)/shard_map/ppermute | solution.py:25
  0.8 18.5 %collective-permute-start.3 = (bf16[2,64,128]{2,1,0:T(8,128)(2,1)S(1)}, bf16[2,64,128]{2,1,0:T(8,128)(2,1)S(1)}, u32[]{:S(2)}, u32[]{:S(2)}) collective-permute-start(bf16[2,64,128]{2,1,0:T(8,128)(2,1)S(1)} %get-tuple-element.28), channel_id=1, source_target_pairs={{15,0},{0,1},{1,2},{2,3},{3,4},{4,5},{5,6},{6,7},{7,8},{8,9},{9,10... | collective-permute-start | bytes 98312 | tf_op jit(solution)/shard_map/ppermute | solution.py:25
  4.3 15.0 %collective-permute-start.2 = (bf16[2,64,256]{2,1,0:T(8,128)(2,1)S(1)}, bf16[2,64,256]{2,1,0:T(8,128)(2,1)S(1)}, u32[]{:S(2)}, u32[]{:S(2)}) collective-permute-start(bf16[2,64,256]{2,1,0:T(8,128)(2,1)S(1)} %get-tuple-element.25), channel_id=1, source_target_pairs={{1,0},{2,1},{3,2},{4,3},{5,4},{6,5},{7,6},{8,7},{9,8},{10,9},{11,1... | collective-permute-start | bytes 196616 | tf_op jit(solution)/shard_map/ppermute | solution.py:25
  7.2 12.1 %collective-permute-start.1 = (bf16[2,64,256]{2,1,0:T(8,128)(2,1)S(1)}, bf16[2,64,256]{2,1,0:T(8,128)(2,1)S(1)}, u32[]{:S(2)}, u32[]{:S(2)}) collective-permute-start(bf16[2,64,256]{2,1,0:T(8,128)(2,1)S(1)} %get-tuple-element.26), channel_id=1, source_target_pairs={{15,0},{0,1},{1,2},{2,3},{3,4},{4,5},{5,6},{6,7},{7,8},{8,9},{9,10... | collective-permute-start | bytes 196616 | tf_op jit(solution)/shard_map/ppermute | solution.py:25
  15.3 20.4 %collective-permute-start = (bf16[528,128]{1,0:T(8,128)(2,1)}, bf16[528,128]{1,0:T(8,128)(2,1)S(1)}, u32[]{:S(2)}, u32[]{:S(2)}) collective-permute-start(bf16[528,128]{1,0:T(8,128)(2,1)} %get-tuple-element.15), channel_id=1, source_target_pairs={{12,0},{13,1},{14,2},{15,3},{0,4},{1,5},{2,6},{3,7},{4,8},{5,9},{6... | collective-permute-start | bytes 405512 | tf_op jit(solution)/shard_map/ppermute | solution.py:25
  15.5 3.8 %copy-start.15 = (bf16[2,64,128]{2,1,0:T(8,128)(2,1)}, bf16[2,64,128]{2,1,0:T(8,128)(2,1)S(1)}, u32[]{:S(2)}) copy-start(bf16[2,64,128]{2,1,0:T(8,128)(2,1)S(1)} %collective-permute-done.4.high_w_ref) | copy-start | bytes 98308
  15.5 33.5 %collective-permute-start.6 = (bf16[528,128]{1,0:T(8,128)(2,1)}, bf16[528,128]{1,0:T(8,128)(2,1)S(1)}, u32[]{:S(2)}, u32[]{:S(2)}) collective-permute-start(bf16[528,128]{1,0:T(8,128)(2,1)} %get-tuple-element.18), channel_id=1, source_target_pairs={{13,0},{14,1},{15,2},{0,3},{1,4},{2,5},{3,6},{4,7},{5,8},{6,9},{7,... | collective-permute-start | bytes 405512 | tf_op jit(solution)/shard_map/ppermute | solution.py:25
  19.3 0.6 copy-start.16
  19.3 0.6 copy-start.13
  19.9 0.6 copy-start.14
  35.6 0.6 copy-start.7
  43.5 12.0 %copy-start.21 = (bf16[528,128]{1,0:T(8,128)(2,1)S(1)}, bf16[528,128]{1,0:T(8,128)(2,1)}, u32[]{:S(2)}) copy-start(bf16[528,128]{1,0:T(8,128)(2,1)} %get-tuple-element.19) | copy-start | bytes 405508
  43.5 13.2 %copy-start.20 = (bf16[528,128]{1,0:T(8,128)(2,1)S(1)}, bf16[528,128]{1,0:T(8,128)(2,1)}, u32[]{:S(2)}) copy-start(bf16[528,128]{1,0:T(8,128)(2,1)} %get-tuple-element.24) | copy-start | bytes 405508
  43.5 16.7 %copy-start.19 = (bf16[528,128]{1,0:T(8,128)(2,1)S(1)}, bf16[528,128]{1,0:T(8,128)(2,1)}, u32[]{:S(2)}) copy-start(bf16[528,128]{1,0:T(8,128)(2,1)} %get-tuple-element.20) | copy-start | bytes 405508
  43.5 21.0 %copy-start.18 = (bf16[528,128]{1,0:T(8,128)(2,1)S(1)}, bf16[528,128]{1,0:T(8,128)(2,1)}, u32[]{:S(2)}) copy-start(bf16[528,128]{1,0:T(8,128)(2,1)} %get-tuple-element.22) | copy-start | bytes 405508
  43.5 30.9 %copy-start.17 = (bf16[528,128]{1,0:T(8,128)(2,1)S(1)}, bf16[528,128]{1,0:T(8,128)(2,1)}, u32[]{:S(2)}) copy-start(bf16[528,128]{1,0:T(8,128)(2,1)} %get-tuple-element.23) | copy-start | bytes 405508
  43.5 70.1 %collective-permute-start.5 = (bf16[256,1024]{1,0:T(8,128)(2,1)}, bf16[256,1024]{1,0:T(8,128)(2,1)S(1)}, u32[]{:S(2)}, u32[]{:S(2)}) collective-permute-start(bf16[256,1024]{1,0:T(8,128)(2,1)} %advect.8), channel_id=1, source_target_pairs={{4,0},{5,1},{6,2},{7,3},{8,4},{9,5},{10,6},{11,7},{12,8},{13,9},{1... | collective-permute-start | bytes 1572872 | tf_op jit(solution)/shard_map/ppermute | solution.py:25
  49.0 0.7 copy-start.6
  55.5 58.3 %collective-permute-start.7 = (bf16[256,1024]{1,0:T(8,128)(2,1)}, bf16[256,1024]{1,0:T(8,128)(2,1)S(1)}, u32[]{:S(2)}, u32[]{:S(2)}) collective-permute-start(bf16[256,1024]{1,0:T(8,128)(2,1)} %advect.9), channel_id=1, source_target_pairs={{3,0},{4,1},{5,2},{6,3},{7,4},{8,5},{9,6},{10,7},{11,8},{12,9},{13... | collective-permute-start | bytes 1572872 | tf_op jit(solution)/shard_map/ppermute | solution.py:25
  55.5 9.0 %collective-permute-start.8 = (bf16[528,128]{1,0:T(8,128)(2,1)S(1)}, bf16[528,128]{1,0:T(8,128)(2,1)S(1)}, u32[]{:S(2)}, u32[]{:S(2)}) collective-permute-start(bf16[528,128]{1,0:T(8,128)(2,1)S(1)} %copy-done.21), channel_id=1, source_target_pairs={{14,0},{15,1},{0,2},{1,3},{2,4},{3,5},{4,6},{5,7},{6,8},{7,9},{8,1... | collective-permute-start | bytes 405512 | tf_op jit(solution)/shard_map/ppermute | solution.py:25
  56.7 17.7 %collective-permute-start.16 = (bf16[528,128]{1,0:T(8,128)(2,1)S(1)}, bf16[528,128]{1,0:T(8,128)(2,1)S(1)}, u32[]{:S(2)}, u32[]{:S(2)}) collective-permute-start(bf16[528,128]{1,0:T(8,128)(2,1)S(1)} %copy-done.20), channel_id=1, source_target_pairs={{3,0},{4,1},{5,2},{6,3},{7,4},{8,5},{9,6},{10,7},{11,8},{12,9},{13... | collective-permute-start | bytes 405512 | tf_op jit(solution)/shard_map/ppermute | solution.py:25
  60.3 27.8 %collective-permute-start.10 = (bf16[528,128]{1,0:T(8,128)(2,1)S(1)}, bf16[528,128]{1,0:T(8,128)(2,1)S(1)}, u32[]{:S(2)}, u32[]{:S(2)}) collective-permute-start(bf16[528,128]{1,0:T(8,128)(2,1)S(1)} %copy-done.19), channel_id=1, source_target_pairs={{15,0},{0,1},{1,2},{2,3},{3,4},{4,5},{5,6},{6,7},{7,8},{8,9},{9,10... | collective-permute-start | bytes 405512 | tf_op jit(solution)/shard_map/ppermute | solution.py:25
  64.6 17.7 %copy-start.11 = (bf16[528,128]{1,0:T(8,128)(2,1)}, bf16[528,128]{1,0:T(8,128)(2,1)S(1)}, u32[]{:S(2)}) copy-start(bf16[528,128]{1,0:T(8,128)(2,1)S(1)} %collective-permute-done.8.msg_ref) | copy-start | bytes 405508
  64.6 32.4 %collective-permute-start.12 = (bf16[528,128]{1,0:T(8,128)(2,1)S(1)}, bf16[528,128]{1,0:T(8,128)(2,1)S(1)}, u32[]{:S(2)}, u32[]{:S(2)}) collective-permute-start(bf16[528,128]{1,0:T(8,128)(2,1)S(1)} %copy-done.18), channel_id=1, source_target_pairs={{1,0},{2,1},{3,2},{4,3},{5,4},{6,5},{7,6},{8,7},{9,8},{10,9},{11,1... | collective-permute-start | bytes 405512 | tf_op jit(solution)/shard_map/ppermute | solution.py:25
  74.4 0.7 copy-start.12
  74.4 31.1 %collective-permute-start.14 = (bf16[528,128]{1,0:T(8,128)(2,1)S(1)}, bf16[528,128]{1,0:T(8,128)(2,1)S(1)}, u32[]{:S(2)}, u32[]{:S(2)}) collective-permute-start(bf16[528,128]{1,0:T(8,128)(2,1)S(1)} %copy-done.17), channel_id=1, source_target_pairs={{2,0},{3,1},{4,2},{5,3},{6,4},{7,5},{8,6},{9,7},{10,8},{11,9},{12,... | collective-permute-start | bytes 405512 | tf_op jit(solution)/shard_map/ppermute | solution.py:25
  88.1 3.7 %copy-start.10 = (bf16[528,128]{1,0:T(8,128)(2,1)}, bf16[528,128]{1,0:T(8,128)(2,1)S(1)}, u32[]{:S(2)}) copy-start(bf16[528,128]{1,0:T(8,128)(2,1)S(1)} %collective-permute-done.10.msg_ref) | copy-start | bytes 405508
  88.1 31.0 %collective-permute-start.9 = (bf16[256,1024]{1,0:T(8,128)(2,1)}, bf16[256,1024]{1,0:T(8,128)(2,1)S(1)}, u32[]{:S(2)}, u32[]{:S(2)}) collective-permute-start(bf16[256,1024]{1,0:T(8,128)(2,1)} %advect.10), channel_id=1, source_target_pairs={{2,0},{3,1},{4,2},{5,3},{6,4},{7,5},{8,6},{9,7},{10,8},{11,9},{12,... | collective-permute-start | bytes 1572872 | tf_op jit(solution)/shard_map/ppermute | solution.py:25
  97.0 2.7 %copy-start.9 = (bf16[528,128]{1,0:T(8,128)(2,1)}, bf16[528,128]{1,0:T(8,128)(2,1)S(1)}, u32[]{:S(2)}) copy-start(bf16[528,128]{1,0:T(8,128)(2,1)S(1)} %collective-permute-done.12.msg_ref) | copy-start | bytes 405508
  97.0 22.2 %collective-permute-start.11 = (bf16[256,1024]{1,0:T(8,128)(2,1)}, bf16[256,1024]{1,0:T(8,128)(2,1)S(1)}, u32[]{:S(2)}, u32[]{:S(2)}) collective-permute-start(bf16[256,1024]{1,0:T(8,128)(2,1)} %advect.11), channel_id=1, source_target_pairs={{1,0},{2,1},{3,2},{4,3},{5,4},{6,5},{7,6},{8,7},{9,8},{10,9},{11,1... | collective-permute-start | bytes 1572872 | tf_op jit(solution)/shard_map/ppermute | solution.py:25
  105.5 8.3 %copy-start.2 = (bf16[256,1024]{1,0:T(8,128)(2,1)S(1)}, bf16[256,1024]{1,0:T(8,128)(2,1)}, u32[]{:S(2)}) copy-start(bf16[256,1024]{1,0:T(8,128)(2,1)} %advect.15) | copy-start | bytes 1572868
  105.5 0.9 copy-start.8
  105.5 13.7 %collective-permute-start.13 = (bf16[256,1024]{1,0:T(8,128)(2,1)}, bf16[256,1024]{1,0:T(8,128)(2,1)S(1)}, u32[]{:S(2)}, u32[]{:S(2)}) collective-permute-start(bf16[256,1024]{1,0:T(8,128)(2,1)} %advect.13), channel_id=1, source_target_pairs={{15,0},{0,1},{1,2},{2,3},{3,4},{4,5},{5,6},{6,7},{7,8},{8,9},{9,10... | collective-permute-start | bytes 1572872 | tf_op jit(solution)/shard_map/ppermute | solution.py:25
  113.6 5.5 %copy-start = (bf16[256,1024]{1,0:T(8,128)(2,1)}, bf16[256,1024]{1,0:T(8,128)(2,1)S(1)}, u32[]{:S(2)}) copy-start(bf16[256,1024]{1,0:T(8,128)(2,1)S(1)} %collective-permute-done.5.rest_0_) | copy-start | bytes 1572868
  113.6 16.3 %collective-permute-start.15 = (bf16[256,1024]{1,0:T(8,128)(2,1)}, bf16[256,1024]{1,0:T(8,128)(2,1)}, u32[]{:S(2)}, u32[]{:S(2)}) collective-permute-start(bf16[256,1024]{1,0:T(8,128)(2,1)} %advect.14), channel_id=1, source_target_pairs={{14,0},{15,1},{0,2},{1,3},{2,4},{3,5},{4,6},{5,7},{6,8},{7,9},{8,1... | collective-permute-start | bytes 1572872 | tf_op jit(solution)/shard_map/ppermute | solution.py:25
  113.7 5.4 %copy-start.1 = (bf16[256,1024]{1,0:T(8,128)(2,1)}, bf16[256,1024]{1,0:T(8,128)(2,1)S(1)}, u32[]{:S(2)}) copy-start(bf16[256,1024]{1,0:T(8,128)(2,1)S(1)} %collective-permute-done.7.rest_1_) | copy-start | bytes 1572868
  113.7 27.9 %collective-permute-start.17 = (bf16[256,1024]{1,0:T(8,128)(2,1)S(1)}, bf16[256,1024]{1,0:T(8,128)(2,1)}, u32[]{:S(2)}, u32[]{:S(2)}) collective-permute-start(bf16[256,1024]{1,0:T(8,128)(2,1)S(1)} %copy-done.2), channel_id=1, source_target_pairs={{13,0},{14,1},{15,2},{0,3},{1,4},{2,5},{3,6},{4,7},{5,8},{6,9},{7,... | collective-permute-start | bytes 1572872 | tf_op jit(solution)/shard_map/ppermute | solution.py:25
  119.2 22.4 %copy-start.3 = (bf16[256,1024]{1,0:T(8,128)(2,1)}, bf16[256,1024]{1,0:T(8,128)(2,1)S(1)}, u32[]{:S(2)}) copy-start(bf16[256,1024]{1,0:T(8,128)(2,1)S(1)} %collective-permute-done.9.rest_2_) | copy-start | bytes 1572868
  119.2 22.4 %copy-start.4 = (bf16[256,1024]{1,0:T(8,128)(2,1)}, bf16[256,1024]{1,0:T(8,128)(2,1)S(1)}, u32[]{:S(2)}) copy-start(bf16[256,1024]{1,0:T(8,128)(2,1)S(1)} %collective-permute-done.11.rest_3_) | copy-start | bytes 1572868
  119.2 22.4 %copy-start.5 = (bf16[256,1024]{1,0:T(8,128)(2,1)}, bf16[256,1024]{1,0:T(8,128)(2,1)S(1)}, u32[]{:S(2)}) copy-start(bf16[256,1024]{1,0:T(8,128)(2,1)S(1)} %collective-permute-done.13.rest_5_) | copy-start | bytes 1572868

commit v2 on v1

v2 whole, which is shorter than its diff:
```python
import functools

import jax
import jax.numpy as jnp
from jax import lax
from jax.experimental import pallas as pl
from jax.experimental.pallas import tpu as pltpu
from jax.sharding import PartitionSpec as P


CAP = 4
TRAJ = 3
FIRST = -4
LAST = 4
LATE = 3
ORDER = (2, -4, -2, 3, -3, 1, -1, 0)
RIM = 2
LANES = 128
META = 16
CLIP_BOUND = 0.95
F32 = jnp.float32
BF16 = jnp.bfloat16


def shifted(block, axis, distance):
    count = lax.axis_size(axis)
    route = [((i - distance) % count, i) for i in range(count)]
    return lax.ppermute(block, axis, route)


def fill_slots(dep_ref, slot_ref, count_ref, bands):
    for offset in range(LAST - FIRST):
        count_ref[offset] = 0
        for slot in range(CAP):
            slot_ref[offset * CAP + slot] = -1

    def place(band, carry):
        offset = dep_ref[0, 0, band] - FIRST
        ordinal = count_ref[offset]
        slot_ref[offset * CAP + ordinal] = band
        count_ref[offset] = ordinal + 1
        return carry

    lax.fori_loop(0, bands, place, 0)


def wind_perm(rows, levels, kinds):
    shape = (rows, kinds * LANES)
    row = lax.broadcasted_iota(jnp.int32, shape, 0)
    column = lax.broadcasted_iota(jnp.int32, shape, 1)
    bits = levels.bit_length() - 1
    kind = lax.shift_right_logical(row, bits) & 3
    group = lax.shift_right_logical(row, bits + 2)
    place = kind * LANES + group * levels + (row & (levels - 1))
    return jnp.where(place == column, 1.0, 0.0).astype(BF16)


def wind_kernel(sizes, dep_hbm_ref, wind_hbm_ref, tracers_ref, *rest):
    columns, rows, inner, bands, band_rows = sizes
    outs = rest[: LAST - FIRST]
    (
        dep_ref,
        wind_ref,
        wide_ref,
        here_ref,
        perm_ref,
        edge_ref,
        sem_ref,
        wind_sem_ref,
        slot_ref,
        count_ref,
    ) = rest[LAST - FIRST :]
    groups = columns // inner
    halves = tracers_ref.shape[-1] // LANES
    pitch = rows + 1
    chunks = [
        pltpu.make_async_copy(
            wind_hbm_ref.at[pl.ds(g * inner, inner)],
            wind_ref.at[pl.ds(g * inner, inner)],
            wind_sem_ref.at[g],
        )
        for g in range(groups)
    ]
    edges = [
        pltpu.make_async_copy(
            tracers_ref.at[pl.ds(side * (columns - RIM), RIM)], edge_ref.at[side], sem_ref.at[side]
        )
        for side in range(2)
    ]
    table = pltpu.make_async_copy(dep_hbm_ref, dep_ref, sem_ref.at[2])
    for copy in [table] + chunks + edges:
        copy.start()
    perm_ref[...] = wind_perm(perm_ref.shape[0], LANES // groups, 2)
    table.wait()
    fill_slots(dep_ref, slot_ref, count_ref, bands)

    def widen(column, carry):
        wide_ref[pl.ds(column * pitch, rows), :] = wind_ref[column].astype(F32)
        return carry

    for g in range(groups):
        chunks[g].wait()
        lax.fori_loop(g * inner, (g + 1) * inner, widen, 0, unroll=4)


    def some_rows(block, carry):
        left = jnp.concatenate(
            [
                jnp.concatenate(
                    [
                        wide_ref[pl.ds(g * inner * pitch + block * 16 + step, inner, stride=pitch), :]
                        for g in range(groups)
                    ],
                    axis=1,
                )
                for step in range(16)
            ],
            axis=0,
        ).astype(BF16)
        moved = jnp.dot(left, perm_ref[...], preferred_element_type=F32)
        for comp in range(2):
            here_ref[comp, pl.ds(block * 16, 16)] = moved[
                :, comp * LANES : (comp + 1) * LANES
            ].reshape(16, inner, LANES)
        return carry

    lax.fori_loop(0, rows // 16, some_rows, 0)
    lane = lax.broadcasted_iota(jnp.int32, (META, LANES), 1)
    size = band_rows * inner
    for offset in range(LAST - FIRST):
        meta = jnp.full((META, LANES), -1.0, F32)
        for slot in range(CAP):
            band = slot_ref[offset * CAP + slot]
            safe = jnp.maximum(band, 0)
            source = jnp.where(band >= 0, safe - dep_ref[0, 1, safe], -1)
            meta = jnp.where(lane == slot, source.astype(F32), meta)
            for comp in range(2):
                outs[offset][pl.ds((slot * 2 + comp) * size, size), :] = (
                    here_ref[comp, pl.ds(safe * band_rows, band_rows)]
                    .reshape(size, LANES)
                    .astype(BF16)
                )
        at = CAP * 2 * size
        outs[offset][pl.ds(at, META), :] = meta.astype(BF16)
        if abs(offset + FIRST) != 1:
            continue
        at += META
        side = 0 if offset + FIRST == 1 else 1
        edges[side].wait()
        for rim in range(RIM):
            column = side * (columns - RIM) + rim
            for half in range(halves):
                outs[offset][pl.ds(at, rows), :] = edge_ref[
                    side, rim, :, half * LANES : (half + 1) * LANES
                ]
                at += rows
            outs[offset][pl.ds(at, rows), :] = wind_ref[column]
            at += rows


def prepare_kernel(
    sizes,
    tracers_ref,
    wind_ref,
    low_ref,
    high_ref,
    perm_ref,
    out_t_ref,
    out_e_ref,
    wide_t_ref,
    wide_w_ref,
    wind_perm_ref,
):
    columns, rows, inner, padded_inner, rim_at = sizes
    batch = 16
    groups = columns // inner
    tracer_ch = tracers_ref.shape[-1]
    halves = tracer_ch // LANES
    pitch = rows + 1

    wind_perm_ref[...] = wind_perm(wind_perm_ref.shape[0], LANES // groups, 4)

    def own(column, carry):
        at = pl.ds((RIM + column) * pitch, rows)
        for half in range(halves):
            wide_t_ref[half, at, :] = tracers_ref[
                column, :, half * LANES : (half + 1) * LANES
            ].astype(F32)
        wide_w_ref[at, :] = wind_ref[column].astype(F32)
        return carry

    lax.fori_loop(0, columns, own, 0, unroll=4)
    for side, ref in ((0, low_ref), (columns + RIM, high_ref)):
        for rim in range(RIM):
            start = rim_at + rim * (halves + 1) * rows
            at = pl.ds((side + rim) * pitch, rows)
            for half in range(halves):
                wide_t_ref[half, at, :] = ref[pl.ds(start + half * rows, rows), :].astype(F32)
            wide_w_ref[at, :] = ref[pl.ds(start + halves * rows, rows), :].astype(F32)
    for column in range(columns + 2 * RIM, columns - inner + padded_inner):
        at = pl.ds(column * pitch, pitch)
        for half in range(halves):
            wide_t_ref[half, at, :] = jnp.zeros((pitch, LANES), F32)
        wide_w_ref[at, :] = jnp.zeros((pitch, LANES), F32)

    def some_rows(block, carry):
        parts_t = []
        parts_w = []
        for step in range(batch):
            pieces_t = []
            pieces_w = []
            for g in range(groups):
                at = pl.ds(g * inner * pitch + block * batch + step, padded_inner, stride=pitch)
                for half in range(halves):
                    pieces_t.append(wide_t_ref[half, at, :])
                pieces_w.append(wide_w_ref[at, :])
            parts_t.append(jnp.concatenate(pieces_t, axis=1))
            parts_w.append(jnp.concatenate(pieces_w, axis=1))
        left_t = jnp.concatenate(parts_t, axis=0).astype(BF16)
        left_w = jnp.concatenate(parts_w, axis=0).astype(BF16)
        at = pl.ds(RIM + block * batch, batch)
        shape = (batch, padded_inner, LANES)
        moved = jnp.dot(left_w, wind_perm_ref[...], preferred_element_type=F32)
        for comp in range(2):
            now = moved[:, comp * LANES : (comp + 1) * LANES]
            before = moved[:, (comp + 2) * LANES : (comp + 3) * LANES]
            out_e_ref[comp, at] = (2.0 * now - before).reshape(shape)
        moved = jnp.dot(left_t, perm_ref[...], preferred_element_type=F32)
        for kind in range(out_t_ref.shape[0]):
            out_t_ref[kind, at] = moved[:, kind * LANES : (kind + 1) * LANES].reshape(shape)
        return carry

    lax.fori_loop(0, rows // batch, some_rows, 0)
    for ref in (out_t_ref, out_e_ref):
        for kind in range(ref.shape[0]):
            for rim in range(RIM):
                ref[kind, rim] = ref[kind, RIM]
                ref[kind, RIM + rows + rim] = ref[kind, RIM + rows - 1]


def cubic_weights(shift):
    e = jnp.abs(shift)
    positive = shift > 0.0
    one_less = 1.0 - e
    one_more = 1.0 + e
    two_less = 2.0 - e
    center = 0.5 * one_less * two_less * one_more
    near = 0.5 * e * two_less * one_more
    across = e * one_less * (-1.0 / 6.0)
    beyond = across * two_less
    far = across * one_more
    zero = jnp.zeros_like(e)
    return (
        jnp.where(positive, far, zero),
        jnp.where(positive, near, beyond),
        center,
        jnp.where(positive, beyond, near),
        jnp.where(positive, zero, far),
    ), positive


def linear_weights(shift):
    return jnp.maximum(shift, 0.0), 1.0 - jnp.abs(shift), jnp.maximum(-shift, 0.0)


def clipped(value):
    return jnp.clip(value, -CLIP_BOUND, CLIP_BOUND)


def advect_kernel(sizes, msg_ref, t_ref, e_ref, perm_ref, out_ref, result_ref, source_ref):
    inner, band_rows = sizes
    size = band_rows * inner
    per_level = t_ref.shape[0]
    meta = msg_ref[pl.ds(CAP * 2 * size, META), :].astype(F32)
    lane = lax.broadcasted_iota(jnp.int32, (META, LANES), 1)
    for slot in range(CAP):
        source_ref[slot] = jnp.max(jnp.where(lane == slot, meta, -1.0)).astype(jnp.int32)

    def one_slot(slot, carry):
        source = source_ref[slot]

        @pl.when(source >= 0)
        def _():
            first = source * band_rows + RIM

            def one_row(row, inner_carry):
                here = [
                    msg_ref[pl.ds((slot * 2 + comp) * size + row * inner, inner), :].astype(F32)
                    for comp in range(2)
                ]
                for eight in range(inner // 8):
                    base = eight * 8
                    wind = [h[base : base + 8] for h in here]
                    window = [
                        [
                            [
                                e_ref[comp, first + row + b, pl.ds(base + RIM + a, 8), :]
                                for a in (-1, 0, 1)
                            ]
                            for b in (-1, 0, 1)
                        ]
                        for comp in range(2)
                    ]
                    shift = [clipped(w) for w in wind]
                    for _ in range(TRAJ):
                        lon = linear_weights(shift[0])
                        lat = linear_weights(shift[1])
                        moved = []
                        for comp in range(2):
                            total = None
                            for b in range(3):
                                line = (
                                    lon[0] * window[comp][b][0]
                                    + lon[1] * window[comp][b][1]
                                    + lon[2] * window[comp][b][2]
                                )
                                line = lat[b] * line
                                total = line if total is None else total + line
                            moved.append(clipped(0.5 * (wind[comp] + total)))
                        shift = moved
                    lon_cubic, _ = cubic_weights(shift[0])
                    lat_cubic, north = cubic_weights(shift[1])
                    low, mid, high = linear_weights(shift[0])
                    zero = jnp.zeros_like(low)
                    lon_linear = (zero, low, mid, high, zero)
                    taps = []
                    for b in range(-2, 3):
                        for a in range(-2, 3):
                            if abs(b) == 2:
                                if abs(a) == 2:
                                    continue
                                weight = lon_linear[a + 2]
                            elif b == 0:
                                weight = lon_cubic[a + 2]
                            elif b == -1:
                                weight = jnp.where(north, lon_cubic[a + 2], lon_linear[a + 2])
                            else:
                                weight = jnp.where(north, lon_linear[a + 2], lon_cubic[a + 2])
                            taps.append((a, b, weight * lat_cubic[b + 2]))
                    for tracer in range(per_level):
                        total = None
                        for a, b, weight in taps:
                            term = weight * t_ref[
                                tracer, first + row + b, pl.ds(base + RIM + a, 8), :
                            ]
                            total = term if total is None else total + term
                        result_ref[
                            pl.ds(slot * size + row * inner + base, 8),
                            tracer * LANES : (tracer + 1) * LANES,
                        ] = total
                return inner_carry

            lax.fori_loop(0, band_rows, one_row, 0)

        return carry

    lax.fori_loop(0, CAP, one_slot, 0)
    out_ref[...] = jnp.dot(
        result_ref[...].astype(BF16), perm_ref[...], preferred_element_type=F32
    ).astype(BF16)


def collect(sizes, slot_ref, ins, wide_ref):
    columns, rows, inner, _, band_rows = sizes
    pitch = rows + 1
    size = band_rows * inner
    halves = wide_ref.shape[0]
    for offset, in_ref in ins:

        def one_slot(slot, carry):
            band = slot_ref[(offset - FIRST) * CAP + slot]

            @pl.when(band >= 0)
            def _():
                for row in range(band_rows):
                    value = in_ref[pl.ds(slot * size + row * inner, inner), :]
                    for g in range(columns // inner):
                        at = pl.ds(
                            g * inner * pitch + band * band_rows + row, inner, stride=pitch
                        )
                        for half in range(halves):
                            first = (g * halves + half) * LANES
                            wide_ref[half, at, :] = value[:, first : first + LANES].astype(F32)

            return carry

        lax.fori_loop(0, CAP, one_slot, 0)


def early_kernel(sizes, offsets, dep_ref, *rest):
    ins = rest[: len(offsets)]
    wide_ref, slot_ref, count_ref = rest[len(offsets) :]
    fill_slots(dep_ref, slot_ref, count_ref, sizes[3])
    collect(sizes, slot_ref, zip(offsets, ins), wide_ref)


def late_kernel(sizes, offsets, dep_ref, *rest):
    columns, rows = sizes[:2]
    ins = rest[: len(offsets)]
    _, out_ref, wide_ref, slot_ref, count_ref, stage_ref, sem_ref = rest[len(offsets) :]
    fill_slots(dep_ref, slot_ref, count_ref, sizes[3])
    collect(sizes, slot_ref, zip(offsets, ins), wide_ref)
    pitch = rows + 1
    halves = wide_ref.shape[0]
    chunks = sem_ref.shape[0]
    width = columns // chunks
    copies = [
        pltpu.make_async_copy(
            stage_ref.at[pl.ds(n * width, width)], out_ref.at[pl.ds(n * width, width)], sem_ref.at[n]
        )
        for n in range(chunks)
    ]

    def narrow(column, carry):
        at = pl.ds(column * pitch, rows)
        for half in range(halves):
            stage_ref[column, :, half * LANES : (half + 1) * LANES] = wide_ref[half, at, :].astype(
                BF16
            )
        return carry

    for n in range(chunks):
        lax.fori_loop(n * width, (n + 1) * width, narrow, 0, unroll=4)
        copies[n].start()
    for copy in copies:
        copy.wait()


def on_device(tracers, wind_fields, departures):
    columns, rows, tracer_ch = tracers.shape
    levels = wind_fields.shape[-1] // 4
    per_level = tracer_ch // levels
    bands = departures.shape[1]
    band_rows = rows // bands
    inner = columns * levels // LANES
    padded_inner = -(-(inner + 2 * RIM) // 8) * 8
    size = band_rows * inner
    offsets = LAST - FIRST
    halves = tracer_ch // LANES
    rim_at = CAP * 2 * size + META
    rim_rows = RIM * (halves + 1) * rows

    wide = per_level * LANES
    index = jnp.arange(wide, dtype=jnp.int32)
    place = (index // levels) % (LANES // levels) * tracer_ch + index % levels * per_level
    place = place + index // LANES
    spread = (place[None, :] == index[:, None]).astype(BF16)
    join = (place[:, None] == index[None, :]).astype(BF16)
    table = jnp.transpose(departures, (0, 2, 1))

    vmem = pl.BlockSpec(memory_space=pltpu.VMEM)
    smem = pl.BlockSpec(memory_space=pltpu.SMEM)
    hbm = pl.BlockSpec(memory_space=pltpu.HBM)
    tables = [pltpu.SMEM((offsets * CAP,), jnp.int32), pltpu.SMEM((offsets,), jnp.int32)]

    def params(mib):
        return pltpu.CompilerParams(vmem_limit_bytes=mib << 20)

    messages = pl.pallas_call(
        functools.partial(wind_kernel, (columns, rows, inner, bands, band_rows)),
        out_shape=[
            jax.ShapeDtypeStruct((rim_at + (rim_rows if abs(n) == 1 else 0), LANES), BF16)
            for n in range(FIRST, LAST)
        ],
        in_specs=[hbm] * 3,
        out_specs=[vmem] * offsets,
        scratch_shapes=[
            pltpu.SMEM(table.shape, jnp.int32),
            pltpu.VMEM(wind_fields.shape, BF16),
            pltpu.VMEM((columns * (rows + 1), LANES), F32),
            pltpu.VMEM((2, rows, inner, LANES), F32),
            pltpu.VMEM((columns // inner * LANES, 2 * LANES), BF16),
            pltpu.VMEM((2, RIM, rows, tracer_ch), BF16),
            pltpu.SemaphoreType.DMA((3,)),
            pltpu.SemaphoreType.DMA((columns // inner,)),
        ]
        + tables,
        compiler_params=params(16),
        cost_estimate=pl.CostEstimate(flops=4_000_000, bytes_accessed=3_000_000, transcendentals=0),
        name="winds",
    )(*(pltpu.with_memory_space_constraint(x, pltpu.HBM) for x in (table, wind_fields, tracers)))

    arrived = {}
    for n in ORDER:
        msg = messages[n - FIRST]
        arrived[n] = msg if n == 0 else shifted(msg, "lon", -n)

    all_rows = (columns - inner + padded_inner) * (rows + 1)
    prepare = pl.pallas_call(
        functools.partial(prepare_kernel, (columns, rows, inner, padded_inner, rim_at)),
        out_shape=[
            jax.ShapeDtypeStruct((per_level, rows + 2 * RIM, padded_inner, LANES), F32),
            jax.ShapeDtypeStruct((2, rows + 2 * RIM, padded_inner, LANES), F32),
        ],
        in_specs=[vmem] * 5,
        out_specs=[vmem] * 2,
        scratch_shapes=[
            pltpu.VMEM((halves, all_rows, LANES), F32),
            pltpu.VMEM((all_rows, LANES), F32),
            pltpu.VMEM((columns // inner * LANES, 4 * LANES), BF16),
        ],
        compiler_params=params(32),
        cost_estimate=pl.CostEstimate(
            flops=16_000_000, bytes_accessed=12_000_000, transcendentals=0
        ),
        name="prepare",
    )
    fields, extra = prepare(tracers, wind_fields, arrived[-1], arrived[1], spread)

    advect = pl.pallas_call(
        functools.partial(advect_kernel, (inner, band_rows)),
        out_shape=jax.ShapeDtypeStruct((CAP * size, wide), BF16),
        in_specs=[vmem] * 4,
        out_specs=vmem,
        scratch_shapes=[
            pltpu.VMEM((CAP * size, wide), F32),
            pltpu.SMEM((CAP,), jnp.int32),
        ],
        compiler_params=params(12),
        cost_estimate=pl.CostEstimate(
            flops=16_000_000, bytes_accessed=6_000_000, transcendentals=0
        ),
        name="advect",
    )
    received = [None] * offsets
    for n in ORDER:
        result = advect(arrived[n], fields, extra, join)
        received[n - FIRST] = result if n == 0 else shifted(result, "lon", n)

    sizes = (columns, rows, inner, bands, band_rows)
    wide_shape = jax.ShapeDtypeStruct((halves, columns * (rows + 1), LANES), F32)
    early = ORDER[: offsets - 1 - LATE] + ORDER[-1:]
    late = ORDER[offsets - 1 - LATE : -1]
    first = pl.pallas_call(
        functools.partial(early_kernel, sizes, early),
        out_shape=wide_shape,
        in_specs=[smem] + [vmem] * len(early),
        out_specs=vmem,
        scratch_shapes=tables,
        compiler_params=params(8),
        cost_estimate=pl.CostEstimate(flops=2_000_000, bytes_accessed=6_000_000, transcendentals=0),
        name="early",
    )
    spread_out = first(table, *[received[n - FIRST] for n in early])
    last = pl.pallas_call(
        functools.partial(late_kernel, sizes, late),
        out_shape=[jax.ShapeDtypeStruct((columns, rows, tracer_ch), BF16), wide_shape],
        in_specs=[smem] + [vmem] * (len(late) + 1),
        out_specs=[pl.BlockSpec(memory_space=pl.ANY), vmem],
        scratch_shapes=tables
        + [pltpu.VMEM((columns, rows, tracer_ch), BF16), pltpu.SemaphoreType.DMA((8,))],
        input_output_aliases={len(late) + 1: 1},
        compiler_params=params(8),
        cost_estimate=pl.CostEstimate(flops=2_000_000, bytes_accessed=6_000_000, transcendentals=0),
        name="late",
    )
    return last(table, *[received[n - FIRST] for n in late], spread_out)[0]


def solution(mesh):
    placed = (
        P(("groups", "lon"), None, None),
        P(("groups", "lon"), None, None),
        P(("groups", "lon"), None, None),
    )
    return jax.shard_map(
        on_device,
        mesh=mesh,
        in_specs=placed,
        out_specs=P(("groups", "lon"), None, None),
        check_vma=False,
    )
```

time: 148 us -> 99.3 us (0.67); the launches traced: 150 us -> 99.2 us
  Pallas kernels: 79 us -> 32.5 us
  waiting for transfers between devices: 29.7 us -> 44.7 us
  starting transfers between devices: 32.3 us -> 20.6 us
  local copies, waits for them, and re-layouts: 6.25 us -> 0.01 us
    pallas_call x11 -> x12, Pallas kernels: 79 us -> 32.5 us  [the longest x8 20.7 us: on_device(): result = advect(arrived[n], fields, extra, join)]
    ppermute x18 -> x14, waiting for transfers between devices: 29.7 us -> 44.7 us  [shifted(): return lax.ppermute(block, axis, route)]
    ppermute x18 -> x14, starting transfers between devices: 32.3 us -> 20.6 us  [shifted(): return lax.ppermute(block, axis, route)]
    unnamed x45 -> x6, local copies, waits for them, and re-layouts: 4.59 us -> 0.01 us
    slice x2 -> x0, local copies, waits for them, and re-layouts: 1.66 us -> none  [the longest x1 0.88 us: on_device(): high_t = shifted(tracers[:RIM], 'lon', -1)]
  transfers between devices with their start and end apart: 18 -> 14, of which waited for: 4 -> 6; matrix products, arithmetic and copies ran while one was open for 3% -> 1% of each run, Pallas kernels for 47% -> 28%
where the time goes in v2:
time: 99.3 us; the launch traced here: 99.2 us
  waiting for transfers between devices  44.7 us (45%)
  Pallas kernels  32.5 us (33%)
  starting transfers between devices  20.6 us (21%)
  other arithmetic  1.3 us (1%)
    ppermute x14, waiting for transfers between devices, shifted(): return lax.ppermute(block, axis, route)  44.7 us
    pallas_call x8, Pallas kernels, on_device(): result = advect(arrived[n], fields, extra, join)  20.7 us
    ppermute x14, starting transfers between devices, shifted(): return lax.ppermute(block, axis, route)  20.6 us
    pallas_call x1, Pallas kernels, on_device(): prepare(tracers, wind_fields, arrived[-1], arrived[1], spread)  5.49 us
    pallas_call x1, Pallas kernels, on_device(): pl.pallas_call(functools.partial(wind_kernel, (columns, rows, inner, band...  2.55 us
    pallas_call x1, Pallas kernels, on_device(): return last(table, *[received[n - FIRST] for n in late], spread_out)[0]  2.48 us
  transfers between devices with their start and end apart: 14, of which 6 were waited for; matrix products, arithmetic and copies ran while one was open for 1% of the time, Pallas kernels for 28%

profile of v2, /device:TPU:1, one launch (start us, length us, event | category | flops | bytes accessed | tf_op | source)
XLA Modules:
  0.0 99.2 jit_solution(5469557715390240853)
XLA Ops:
  0.0 0.0 copy-start.1
  0.0 0.0 copy-start
  0.0 2.5 %winds.1 = (bf16[528,128]{1,0:T(8,128)(2,1)S(1)}, bf16[528,128]{1,0:T(8,128)(2,1)S(1)}, bf16[528,128]{1,0:T(8,128)(2,1)S(1)}, bf16[912,128]{1,0:T(8,128)(2,1)S(1...) custom-call(s32[1,2,16]{2,1,0:T(2,128)} %bitcast.1, ...), custom_call_target="tpu_custom_call" | custom-call | flops 4000000 | bytes 3000000 | tf_op jit(solution)/shard_map/winds/pallas_call | solution.py:459
  2.6 5.1 %collective-permute-start.6 = (bf16[528,128]{1,0:T(8,128)(2,1)S(1)}, bf16[528,128]{1,0:T(8,128)(2,1)S(1)}, u32[]{:S(2)}, u32[]{:S(2)}) collective-permute-start(bf16[528,128]{1,0:T(8,128)(2,1)S(1)} %get-tuple-element.21), channel_id=1, source_target_pairs={{2,0},{3,1},{4,2},{5,3},{6,4},{7,5},{8,6},{9,7},{10,8},{11,9},{12,... | collective-permute-start | bytes 405512 | tf_op jit(solution)/shard_map/ppermute | solution.py:28
  7.7 0.0 collective-permute-start.8
  7.7 0.0 collective-permute-start.1
  7.7 1.0 collective-permute-start.2
  8.7 1.3 %fusion.1 = (bf16[1024,1024]{1,0:T(8,128)(2,1)S(1)}, bf16[1024,1024]{1,0:T(8,128)(2,1)S(1)}) fusion(s32[1024]{0:T(1024)S(1)} %fusion.11), kind=kLoop, calls=%fused_computation.3 | loop fusion | flops 4194304 | bytes 4198400 | tf_op jit(solution)/shard_map/convert_element_type | solution.py:448
  10.0 1.5 %collective-permute-done.1.low_ref.msg_ref = bf16[912,128]{1,0:T(8,128)(2,1)S(1)} collective-permute-done((bf16[912,128]{1,0:T(8,128)(2,1)S(1)}, bf16[912,128]{1,0:T(8,128)(2,1)S(1)}, u32[]{:S(2)}, u32[]{:S(2)}) %collective-permute-start.1) | collective-permute-done | bytes 233504 | tf_op jit(solution)/shard_map/ppermute | solution.py:28
  11.5 1.7 %collective-permute-done.2.high_ref.msg_ref = bf16[912,128]{1,0:T(8,128)(2,1)S(1)} collective-permute-done((bf16[912,128]{1,0:T(8,128)(2,1)S(1)}, bf16[912,128]{1,0:T(8,128)(2,1)S(1)}, u32[]{:S(2)}, u32[]{:S(2)}) %collective-permute-start.2) | collective-permute-done | bytes 233504 | tf_op jit(solution)/shard_map/ppermute | solution.py:28
  13.2 0.0 copy-done.1
  13.2 0.0 copy-done
  13.2 5.5 %prepare.1 = (f32[8,68,24,128]{3,2,1,0:T(8,128)S(1)}, f32[2,68,24,128]{3,2,1,0:T(8,128)S(1)}) custom-call(bf16[64,64,256]{2,1,0:T(8,128)(2,1)S(1)} %copy-done, bf16[64,64,128]{2,1,0:T(8,128)(2,1)S(1)} %copy-done.1, bf16[912,128]{1,0:T(8,128)(2,1)S(1)} %collective-permute-done.1.low_ref.msg_ref, bf16[912,128]{1,0:T(8,128)(2,1)S(1)} %collective-permute-done.2.high_ref.msg_ref, ...), custom_call_target="tpu_custom_call" | custom-call | flops 16000000 | bytes 12000000 | tf_op jit(solution)/shard_map/prepare/pallas_call | solution.py:508
  18.7 0.0 collective-permute-done.6.msg_ref
  18.7 2.3 %advect.11 = bf16[256,1024]{1,0:T(8,128)(2,1)S(1)} custom-call(bf16[528,128]{1,0:T(8,128)(2,1)S(1)} %collective-permute-done.6.msg_ref, f32[8,68,24,128]{3,2,1,0:T(8,128)S(1)} %get-tuple-element.19.t_ref, f32[2,68,24,128]{3,2,1,0:T(8,128)S(1)} %get-tuple-element.20.e_ref, bf16[1024,1024]{1,0:T(8,128)(2,1)S(1)} %get-tuple-element.27.perm_ref), custom_call_target="tpu_custom_call" | custom-call | flops 16000000 | bytes 6000000 | tf_op jit(solution)/shard_map/advect/pallas_call | solution.py:527
  21.0 6.1 %collective-permute-start.7 = (bf16[256,1024]{1,0:T(8,128)(2,1)S(1)}, bf16[256,1024]{1,0:T(8,128)(2,1)S(1)}, u32[]{:S(2)}, u32[]{:S(2)}) collective-permute-start(bf16[256,1024]{1,0:T(8,128)(2,1)S(1)} %advect.11), channel_id=1, source_target_pairs={{14,0},{15,1},{0,2},{1,3},{2,4},{3,5},{4,6},{5,7},{6,8},{7,9},{8,1... | collective-permute-start | bytes 1572872 | tf_op jit(solution)/shard_map/ppermute | solution.py:28
  27.1 0.0 collective-permute-done.8.msg_ref
  27.1 3.0 %advect.12 = bf16[256,1024]{1,0:T(8,128)(2,1)S(1)} custom-call(bf16[528,128]{1,0:T(8,128)(2,1)S(1)} %collective-permute-done.8.msg_ref, f32[8,68,24,128]{3,2,1,0:T(8,128)S(1)} %get-tuple-element.19.t_ref, f32[2,68,24,128]{3,2,1,0:T(8,128)S(1)} %get-tuple-element.20.e_ref, bf16[1024,1024]{1,0:T(8,128)(2,1)S(1)} %get-tuple-element.27.perm_ref), custom_call_target="tpu_custom_call" | custom-call | flops 16000000 | bytes 6000000 | tf_op jit(solution)/shard_map/advect/pallas_call | solution.py:527
  30.2 0.8 collective-permute-start.9
  31.0 0.0 collective-permute-start
  31.0 0.0 collective-permute-start.10
  31.0 4.9 %collective-permute-start.12 = (bf16[528,128]{1,0:T(8,128)(2,1)S(1)}, bf16[528,128]{1,0:T(8,128)(2,1)S(1)}, u32[]{:S(2)}, u32[]{:S(2)}) collective-permute-start(bf16[528,128]{1,0:T(8,128)(2,1)S(1)} %get-tuple-element.24), channel_id=1, source_target_pairs={{3,0},{4,1},{5,2},{6,3},{7,4},{8,5},{9,6},{10,7},{11,8},{12,9},{13... | collective-permute-start | bytes 405512 | tf_op jit(solution)/shard_map/ppermute | solution.py:28
  35.9 19.1 %collective-permute-done.msg_ref = bf16[528,128]{1,0:T(8,128)(2,1)S(1)} collective-permute-done((bf16[528,128]{1,0:T(8,128)(2,1)S(1)}, bf16[528,128]{1,0:T(8,128)(2,1)S(1)}, u32[]{:S(2)}, u32[]{:S(2)}) %collective-permute-start) | collective-permute-done | bytes 135200 | tf_op jit(solution)/shard_map/ppermute | solution.py:28
  55.0 3.8 %advect.8 = bf16[256,1024]{1,0:T(8,128)(2,1)S(1)} custom-call(bf16[528,128]{1,0:T(8,128)(2,1)S(1)} %collective-permute-done.msg_ref, f32[8,68,24,128]{3,2,1,0:T(8,128)S(1)} %get-tuple-element.19.t_ref, f32[2,68,24,128]{3,2,1,0:T(8,128)S(1)} %get-tuple-element.20.e_ref, bf16[1024,1024]{1,0:T(8,128)(2,1)S(1)} %get-tuple-element.27.perm_ref), custom_call_target="tpu_custom_call" | custom-call | flops 16000000 | bytes 6000000 | tf_op jit(solution)/shard_map/advect/pallas_call | solution.py:527
  58.7 1.0 %collective-permute-start.3 = (bf16[256,1024]{1,0:T(8,128)(2,1)S(1)}, bf16[256,1024]{1,0:T(8,128)(2,1)S(1)}, u32[]{:S(2)}, u32[]{:S(2)}) collective-permute-start(bf16[256,1024]{1,0:T(8,128)(2,1)S(1)} %advect.8), channel_id=1, source_target_pairs={{3,0},{4,1},{5,2},{6,3},{7,4},{8,5},{9,6},{10,7},{11,8},{12,9},{13... | collective-permute-start | bytes 1572872 | tf_op jit(solution)/shard_map/ppermute | solution.py:28
  59.8 0.0 collective-permute-done.10.msg_ref
  59.8 1.6 %advect.13 = bf16[256,1024]{1,0:T(8,128)(2,1)S(1)} custom-call(bf16[528,128]{1,0:T(8,128)(2,1)S(1)} %collective-permute-done.10.msg_ref, f32[8,68,24,128]{3,2,1,0:T(8,128)S(1)} %get-tuple-element.19.t_ref, f32[2,68,24,128]{3,2,1,0:T(8,128)S(1)} %get-tuple-element.20.e_ref, bf16[1024,1024]{1,0:T(8,128)(2,1)S(1)} %get-tuple-element.27.perm_ref), custom_call_target="tpu_custom_call" | custom-call | flops 16000000 | bytes 6000000 | tf_op jit(solution)/shard_map/advect/pallas_call | solution.py:527
  61.4 0.1 collective-permute-start.11
  61.5 0.0 collective-permute-done.12.msg_ref
  61.5 3.0 %advect.14 = bf16[256,1024]{1,0:T(8,128)(2,1)S(1)} custom-call(bf16[528,128]{1,0:T(8,128)(2,1)S(1)} %collective-permute-done.12.msg_ref, f32[8,68,24,128]{3,2,1,0:T(8,128)S(1)} %get-tuple-element.19.t_ref, f32[2,68,24,128]{3,2,1,0:T(8,128)S(1)} %get-tuple-element.20.e_ref, bf16[1024,1024]{1,0:T(8,128)(2,1)S(1)} %get-tuple-element.27.perm_ref), custom_call_target="tpu_custom_call" | custom-call | flops 16000000 | bytes 6000000 | tf_op jit(solution)/shard_map/advect/pallas_call | solution.py:527
  64.5 0.8 collective-permute-start.13
  65.3 2.3 %advect.10 = bf16[256,1024]{1,0:T(8,128)(2,1)S(1)} custom-call(bf16[912,128]{1,0:T(8,128)(2,1)S(1)} %collective-permute-done.1.low_ref.msg_ref, f32[8,68,24,128]{3,2,1,0:T(8,128)S(1)} %get-tuple-element.19.t_ref, f32[2,68,24,128]{3,2,1,0:T(8,128)S(1)} %get-tuple-element.20.e_ref, bf16[1024,1024]{1,0:T(8,128)(2,1)S(1)} %get-tuple-element.27.perm_ref), custom_call_target="tpu_custom_call" | custom-call | flops 16000000 | bytes 6000000 | tf_op jit(solution)/shard_map/advect/pallas_call | solution.py:527
  67.7 2.3 %advect.9 = bf16[256,1024]{1,0:T(8,128)(2,1)S(1)} custom-call(bf16[912,128]{1,0:T(8,128)(2,1)S(1)} %collective-permute-done.2.high_ref.msg_ref, f32[8,68,24,128]{3,2,1,0:T(8,128)S(1)} %get-tuple-element.19.t_ref, f32[2,68,24,128]{3,2,1,0:T(8,128)S(1)} %get-tuple-element.20.e_ref, bf16[1024,1024]{1,0:T(8,128)(2,1)S(1)} %get-tuple-element.27.perm_ref), custom_call_target="tpu_custom_call" | custom-call | flops 16000000 | bytes 6000000 | tf_op jit(solution)/shard_map/advect/pallas_call | solution.py:527
  70.0 0.0 collective-permute-done.7.rest_0_
  70.0 0.7 collective-permute-start.4
  70.7 0.0 collective-permute-done.9.rest_1_
  70.7 0.0 collective-permute-start.5
  70.7 0.0 copy-start.2
  70.7 2.3 %advect.15.rest_4_ = bf16[256,1024]{1,0:T(8,128)(2,1)S(1)} custom-call(bf16[528,128]{1,0:T(8,128)(2,1)S(1)} %get-tuple-element.25.msg_ref, f32[8,68,24,128]{3,2,1,0:T(8,128)S(1)} %get-tuple-element.19.t_ref, f32[2,68,24,128]{3,2,1,0:T(8,128)S(1)} %get-tuple-element.20.e_ref, bf16[1024,1024]{1,0:T(8,128)(2,1)S(1)} %get-tuple-element.27.perm_ref), custom_call_target="tpu_custom_call" | custom-call | flops 16000000 | bytes 6000000 | tf_op jit(solution)/shard_map/advect/pallas_call | solution.py:527
  73.1 13.5 %collective-permute-done.11.rest_2_ = bf16[256,1024]{1,0:T(8,128)(2,1)S(1)} collective-permute-done((bf16[256,1024]{1,0:T(8,128)(2,1)S(1)}, bf16[256,1024]{1,0:T(8,128)(2,1)S(1)}, u32[]{:S(2)}, u32[]{:S(2)}) %collective-permute-start.11) | collective-permute-done | bytes 524320 | tf_op jit(solution)/shard_map/ppermute | solution.py:28
  86.6 6.4 %collective-permute-done.13.rest_3_ = bf16[256,1024]{1,0:T(8,128)(2,1)S(1)} collective-permute-done((bf16[256,1024]{1,0:T(8,128)(2,1)S(1)}, bf16[256,1024]{1,0:T(8,128)(2,1)S(1)}, u32[]{:S(2)}, u32[]{:S(2)}) %collective-permute-start.13) | collective-permute-done | bytes 524320 | tf_op jit(solution)/shard_map/ppermute | solution.py:28
  93.0 0.0 copy-done.2
  93.0 1.2 %early.1.rest_3_ = f32[2,4160,128]{2,1,0:T(8,128)S(1)} custom-call(s32[1,2,16]{2,1,0:T(2,128)S(1)} %bitcast.2, bf16[256,1024]{1,0:T(8,128)(2,1)S(1)} %collective-permute-done.7.rest_0_, bf16[256,1024]{1,0:T(8,128)(2,1)S(1)} %collective-permute-done.9.rest_1_, bf16[256,1024]{1,0:T(8,128)(2,1)S(1)} %collective-permute-done.11.rest_2_, ...), custom_call_target="tpu_custom_call" | custom-call | flops 2000000 | bytes 6000000 | tf_op jit(solution)/shard_map/early/pallas_call | solution.py:544
  94.2 0.0 collective-permute-done.3.rest_0_
  94.2 2.5 %collective-permute-done.4.rest_1_ = bf16[256,1024]{1,0:T(8,128)(2,1)S(1)} collective-permute-done((bf16[256,1024]{1,0:T(8,128)(2,1)S(1)}, bf16[256,1024]{1,0:T(8,128)(2,1)S(1)}, u32[]{:S(2)}, u32[]{:S(2)}) %collective-permute-start.4) | collective-permute-done | bytes 524320 | tf_op jit(solution)/shard_map/ppermute | solution.py:28
  96.7 0.0 collective-permute-done.5.rest_2_
  96.7 2.5 %late.1 = (bf16[64,64,256]{2,1,0:T(8,128)(2,1)}, f32[2,4160,128]{2,1,0:T(8,128)S(1)}) custom-call(s32[1,2,16]{2,1,0:T(2,128)S(1)} %bitcast.3, bf16[256,1024]{1,0:T(8,128)(2,1)S(1)} %collective-permute-done.3.rest_0_, bf16[256,1024]{1,0:T(8,128)(2,1)S(1)} %collective-permute-done.4.rest_1_, ...), custom_call_target="tpu_custom_call", output_to_operand_aliasing={{1}: (4, {})} | custom-call | flops 2000000 | bytes 6000000 | tf_op jit(solution)/shard_map/late/pallas_call | solution.py:557
  (1 shorter events, 0.0 us)
Async XLA Ops:
  0.0 13.2 %copy-start.1 = (bf16[64,64,128]{2,1,0:T(8,128)(2,1)S(1)}, bf16[64,64,128]{2,1,0:T(8,128)(2,1)}, u32[]{:S(2)}) copy-start(bf16[64,64,128]{2,1,0:T(8,128)(2,1)} %wind_ref.1) | copy-start | bytes 3145732
  0.0 13.2 %copy-start = (bf16[64,64,256]{2,1,0:T(8,128)(2,1)S(1)}, bf16[64,64,256]{2,1,0:T(8,128)(2,1)}, u32[]{:S(2)}) copy-start(bf16[64,64,256]{2,1,0:T(8,128)(2,1)} %tracers_ref.3) | copy-start | bytes 6291460
  2.6 16.2 %collective-permute-start.6 = (bf16[528,128]{1,0:T(8,128)(2,1)S(1)}, bf16[528,128]{1,0:T(8,128)(2,1)S(1)}, u32[]{:S(2)}, u32[]{:S(2)}) collective-permute-start(bf16[528,128]{1,0:T(8,128)(2,1)S(1)} %get-tuple-element.21), channel_id=1, source_target_pairs={{2,0},{3,1},{4,2},{5,3},{6,4},{7,5},{8,6},{9,7},{10,8},{11,9},{12,... | collective-permute-start | bytes 405512 | tf_op jit(solution)/shard_map/ppermute | solution.py:28
  7.7 19.4 %collective-permute-start.8 = (bf16[528,128]{1,0:T(8,128)(2,1)S(1)}, bf16[528,128]{1,0:T(8,128)(2,1)S(1)}, u32[]{:S(2)}, u32[]{:S(2)}) collective-permute-start(bf16[528,128]{1,0:T(8,128)(2,1)S(1)} %get-tuple-element.22), channel_id=1, source_target_pairs={{12,0},{13,1},{14,2},{15,3},{0,4},{1,5},{2,6},{3,7},{4,8},{5,9},{6... | collective-permute-start | bytes 405512 | tf_op jit(solution)/shard_map/ppermute | solution.py:28
  7.7 3.8 %collective-permute-start.1 = (bf16[912,128]{1,0:T(8,128)(2,1)S(1)}, bf16[912,128]{1,0:T(8,128)(2,1)S(1)}, u32[]{:S(2)}, u32[]{:S(2)}) collective-permute-start(bf16[912,128]{1,0:T(8,128)(2,1)S(1)} %get-tuple-element.17), channel_id=1, source_target_pairs={{15,0},{0,1},{1,2},{2,3},{3,4},{4,5},{5,6},{6,7},{7,8},{8,9},{9,10... | collective-permute-start | bytes 700424 | tf_op jit(solution)/shard_map/ppermute | solution.py:28
  7.7 5.5 %collective-permute-start.2 = (bf16[912,128]{1,0:T(8,128)(2,1)S(1)}, bf16[912,128]{1,0:T(8,128)(2,1)S(1)}, u32[]{:S(2)}, u32[]{:S(2)}) collective-permute-start(bf16[912,128]{1,0:T(8,128)(2,1)S(1)} %get-tuple-element.18), channel_id=1, source_target_pairs={{1,0},{2,1},{3,2},{4,3},{5,4},{6,5},{7,6},{8,7},{9,8},{10,9},{11,1... | collective-permute-start | bytes 700424 | tf_op jit(solution)/shard_map/ppermute | solution.py:28
  21.0 49.0 %collective-permute-start.7 = (bf16[256,1024]{1,0:T(8,128)(2,1)S(1)}, bf16[256,1024]{1,0:T(8,128)(2,1)S(1)}, u32[]{:S(2)}, u32[]{:S(2)}) collective-permute-start(bf16[256,1024]{1,0:T(8,128)(2,1)S(1)} %advect.11), channel_id=1, source_target_pairs={{14,0},{15,1},{0,2},{1,3},{2,4},{3,5},{4,6},{5,7},{6,8},{7,9},{8,1... | collective-permute-start | bytes 1572872 | tf_op jit(solution)/shard_map/ppermute | solution.py:28
  30.2 40.6 %collective-permute-start.9 = (bf16[256,1024]{1,0:T(8,128)(2,1)S(1)}, bf16[256,1024]{1,0:T(8,128)(2,1)S(1)}, u32[]{:S(2)}, u32[]{:S(2)}) collective-permute-start(bf16[256,1024]{1,0:T(8,128)(2,1)S(1)} %advect.12), channel_id=1, source_target_pairs={{4,0},{5,1},{6,2},{7,3},{8,4},{9,5},{10,6},{11,7},{12,8},{13,9},{1... | collective-permute-start | bytes 1572872 | tf_op jit(solution)/shard_map/ppermute | solution.py:28
  31.0 24.0 %collective-permute-start = (bf16[528,128]{1,0:T(8,128)(2,1)S(1)}, bf16[528,128]{1,0:T(8,128)(2,1)S(1)}, u32[]{:S(2)}, u32[]{:S(2)}) collective-permute-start(bf16[528,128]{1,0:T(8,128)(2,1)S(1)} %get-tuple-element.16), channel_id=1, source_target_pairs={{13,0},{14,1},{15,2},{0,3},{1,4},{2,5},{3,6},{4,7},{5,8},{6,9},{7,... | collective-permute-start | bytes 405512 | tf_op jit(solution)/shard_map/ppermute | solution.py:28
  31.0 28.8 %collective-permute-start.10 = (bf16[528,128]{1,0:T(8,128)(2,1)S(1)}, bf16[528,128]{1,0:T(8,128)(2,1)S(1)}, u32[]{:S(2)}, u32[]{:S(2)}) collective-permute-start(bf16[528,128]{1,0:T(8,128)(2,1)S(1)} %get-tuple-element.23), channel_id=1, source_target_pairs={{14,0},{15,1},{0,2},{1,3},{2,4},{3,5},{4,6},{5,7},{6,8},{7,9},{8,1... | collective-permute-start | bytes 405512 | tf_op jit(solution)/shard_map/ppermute | solution.py:28
  31.0 30.4 %collective-permute-start.12 = (bf16[528,128]{1,0:T(8,128)(2,1)S(1)}, bf16[528,128]{1,0:T(8,128)(2,1)S(1)}, u32[]{:S(2)}, u32[]{:S(2)}) collective-permute-start(bf16[528,128]{1,0:T(8,128)(2,1)S(1)} %get-tuple-element.24), channel_id=1, source_target_pairs={{3,0},{4,1},{5,2},{6,3},{7,4},{8,5},{9,6},{10,7},{11,8},{12,9},{13... | collective-permute-start | bytes 405512 | tf_op jit(solution)/shard_map/ppermute | solution.py:28
  58.7 35.5 %collective-permute-start.3 = (bf16[256,1024]{1,0:T(8,128)(2,1)S(1)}, bf16[256,1024]{1,0:T(8,128)(2,1)S(1)}, u32[]{:S(2)}, u32[]{:S(2)}) collective-permute-start(bf16[256,1024]{1,0:T(8,128)(2,1)S(1)} %advect.8), channel_id=1, source_target_pairs={{3,0},{4,1},{5,2},{6,3},{7,4},{8,5},{9,6},{10,7},{11,8},{12,9},{13... | collective-permute-start | bytes 1572872 | tf_op jit(solution)/shard_map/ppermute | solution.py:28
  61.4 25.2 %collective-permute-start.11 = (bf16[256,1024]{1,0:T(8,128)(2,1)S(1)}, bf16[256,1024]{1,0:T(8,128)(2,1)S(1)}, u32[]{:S(2)}, u32[]{:S(2)}) collective-permute-start(bf16[256,1024]{1,0:T(8,128)(2,1)S(1)} %advect.13), channel_id=1, source_target_pairs={{2,0},{3,1},{4,2},{5,3},{6,4},{7,5},{8,6},{9,7},{10,8},{11,9},{12,... | collective-permute-start | bytes 1572872 | tf_op jit(solution)/shard_map/ppermute | solution.py:28
  64.5 28.5 %collective-permute-start.13 = (bf16[256,1024]{1,0:T(8,128)(2,1)S(1)}, bf16[256,1024]{1,0:T(8,128)(2,1)S(1)}, u32[]{:S(2)}, u32[]{:S(2)}) collective-permute-start(bf16[256,1024]{1,0:T(8,128)(2,1)S(1)} %advect.14), channel_id=1, source_target_pairs={{13,0},{14,1},{15,2},{0,3},{1,4},{2,5},{3,6},{4,7},{5,8},{6,9},{7,... | collective-permute-start | bytes 1572872 | tf_op jit(solution)/shard_map/ppermute | solution.py:28
  70.0 26.7 %collective-permute-start.4 = (bf16[256,1024]{1,0:T(8,128)(2,1)S(1)}, bf16[256,1024]{1,0:T(8,128)(2,1)S(1)}, u32[]{:S(2)}, u32[]{:S(2)}) collective-permute-start(bf16[256,1024]{1,0:T(8,128)(2,1)S(1)} %advect.9), channel_id=1, source_target_pairs={{15,0},{0,1},{1,2},{2,3},{3,4},{4,5},{5,6},{6,7},{7,8},{8,9},{9,10... | collective-permute-start | bytes 1572872 | tf_op jit(solution)/shard_map/ppermute | solution.py:28
  70.7 26.0 %collective-permute-start.5 = (bf16[256,1024]{1,0:T(8,128)(2,1)S(1)}, bf16[256,1024]{1,0:T(8,128)(2,1)S(1)}, u32[]{:S(2)}, u32[]{:S(2)}) collective-permute-start(bf16[256,1024]{1,0:T(8,128)(2,1)S(1)} %advect.10), channel_id=1, source_target_pairs={{1,0},{2,1},{3,2},{4,3},{5,4},{6,5},{7,6},{8,7},{9,8},{10,9},{11,1... | collective-permute-start | bytes 1572872 | tf_op jit(solution)/shard_map/ppermute | solution.py:28
  70.7 22.3 %copy-start.2 = (s32[1,16,2]{1,2,0:T(2,128)S(1)}, s32[1,16,2]{1,2,0:T(2,128)}, u32[]{:S(2)}) copy-start(s32[1,16,2]{1,2,0:T(2,128)} %param.5) | copy-start | bytes 388

commit v3 on v2

--- a/solution.py
+++ b/solution.py
@@ -13,7 +13,7 @@
 FIRST = -4
 LAST = 4
 LATE = 3
-ORDER = (2, -4, -2, 3, -3, 1, -1, 0)
+ORDER = (-2, -4, 2, 3, -3, 1, -1, 0)
 RIM = 2
 LANES = 128
 META = 16
@@ -55,10 +55,38 @@
     return jnp.where(place == column, 1.0, 0.0).astype(BF16)
 
 
+def tracer_perms(spread_ref, join_ref, groups, levels):
+    per_level = join_ref.shape[0] // LANES
+    tracer_ch = levels * per_level
+    bits = per_level.bit_length() - 1
+
+    def ones(place, offset):
+        lane = lax.broadcasted_iota(jnp.int32, place.shape, 1)
+        return jnp.where(place == lane - offset, 1.0, 0.0).astype(BF16)
+
+    row = lax.broadcasted_iota(jnp.int32, (LANES, LANES), 0)
+    group = lax.shift_right_logical(row, levels.bit_length() - 1)
+    place = group * tracer_ch + (row & (levels - 1)) * per_level
+    for tracer in range(per_level):
+        for tile in range(per_level):
+            join_ref[
+                tracer * LANES : (tracer + 1) * LANES, tile * LANES : (tile + 1) * LANES
+            ] = ones(place, tracer - tile * LANES)
+    row = lax.broadcasted_iota(jnp.int32, (tracer_ch, LANES), 0)
+    place = (row & (per_level - 1)) * LANES + lax.shift_right_logical(row, bits)
+    for group in range(groups):
+        for tile in range(per_level):
+            spread_ref[
+                group * tracer_ch : (group + 1) * tracer_ch, tile * LANES : (tile + 1) * LANES
+            ] = ones(place, group * levels - tile * LANES)
+
+
 def wind_kernel(sizes, dep_hbm_ref, wind_hbm_ref, tracers_ref, *rest):
     columns, rows, inner, bands, band_rows = sizes
     outs = rest[: LAST - FIRST]
     (
+        spread_ref,
+        join_ref,
         dep_ref,
         wind_ref,
         wide_ref,
@@ -91,6 +119,7 @@
     for copy in [table] + chunks + edges:
         copy.start()
     perm_ref[...] = wind_perm(perm_ref.shape[0], LANES // groups, 2)
+    tracer_perms(spread_ref, join_ref, groups, LANES // groups)
     table.wait()
     fill_slots(dep_ref, slot_ref, count_ref, bands)
 
@@ -172,7 +201,7 @@
     wind_perm_ref,
 ):
     columns, rows, inner, padded_inner, rim_at = sizes
-    batch = 16
+    batch = 32
     groups = columns // inner
     tracer_ch = tracers_ref.shape[-1]
     halves = tracer_ch // LANES
@@ -249,14 +278,11 @@
     across = e * one_less * (-1.0 / 6.0)
     beyond = across * two_less
     far = across * one_more
-    zero = jnp.zeros_like(e)
     return (
-        jnp.where(positive, far, zero),
-        jnp.where(positive, near, beyond),
-        center,
-        jnp.where(positive, beyond, near),
-        jnp.where(positive, zero, far),
-    ), positive
+        far,
+        (jnp.where(positive, near, beyond), center, jnp.where(positive, beyond, near)),
+        positive,
+    )
 
 
 def linear_weights(shift):
@@ -318,32 +344,32 @@
                                 total = line if total is None else total + line
                             moved.append(clipped(0.5 * (wind[comp] + total)))
                         shift = moved
-                    lon_cubic, _ = cubic_weights(shift[0])
-                    lat_cubic, north = cubic_weights(shift[1])
+                    far, lon_cubic, east = cubic_weights(shift[0])
+                    far_lat, lat_cubic, north = cubic_weights(shift[1])
                     low, mid, high = linear_weights(shift[0])
+                    side = low + high
                     zero = jnp.zeros_like(low)
-                    lon_linear = (zero, low, mid, high, zero)
-                    taps = []
-                    for b in range(-2, 3):
-                        for a in range(-2, 3):
-                            if abs(b) == 2:
-                                if abs(a) == 2:
-                                    continue
-                                weight = lon_linear[a + 2]
-                            elif b == 0:
-                                weight = lon_cubic[a + 2]
-                            elif b == -1:
-                                weight = jnp.where(north, lon_cubic[a + 2], lon_linear[a + 2])
-                            else:
-                                weight = jnp.where(north, lon_linear[a + 2], lon_cubic[a + 2])
-                            taps.append((a, b, weight * lat_cubic[b + 2]))
+                    rows_of = []
+                    for b, inside in ((-1, north), (0, None), (1, jnp.logical_not(north))):
+                        weights = []
+                        for cubic, linear in zip((far,) + lon_cubic, (zero, low, mid, high)):
+                            if inside is not None:
+                                cubic = jnp.where(inside, cubic, linear)
+                            weights.append(cubic * lat_cubic[b + 1])
+                        rows_of.append((b, weights))
+                    mid = mid * far_lat
+                    side = side * far_lat
                     for tracer in range(per_level):
-                        total = None
-                        for a, b, weight in taps:
-                            term = weight * t_ref[
-                                tracer, first + row + b, pl.ds(base + RIM + a, 8), :
-                            ]
-                            total = term if total is None else total + term
+
+                        def at(a, b):
+                            return t_ref[tracer, first + row + b, pl.ds(base + RIM + a, 8), :]
+
+                        edge = [jnp.where(north, at(a, -2), at(a, 2)) for a in (-1, 0, 1)]
+                        total = mid * edge[1] + side * jnp.where(east, edge[0], edge[2])
+                        for b, weights in rows_of:
+                            total = total + weights[0] * jnp.where(east, at(-2, b), at(2, b))
+                            for a in (-1, 0, 1):
+                                total = total + weights[a + 2] * at(a, b)
                         result_ref[
                             pl.ds(slot * size + row * inner + base, 8),
                             tracer * LANES : (tracer + 1) * LANES,
@@ -441,11 +467,6 @@
     rim_rows = RIM * (halves + 1) * rows
 
     wide = per_level * LANES
-    index = jnp.arange(wide, dtype=jnp.int32)
-    place = (index // levels) % (LANES // levels) * tracer_ch + index % levels * per_level
-    place = place + index // LANES
-    spread = (place[None, :] == index[:, None]).astype(BF16)
-    join = (place[:, None] == index[None, :]).astype(BF16)
     table = jnp.transpose(departures, (0, 2, 1))
 
     vmem = pl.BlockSpec(memory_space=pltpu.VMEM)
@@ -456,14 +477,15 @@
     def params(mib):
         return pltpu.CompilerParams(vmem_limit_bytes=mib << 20)
 
-    messages = pl.pallas_call(
+    *messages, spread, join = pl.pallas_call(
         functools.partial(wind_kernel, (columns, rows, inner, bands, band_rows)),
         out_shape=[
             jax.ShapeDtypeStruct((rim_at + (rim_rows if abs(n) == 1 else 0), LANES), BF16)
             for n in range(FIRST, LAST)
-        ],
+        ]
+        + [jax.ShapeDtypeStruct((wide, wide), BF16)] * 2,
         in_specs=[hbm] * 3,
-        out_specs=[vmem] * offsets,
+        out_specs=[vmem] * (offsets + 2),
         scratch_shapes=[
             pltpu.SMEM(table.shape, jnp.int32),
             pltpu.VMEM(wind_fields.shape, BF16),
@@ -489,8 +511,8 @@
     prepare = pl.pallas_call(
         functools.partial(prepare_kernel, (columns, rows, inner, padded_inner, rim_at)),
         out_shape=[
-            jax.ShapeDtypeStruct((per_level, rows + 2 * RIM, padded_inner, LANES), F32),
-            jax.ShapeDtypeStruct((2, rows + 2 * RIM, padded_inner, LANES), F32),
+            jax.ShapeDtypeStruct((per_level, rows + 2 * RIM + 1, padded_inner, LANES), F32),
+            jax.ShapeDtypeStruct((2, rows + 2 * RIM + 1, padded_inner, LANES), F32),
         ],
         in_specs=[vmem] * 5,
         out_specs=[vmem] * 2,

time: 99.3 us -> 94.3 us (0.950)
  the two profiles are of different devices: /device:TPU:1 before, /device:TPU:0 now
where the time goes in v3:
time: 94.3 us; the launch traced here: 92.5 us
  waiting for transfers between devices  40.9 us (43%)
  Pallas kernels  26 us (28%)
  starting transfers between devices  25.4 us (27%)
    ppermute x14, waiting for transfers between devices, shifted(): return lax.ppermute(block, axis, route)  40.9 us
    ppermute x14, starting transfers between devices, shifted(): return lax.ppermute(block, axis, route)  25.4 us
    pallas_call x8, Pallas kernels, on_device(): result = advect(arrived[n], fields, extra, join)  14.4 us
    pallas_call x1, Pallas kernels, on_device(): prepare(tracers, wind_fields, arrived[-1], arrived[1], spread)  5.08 us
    pallas_call x1, Pallas kernels, on_device(): pl.pallas_call(functools.partial(wind_kernel, (columns, rows, inner, band...  2.74 us
    pallas_call x1, Pallas kernels, on_device(): return last(table, *[received[n - FIRST] for n in late], spread_out)[0]  2.47 us
  transfers between devices with their start and end apart: 14, of which 5 were waited for; matrix products, arithmetic and copies ran while one was open for 0% of the time, Pallas kernels for 22%

profile of v3, /device:TPU:0, one launch (start us, length us, event | category | flops | bytes accessed | tf_op | source)
XLA Modules:
  0.0 92.5 jit_solution(5407209243267300092)
XLA Ops:
  0.0 0.0 copy-start.1
  0.0 0.0 copy-start
  0.0 2.7 %winds.1 = (bf16[528,128]{1,0:T(8,128)(2,1)S(1)}, bf16[528,128]{1,0:T(8,128)(2,1)S(1)}, bf16[528,128]{1,0:T(8,128)(2,1)S(1)}, bf16[912,128]{1,0:T(8,128)(2,1)S(1...) custom-call(s32[1,2,16]{2,1,0:T(2,128)} %bitcast.1, ...), custom_call_target="tpu_custom_call" | custom-call | flops 4000000 | bytes 3000000 | tf_op jit(solution)/shard_map/winds/pallas_call | solution.py:480
  2.8 0.5 collective-permute-start.1
  3.3 5.0 %collective-permute-start.2 = (bf16[912,128]{1,0:T(8,128)(2,1)S(1)}, bf16[912,128]{1,0:T(8,128)(2,1)S(1)}, u32[]{:S(2)}, u32[]{:S(2)}) collective-permute-start(bf16[912,128]{1,0:T(8,128)(2,1)S(1)} %get-tuple-element.20), channel_id=1, source_target_pairs={{1,0},{2,1},{3,2},{4,3},{5,4},{6,5},{7,6},{8,7},{9,8},{10,9},{11,1... | collective-permute-start | bytes 700424 | tf_op jit(solution)/shard_map/ppermute | solution.py:28
  8.3 0.0 collective-permute-start.6
  8.3 0.8 collective-permute-start.8
  9.1 3.0 %collective-permute-done.1.low_ref.msg_ref = bf16[912,128]{1,0:T(8,128)(2,1)S(1)} collective-permute-done((bf16[912,128]{1,0:T(8,128)(2,1)S(1)}, bf16[912,128]{1,0:T(8,128)(2,1)S(1)}, u32[]{:S(2)}, u32[]{:S(2)}) %collective-permute-start.1) | collective-permute-done | bytes 233504 | tf_op jit(solution)/shard_map/ppermute | solution.py:28
  12.1 0.7 collective-permute-done.2.high_ref.msg_ref
  12.9 0.0 copy-done.1
  12.9 0.0 copy-done
  12.9 5.1 %prepare.1 = (f32[8,69,24,128]{3,2,1,0:T(8,128)S(1)}, f32[2,69,24,128]{3,2,1,0:T(8,128)S(1)}) custom-call(bf16[64,64,256]{2,1,0:T(8,128)(2,1)S(1)} %copy-done, bf16[64,64,128]{2,1,0:T(8,128)(2,1)S(1)} %copy-done.1, bf16[912,128]{1,0:T(8,128)(2,1)S(1)} %collective-permute-done.1.low_ref.msg_ref, bf16[912,128]{1,0:T(8,128)(2,1)S(1)} %collective-permute-done.2.high_ref.msg_ref, ...), custom_call_target="tpu_custom_call" | custom-call | flops 16000000 | bytes 12000000 | tf_op jit(solution)/shard_map/prepare/pallas_call | solution.py:530
  17.9 0.0 collective-permute-done.6.msg_ref
  18.0 2.1 %advect.11 = bf16[256,1024]{1,0:T(8,128)(2,1)S(1)} custom-call(bf16[528,128]{1,0:T(8,128)(2,1)S(1)} %collective-permute-done.6.msg_ref, f32[8,69,24,128]{3,2,1,0:T(8,128)S(1)} %get-tuple-element.22.t_ref, f32[2,69,24,128]{3,2,1,0:T(8,128)S(1)} %get-tuple-element.23.e_ref, bf16[1024,1024]{1,0:T(8,128)(2,1)S(1)} %get-tuple-element.24.perm_ref), custom_call_target="tpu_custom_call" | custom-call | flops 16000000 | bytes 6000000 | tf_op jit(solution)/shard_map/advect/pallas_call | solution.py:549
  20.1 5.2 %collective-permute-start.7 = (bf16[256,1024]{1,0:T(8,128)(2,1)S(1)}, bf16[256,1024]{1,0:T(8,128)(2,1)S(1)}, u32[]{:S(2)}, u32[]{:S(2)}) collective-permute-start(bf16[256,1024]{1,0:T(8,128)(2,1)S(1)} %advect.11), channel_id=1, source_target_pairs={{2,0},{3,1},{4,2},{5,3},{6,4},{7,5},{8,6},{9,7},{10,8},{11,9},{12,... | collective-permute-start | bytes 1572872 | tf_op jit(solution)/shard_map/ppermute | solution.py:28
  25.3 0.0 collective-permute-done.8.msg_ref
  25.3 1.5 %advect.12 = bf16[256,1024]{1,0:T(8,128)(2,1)S(1)} custom-call(bf16[528,128]{1,0:T(8,128)(2,1)S(1)} %collective-permute-done.8.msg_ref, f32[8,69,24,128]{3,2,1,0:T(8,128)S(1)} %get-tuple-element.22.t_ref, f32[2,69,24,128]{3,2,1,0:T(8,128)S(1)} %get-tuple-element.23.e_ref, bf16[1024,1024]{1,0:T(8,128)(2,1)S(1)} %get-tuple-element.24.perm_ref), custom_call_target="tpu_custom_call" | custom-call | flops 16000000 | bytes 6000000 | tf_op jit(solution)/shard_map/advect/pallas_call | solution.py:549
  26.8 1.7 %collective-permute-start.9 = (bf16[256,1024]{1,0:T(8,128)(2,1)S(1)}, bf16[256,1024]{1,0:T(8,128)(2,1)S(1)}, u32[]{:S(2)}, u32[]{:S(2)}) collective-permute-start(bf16[256,1024]{1,0:T(8,128)(2,1)S(1)} %advect.12), channel_id=1, source_target_pairs={{4,0},{5,1},{6,2},{7,3},{8,4},{9,5},{10,6},{11,7},{12,8},{13,9},{1... | collective-permute-start | bytes 1572872 | tf_op jit(solution)/shard_map/ppermute | solution.py:28
  28.6 0.8 collective-permute-start
  29.4 3.0 %collective-permute-start.10 = (bf16[528,128]{1,0:T(8,128)(2,1)S(1)}, bf16[528,128]{1,0:T(8,128)(2,1)S(1)}, u32[]{:S(2)}, u32[]{:S(2)}) collective-permute-start(bf16[528,128]{1,0:T(8,128)(2,1)S(1)} %get-tuple-element.27), channel_id=1, source_target_pairs={{2,0},{3,1},{4,2},{5,3},{6,4},{7,5},{8,6},{9,7},{10,8},{11,9},{12,... | collective-permute-start | bytes 405512 | tf_op jit(solution)/shard_map/ppermute | solution.py:28
  32.4 0.0 collective-permute-start.12
  32.4 19.1 %collective-permute-done.msg_ref = bf16[528,128]{1,0:T(8,128)(2,1)S(1)} collective-permute-done((bf16[528,128]{1,0:T(8,128)(2,1)S(1)}, bf16[528,128]{1,0:T(8,128)(2,1)S(1)}, u32[]{:S(2)}, u32[]{:S(2)}) %collective-permute-start) | collective-permute-done | bytes 135200 | tf_op jit(solution)/shard_map/ppermute | solution.py:28
  51.5 2.7 %advect.8 = bf16[256,1024]{1,0:T(8,128)(2,1)S(1)} custom-call(bf16[528,128]{1,0:T(8,128)(2,1)S(1)} %collective-permute-done.msg_ref, f32[8,69,24,128]{3,2,1,0:T(8,128)S(1)} %get-tuple-element.22.t_ref, f32[2,69,24,128]{3,2,1,0:T(8,128)S(1)} %get-tuple-element.23.e_ref, bf16[1024,1024]{1,0:T(8,128)(2,1)S(1)} %get-tuple-element.24.perm_ref), custom_call_target="tpu_custom_call" | custom-call | flops 16000000 | bytes 6000000 | tf_op jit(solution)/shard_map/advect/pallas_call | solution.py:549
  54.2 0.1 collective-permute-start.3
  54.3 0.0 collective-permute-done.10.msg_ref
  54.3 0.9 advect.13
  55.2 2.1 %collective-permute-start.11 = (bf16[256,1024]{1,0:T(8,128)(2,1)S(1)}, bf16[256,1024]{1,0:T(8,128)(2,1)S(1)}, u32[]{:S(2)}, u32[]{:S(2)}) collective-permute-start(bf16[256,1024]{1,0:T(8,128)(2,1)S(1)} %advect.13), channel_id=1, source_target_pairs={{14,0},{15,1},{0,2},{1,3},{2,4},{3,5},{4,6},{5,7},{6,8},{7,9},{8,1... | collective-permute-start | bytes 1572872 | tf_op jit(solution)/shard_map/ppermute | solution.py:28
  57.3 0.0 collective-permute-done.12.msg_ref
  57.3 1.5 %advect.14 = bf16[256,1024]{1,0:T(8,128)(2,1)S(1)} custom-call(bf16[528,128]{1,0:T(8,128)(2,1)S(1)} %collective-permute-done.12.msg_ref, f32[8,69,24,128]{3,2,1,0:T(8,128)S(1)} %get-tuple-element.22.t_ref, f32[2,69,24,128]{3,2,1,0:T(8,128)S(1)} %get-tuple-element.23.e_ref, bf16[1024,1024]{1,0:T(8,128)(2,1)S(1)} %get-tuple-element.24.perm_ref), custom_call_target="tpu_custom_call" | custom-call | flops 16000000 | bytes 6000000 | tf_op jit(solution)/shard_map/advect/pallas_call | solution.py:549
  58.8 1.6 %collective-permute-start.13 = (bf16[256,1024]{1,0:T(8,128)(2,1)S(1)}, bf16[256,1024]{1,0:T(8,128)(2,1)S(1)}, u32[]{:S(2)}, u32[]{:S(2)}) collective-permute-start(bf16[256,1024]{1,0:T(8,128)(2,1)S(1)} %advect.14), channel_id=1, source_target_pairs={{13,0},{14,1},{15,2},{0,3},{1,4},{2,5},{3,6},{4,7},{5,8},{6,9},{7,... | collective-permute-start | bytes 1572872 | tf_op jit(solution)/shard_map/ppermute | solution.py:28
  60.4 2.1 %advect.10 = bf16[256,1024]{1,0:T(8,128)(2,1)S(1)} custom-call(bf16[912,128]{1,0:T(8,128)(2,1)S(1)} %collective-permute-done.1.low_ref.msg_ref, f32[8,69,24,128]{3,2,1,0:T(8,128)S(1)} %get-tuple-element.22.t_ref, f32[2,69,24,128]{3,2,1,0:T(8,128)S(1)} %get-tuple-element.23.e_ref, bf16[1024,1024]{1,0:T(8,128)(2,1)S(1)} %get-tuple-element.24.perm_ref), custom_call_target="tpu_custom_call" | custom-call | flops 16000000 | bytes 6000000 | tf_op jit(solution)/shard_map/advect/pallas_call | solution.py:549
  62.5 1.5 %advect.9 = bf16[256,1024]{1,0:T(8,128)(2,1)S(1)} custom-call(bf16[912,128]{1,0:T(8,128)(2,1)S(1)} %collective-permute-done.2.high_ref.msg_ref, f32[8,69,24,128]{3,2,1,0:T(8,128)S(1)} %get-tuple-element.22.t_ref, f32[2,69,24,128]{3,2,1,0:T(8,128)S(1)} %get-tuple-element.23.e_ref, bf16[1024,1024]{1,0:T(8,128)(2,1)S(1)} %get-tuple-element.24.perm_ref), custom_call_target="tpu_custom_call" | custom-call | flops 16000000 | bytes 6000000 | tf_op jit(solution)/shard_map/advect/pallas_call | solution.py:549
  64.0 0.0 collective-permute-done.7.rest_0_
  64.1 2.0 %collective-permute-start.4 = (bf16[256,1024]{1,0:T(8,128)(2,1)S(1)}, bf16[256,1024]{1,0:T(8,128)(2,1)S(1)}, u32[]{:S(2)}, u32[]{:S(2)}) collective-permute-start(bf16[256,1024]{1,0:T(8,128)(2,1)S(1)} %advect.9), channel_id=1, source_target_pairs={{15,0},{0,1},{1,2},{2,3},{3,4},{4,5},{5,6},{6,7},{7,8},{8,9},{9,10... | collective-permute-start | bytes 1572872 | tf_op jit(solution)/shard_map/ppermute | solution.py:28
  66.0 0.0 collective-permute-done.9.rest_1_
  66.0 2.5 %collective-permute-start.5 = (bf16[256,1024]{1,0:T(8,128)(2,1)S(1)}, bf16[256,1024]{1,0:T(8,128)(2,1)S(1)}, u32[]{:S(2)}, u32[]{:S(2)}) collective-permute-start(bf16[256,1024]{1,0:T(8,128)(2,1)S(1)} %advect.10), channel_id=1, source_target_pairs={{1,0},{2,1},{3,2},{4,3},{5,4},{6,5},{7,6},{8,7},{9,8},{10,9},{11,1... | collective-permute-start | bytes 1572872 | tf_op jit(solution)/shard_map/ppermute | solution.py:28
  68.6 0.0 copy-start.2
  68.6 2.1 %advect.15.rest_4_ = bf16[256,1024]{1,0:T(8,128)(2,1)S(1)} custom-call(bf16[528,128]{1,0:T(8,128)(2,1)S(1)} %get-tuple-element.29.msg_ref, f32[8,69,24,128]{3,2,1,0:T(8,128)S(1)} %get-tuple-element.22.t_ref, f32[2,69,24,128]{3,2,1,0:T(8,128)S(1)} %get-tuple-element.23.e_ref, bf16[1024,1024]{1,0:T(8,128)(2,1)S(1)} %get-tuple-element.24.perm_ref), custom_call_target="tpu_custom_call" | custom-call | flops 16000000 | bytes 6000000 | tf_op jit(solution)/shard_map/advect/pallas_call | solution.py:549
  70.7 3.3 %collective-permute-done.11.rest_2_ = bf16[256,1024]{1,0:T(8,128)(2,1)S(1)} collective-permute-done((bf16[256,1024]{1,0:T(8,128)(2,1)S(1)}, bf16[256,1024]{1,0:T(8,128)(2,1)S(1)}, u32[]{:S(2)}, u32[]{:S(2)}) %collective-permute-start.11) | collective-permute-done | bytes 524320 | tf_op jit(solution)/shard_map/ppermute | solution.py:28
  74.0 14.8 %collective-permute-done.13.rest_3_ = bf16[256,1024]{1,0:T(8,128)(2,1)S(1)} collective-permute-done((bf16[256,1024]{1,0:T(8,128)(2,1)S(1)}, bf16[256,1024]{1,0:T(8,128)(2,1)S(1)}, u32[]{:S(2)}, u32[]{:S(2)}) %collective-permute-start.13) | collective-permute-done | bytes 524320 | tf_op jit(solution)/shard_map/ppermute | solution.py:28
  88.8 0.0 copy-done.2
  88.8 1.2 %early.1.rest_3_ = f32[2,4160,128]{2,1,0:T(8,128)S(1)} custom-call(s32[1,2,16]{2,1,0:T(2,128)S(1)} %bitcast.2, bf16[256,1024]{1,0:T(8,128)(2,1)S(1)} %collective-permute-done.7.rest_0_, bf16[256,1024]{1,0:T(8,128)(2,1)S(1)} %collective-permute-done.9.rest_1_, bf16[256,1024]{1,0:T(8,128)(2,1)S(1)} %collective-permute-done.11.rest_2_, ...), custom_call_target="tpu_custom_call" | custom-call | flops 2000000 | bytes 6000000 | tf_op jit(solution)/shard_map/early/pallas_call | solution.py:566
  90.0 0.0 collective-permute-done.3.rest_0_
  90.0 0.0 collective-permute-done.4.rest_1_
  90.0 0.0 collective-permute-done.5.rest_2_
  90.0 2.5 %late.1 = (bf16[64,64,256]{2,1,0:T(8,128)(2,1)}, f32[2,4160,128]{2,1,0:T(8,128)S(1)}) custom-call(s32[1,2,16]{2,1,0:T(2,128)S(1)} %bitcast.3, bf16[256,1024]{1,0:T(8,128)(2,1)S(1)} %collective-permute-done.3.rest_0_, bf16[256,1024]{1,0:T(8,128)(2,1)S(1)} %collective-permute-done.4.rest_1_, ...), custom_call_target="tpu_custom_call", output_to_operand_aliasing={{1}: (4, {})} | custom-call | flops 2000000 | bytes 6000000 | tf_op jit(solution)/shard_map/late/pallas_call | solution.py:579
Async XLA Ops:
  0.0 12.9 %copy-start.1 = (bf16[64,64,128]{2,1,0:T(8,128)(2,1)S(1)}, bf16[64,64,128]{2,1,0:T(8,128)(2,1)}, u32[]{:S(2)}) copy-start(bf16[64,64,128]{2,1,0:T(8,128)(2,1)} %wind_ref.1) | copy-start | bytes 3145732
  0.0 12.9 %copy-start = (bf16[64,64,256]{2,1,0:T(8,128)(2,1)S(1)}, bf16[64,64,256]{2,1,0:T(8,128)(2,1)}, u32[]{:S(2)}) copy-start(bf16[64,64,256]{2,1,0:T(8,128)(2,1)} %tracers_ref.3) | copy-start | bytes 6291460
  2.8 9.4 %collective-permute-start.1 = (bf16[912,128]{1,0:T(8,128)(2,1)S(1)}, bf16[912,128]{1,0:T(8,128)(2,1)S(1)}, u32[]{:S(2)}, u32[]{:S(2)}) collective-permute-start(bf16[912,128]{1,0:T(8,128)(2,1)S(1)} %get-tuple-element.19), channel_id=1, source_target_pairs={{15,0},{0,1},{1,2},{2,3},{3,4},{4,5},{5,6},{6,7},{7,8},{8,9},{9,10... | collective-permute-start | bytes 700424 | tf_op jit(solution)/shard_map/ppermute | solution.py:28
  3.3 9.5 %collective-permute-start.2 = (bf16[912,128]{1,0:T(8,128)(2,1)S(1)}, bf16[912,128]{1,0:T(8,128)(2,1)S(1)}, u32[]{:S(2)}, u32[]{:S(2)}) collective-permute-start(bf16[912,128]{1,0:T(8,128)(2,1)S(1)} %get-tuple-element.20), channel_id=1, source_target_pairs={{1,0},{2,1},{3,2},{4,3},{5,4},{6,5},{7,6},{8,7},{9,8},{10,9},{11,1... | collective-permute-start | bytes 700424 | tf_op jit(solution)/shard_map/ppermute | solution.py:28
  8.3 9.6 %collective-permute-start.6 = (bf16[528,128]{1,0:T(8,128)(2,1)S(1)}, bf16[528,128]{1,0:T(8,128)(2,1)S(1)}, u32[]{:S(2)}, u32[]{:S(2)}) collective-permute-start(bf16[528,128]{1,0:T(8,128)(2,1)S(1)} %get-tuple-element.25), channel_id=1, source_target_pairs={{14,0},{15,1},{0,2},{1,3},{2,4},{3,5},{4,6},{5,7},{6,8},{7,9},{8,1... | collective-permute-start | bytes 405512 | tf_op jit(solution)/shard_map/ppermute | solution.py:28
  8.3 17.0 %collective-permute-start.8 = (bf16[528,128]{1,0:T(8,128)(2,1)S(1)}, bf16[528,128]{1,0:T(8,128)(2,1)S(1)}, u32[]{:S(2)}, u32[]{:S(2)}) collective-permute-start(bf16[528,128]{1,0:T(8,128)(2,1)S(1)} %get-tuple-element.26), channel_id=1, source_target_pairs={{12,0},{13,1},{14,2},{15,3},{0,4},{1,5},{2,6},{3,7},{4,8},{5,9},{6... | collective-permute-start | bytes 405512 | tf_op jit(solution)/shard_map/ppermute | solution.py:28
  20.1 44.0 %collective-permute-start.7 = (bf16[256,1024]{1,0:T(8,128)(2,1)S(1)}, bf16[256,1024]{1,0:T(8,128)(2,1)S(1)}, u32[]{:S(2)}, u32[]{:S(2)}) collective-permute-start(bf16[256,1024]{1,0:T(8,128)(2,1)S(1)} %advect.11), channel_id=1, source_target_pairs={{2,0},{3,1},{4,2},{5,3},{6,4},{7,5},{8,6},{9,7},{10,8},{11,9},{12,... | collective-permute-start | bytes 1572872 | tf_op jit(solution)/shard_map/ppermute | solution.py:28
  26.8 39.2 %collective-permute-start.9 = (bf16[256,1024]{1,0:T(8,128)(2,1)S(1)}, bf16[256,1024]{1,0:T(8,128)(2,1)S(1)}, u32[]{:S(2)}, u32[]{:S(2)}) collective-permute-start(bf16[256,1024]{1,0:T(8,128)(2,1)S(1)} %advect.12), channel_id=1, source_target_pairs={{4,0},{5,1},{6,2},{7,3},{8,4},{9,5},{10,6},{11,7},{12,8},{13,9},{1... | collective-permute-start | bytes 1572872 | tf_op jit(solution)/shard_map/ppermute | solution.py:28
  28.6 22.9 %collective-permute-start = (bf16[528,128]{1,0:T(8,128)(2,1)S(1)}, bf16[528,128]{1,0:T(8,128)(2,1)S(1)}, u32[]{:S(2)}, u32[]{:S(2)}) collective-permute-start(bf16[528,128]{1,0:T(8,128)(2,1)S(1)} %get-tuple-element.18), channel_id=1, source_target_pairs={{13,0},{14,1},{15,2},{0,3},{1,4},{2,5},{3,6},{4,7},{5,8},{6,9},{7,... | collective-permute-start | bytes 405512 | tf_op jit(solution)/shard_map/ppermute | solution.py:28
  29.4 24.9 %collective-permute-start.10 = (bf16[528,128]{1,0:T(8,128)(2,1)S(1)}, bf16[528,128]{1,0:T(8,128)(2,1)S(1)}, u32[]{:S(2)}, u32[]{:S(2)}) collective-permute-start(bf16[528,128]{1,0:T(8,128)(2,1)S(1)} %get-tuple-element.27), channel_id=1, source_target_pairs={{2,0},{3,1},{4,2},{5,3},{6,4},{7,5},{8,6},{9,7},{10,8},{11,9},{12,... | collective-permute-start | bytes 405512 | tf_op jit(solution)/shard_map/ppermute | solution.py:28
  32.4 24.9 %collective-permute-start.12 = (bf16[528,128]{1,0:T(8,128)(2,1)S(1)}, bf16[528,128]{1,0:T(8,128)(2,1)S(1)}, u32[]{:S(2)}, u32[]{:S(2)}) collective-permute-start(bf16[528,128]{1,0:T(8,128)(2,1)S(1)} %get-tuple-element.28), channel_id=1, source_target_pairs={{3,0},{4,1},{5,2},{6,3},{7,4},{8,5},{9,6},{10,7},{11,8},{12,9},{13... | collective-permute-start | bytes 405512 | tf_op jit(solution)/shard_map/ppermute | solution.py:28
  54.2 35.8 %collective-permute-start.3 = (bf16[256,1024]{1,0:T(8,128)(2,1)S(1)}, bf16[256,1024]{1,0:T(8,128)(2,1)S(1)}, u32[]{:S(2)}, u32[]{:S(2)}) collective-permute-start(bf16[256,1024]{1,0:T(8,128)(2,1)S(1)} %advect.8), channel_id=1, source_target_pairs={{3,0},{4,1},{5,2},{6,3},{7,4},{8,5},{9,6},{10,7},{11,8},{12,9},{13... | collective-permute-start | bytes 1572872 | tf_op jit(solution)/shard_map/ppermute | solution.py:28
  55.2 18.8 %collective-permute-start.11 = (bf16[256,1024]{1,0:T(8,128)(2,1)S(1)}, bf16[256,1024]{1,0:T(8,128)(2,1)S(1)}, u32[]{:S(2)}, u32[]{:S(2)}) collective-permute-start(bf16[256,1024]{1,0:T(8,128)(2,1)S(1)} %advect.13), channel_id=1, source_target_pairs={{14,0},{15,1},{0,2},{1,3},{2,4},{3,5},{4,6},{5,7},{6,8},{7,9},{8,1... | collective-permute-start | bytes 1572872 | tf_op jit(solution)/shard_map/ppermute | solution.py:28
  58.8 29.9 %collective-permute-start.13 = (bf16[256,1024]{1,0:T(8,128)(2,1)S(1)}, bf16[256,1024]{1,0:T(8,128)(2,1)S(1)}, u32[]{:S(2)}, u32[]{:S(2)}) collective-permute-start(bf16[256,1024]{1,0:T(8,128)(2,1)S(1)} %advect.14), channel_id=1, source_target_pairs={{13,0},{14,1},{15,2},{0,3},{1,4},{2,5},{3,6},{4,7},{5,8},{6,9},{7,... | collective-permute-start | bytes 1572872 | tf_op jit(solution)/shard_map/ppermute | solution.py:28
  64.1 26.0 %collective-permute-start.4 = (bf16[256,1024]{1,0:T(8,128)(2,1)S(1)}, bf16[256,1024]{1,0:T(8,128)(2,1)S(1)}, u32[]{:S(2)}, u32[]{:S(2)}) collective-permute-start(bf16[256,1024]{1,0:T(8,128)(2,1)S(1)} %advect.9), channel_id=1, source_target_pairs={{15,0},{0,1},{1,2},{2,3},{3,4},{4,5},{5,6},{6,7},{7,8},{8,9},{9,10... | collective-permute-start | bytes 1572872 | tf_op jit(solution)/shard_map/ppermute | solution.py:28
  66.0 24.0 %collective-permute-start.5 = (bf16[256,1024]{1,0:T(8,128)(2,1)S(1)}, bf16[256,1024]{1,0:T(8,128)(2,1)S(1)}, u32[]{:S(2)}, u32[]{:S(2)}) collective-permute-start(bf16[256,1024]{1,0:T(8,128)(2,1)S(1)} %advect.10), channel_id=1, source_target_pairs={{1,0},{2,1},{3,2},{4,3},{5,4},{6,5},{7,6},{8,7},{9,8},{10,9},{11,1... | collective-permute-start | bytes 1572872 | tf_op jit(solution)/shard_map/ppermute | solution.py:28
  68.6 20.2 %copy-start.2 = (s32[1,16,2]{1,2,0:T(2,128)S(1)}, s32[1,16,2]{1,2,0:T(2,128)}, u32[]{:S(2)}) copy-start(s32[1,16,2]{1,2,0:T(2,128)} %param.5) | copy-start | bytes 388

commit v4 on v3

--- a/solution.py
+++ b/solution.py
@@ -16,7 +16,7 @@
 ORDER = (-2, -4, 2, 3, -3, 1, -1, 0)
 RIM = 2
 LANES = 128
-META = 16
+META = 8
 CLIP_BOUND = 0.95
 F32 = jnp.float32
 BF16 = jnp.bfloat16
@@ -177,14 +177,12 @@
         side = 0 if offset + FIRST == 1 else 1
         edges[side].wait()
         for rim in range(RIM):
-            column = side * (columns - RIM) + rim
             for half in range(halves):
                 outs[offset][pl.ds(at, rows), :] = edge_ref[
                     side, rim, :, half * LANES : (half + 1) * LANES
                 ]
                 at += rows
-            outs[offset][pl.ds(at, rows), :] = wind_ref[column]
-            at += rows
+        outs[offset][pl.ds(at, rows), :] = wind_ref[side * (columns - 1)]
 
 
 def prepare_kernel(
@@ -219,13 +217,20 @@
         return carry
 
     lax.fori_loop(0, columns, own, 0, unroll=4)
-    for side, ref in ((0, low_ref), (columns + RIM, high_ref)):
+    for side, near, far, ref in (
+        (0, RIM - 1, 0, low_ref),
+        (columns + RIM, columns + RIM, columns + 2 * RIM - 1, high_ref),
+    ):
         for rim in range(RIM):
-            start = rim_at + rim * (halves + 1) * rows
             at = pl.ds((side + rim) * pitch, rows)
             for half in range(halves):
-                wide_t_ref[half, at, :] = ref[pl.ds(start + half * rows, rows), :].astype(F32)
-            wide_w_ref[at, :] = ref[pl.ds(start + halves * rows, rows), :].astype(F32)
+                wide_t_ref[half, at, :] = ref[
+                    pl.ds(rim_at + (rim * halves + half) * rows, rows), :
+                ].astype(F32)
+        wide_w_ref[pl.ds(near * pitch, rows), :] = ref[
+            pl.ds(rim_at + RIM * halves * rows, rows), :
+        ].astype(F32)
+        wide_w_ref[pl.ds(far * pitch, rows), :] = jnp.zeros((rows, LANES), F32)
     for column in range(columns + 2 * RIM, columns - inner + padded_inner):
         at = pl.ds(column * pitch, pitch)
         for half in range(halves):
@@ -464,7 +469,7 @@
     offsets = LAST - FIRST
     halves = tracer_ch // LANES
     rim_at = CAP * 2 * size + META
-    rim_rows = RIM * (halves + 1) * rows
+    rim_rows = (RIM * halves + 1) * rows
 
     wide = per_level * LANES
     table = jnp.transpose(departures, (0, 2, 1))

time: 94.3 us -> 93.8 us (level)
  transfers between devices with their start and end apart: 14 -> 14, of which waited for: 5 -> 5; matrix products, arithmetic and copies ran while one was open for 0% -> 0% of each run, Pallas kernels for 22% -> 23%
where the time goes in v4:
time: 93.8 us; the launch traced here: 92.1 us
  waiting for transfers between devices  40.8 us (43%)
  Pallas kernels  25.9 us (28%)
  starting transfers between devices  25.2 us (27%)
    ppermute x14, waiting for transfers between devices, shifted(): return lax.ppermute(block, axis, route)  40.8 us
    ppermute x14, starting transfers between devices, shifted(): return lax.ppermute(block, axis, route)  25.2 us
    pallas_call x8, Pallas kernels, on_device(): result = advect(arrived[n], fields, extra, join)  14.4 us
    pallas_call x1, Pallas kernels, on_device(): prepare(tracers, wind_fields, arrived[-1], arrived[1], spread)  5.08 us
    pallas_call x1, Pallas kernels, on_device(): pl.pallas_call(functools.partial(wind_kernel, (columns, rows, inner, band...  2.75 us
    pallas_call x1, Pallas kernels, on_device(): return last(table, *[received[n - FIRST] for n in late], spread_out)[0]  2.47 us
  transfers between devices with their start and end apart: 14, of which 5 were waited for; matrix products, arithmetic and copies ran while one was open for 0% of the time, Pallas kernels for 23%

profile of v4, /device:TPU:0, one launch (start us, length us, event | category | flops | bytes accessed | tf_op | source)
XLA Modules:
  0.0 92.1 jit_solution(15494596875464385353)
XLA Ops:
  0.0 0.0 copy-start.1
  0.0 0.0 copy-start
  0.0 2.7 %winds.1 = (bf16[520,128]{1,0:T(8,128)(2,1)S(1)}, bf16[520,128]{1,0:T(8,128)(2,1)S(1)}, bf16[520,128]{1,0:T(8,128)(2,1)S(1)}, bf16[840,128]{1,0:T(8,128)(2,1)S(1...) custom-call(s32[1,2,16]{2,1,0:T(2,128)} %bitcast.1, ...), custom_call_target="tpu_custom_call" | custom-call | flops 4000000 | bytes 3000000 | tf_op jit(solution)/shard_map/winds/pallas_call | solution.py:485
  2.8 0.5 collective-permute-start.1
  3.3 5.0 %collective-permute-start.2 = (bf16[840,128]{1,0:T(8,128)(2,1)S(1)}, bf16[840,128]{1,0:T(8,128)(2,1)S(1)}, u32[]{:S(2)}, u32[]{:S(2)}) collective-permute-start(bf16[840,128]{1,0:T(8,128)(2,1)S(1)} %get-tuple-element.20), channel_id=1, source_target_pairs={{1,0},{2,1},{3,2},{4,3},{5,4},{6,5},{7,6},{8,7},{9,8},{10,9},{11,1... | collective-permute-start | bytes 645128 | tf_op jit(solution)/shard_map/ppermute | solution.py:28
  8.3 0.0 collective-permute-start.6
  8.4 0.8 collective-permute-start.8
  9.1 2.8 %collective-permute-done.1.low_ref.msg_ref = bf16[840,128]{1,0:T(8,128)(2,1)S(1)} collective-permute-done((bf16[840,128]{1,0:T(8,128)(2,1)S(1)}, bf16[840,128]{1,0:T(8,128)(2,1)S(1)}, u32[]{:S(2)}, u32[]{:S(2)}) %collective-permute-start.1) | collective-permute-done | bytes 215072 | tf_op jit(solution)/shard_map/ppermute | solution.py:28
  11.9 0.7 collective-permute-done.2.high_ref.msg_ref
  12.6 0.0 copy-done.1
  12.6 0.0 copy-done
  12.6 5.1 %prepare.1 = (f32[8,69,24,128]{3,2,1,0:T(8,128)S(1)}, f32[2,69,24,128]{3,2,1,0:T(8,128)S(1)}) custom-call(bf16[64,64,256]{2,1,0:T(8,128)(2,1)S(1)} %copy-done, bf16[64,64,128]{2,1,0:T(8,128)(2,1)S(1)} %copy-done.1, bf16[840,128]{1,0:T(8,128)(2,1)S(1)} %collective-permute-done.1.low_ref.msg_ref, bf16[840,128]{1,0:T(8,128)(2,1)S(1)} %collective-permute-done.2.high_ref.msg_ref, ...), custom_call_target="tpu_custom_call" | custom-call | flops 16000000 | bytes 12000000 | tf_op jit(solution)/shard_map/prepare/pallas_call | solution.py:535
  17.7 0.0 collective-permute-done.6.msg_ref
  17.7 2.1 %advect.11 = bf16[256,1024]{1,0:T(8,128)(2,1)S(1)} custom-call(bf16[520,128]{1,0:T(8,128)(2,1)S(1)} %collective-permute-done.6.msg_ref, f32[8,69,24,128]{3,2,1,0:T(8,128)S(1)} %get-tuple-element.22.t_ref, f32[2,69,24,128]{3,2,1,0:T(8,128)S(1)} %get-tuple-element.23.e_ref, bf16[1024,1024]{1,0:T(8,128)(2,1)S(1)} %get-tuple-element.24.perm_ref), custom_call_target="tpu_custom_call" | custom-call | flops 16000000 | bytes 6000000 | tf_op jit(solution)/shard_map/advect/pallas_call | solution.py:554
  19.9 5.0 %collective-permute-start.7 = (bf16[256,1024]{1,0:T(8,128)(2,1)S(1)}, bf16[256,1024]{1,0:T(8,128)(2,1)S(1)}, u32[]{:S(2)}, u32[]{:S(2)}) collective-permute-start(bf16[256,1024]{1,0:T(8,128)(2,1)S(1)} %advect.11), channel_id=1, source_target_pairs={{2,0},{3,1},{4,2},{5,3},{6,4},{7,5},{8,6},{9,7},{10,8},{11,9},{12,... | collective-permute-start | bytes 1572872 | tf_op jit(solution)/shard_map/ppermute | solution.py:28
  24.9 0.0 collective-permute-done.8.msg_ref
  24.9 1.5 %advect.12 = bf16[256,1024]{1,0:T(8,128)(2,1)S(1)} custom-call(bf16[520,128]{1,0:T(8,128)(2,1)S(1)} %collective-permute-done.8.msg_ref, f32[8,69,24,128]{3,2,1,0:T(8,128)S(1)} %get-tuple-element.22.t_ref, f32[2,69,24,128]{3,2,1,0:T(8,128)S(1)} %get-tuple-element.23.e_ref, bf16[1024,1024]{1,0:T(8,128)(2,1)S(1)} %get-tuple-element.24.perm_ref), custom_call_target="tpu_custom_call" | custom-call | flops 16000000 | bytes 6000000 | tf_op jit(solution)/shard_map/advect/pallas_call | solution.py:554
  26.4 1.7 %collective-permute-start.9 = (bf16[256,1024]{1,0:T(8,128)(2,1)S(1)}, bf16[256,1024]{1,0:T(8,128)(2,1)S(1)}, u32[]{:S(2)}, u32[]{:S(2)}) collective-permute-start(bf16[256,1024]{1,0:T(8,128)(2,1)S(1)} %advect.12), channel_id=1, source_target_pairs={{4,0},{5,1},{6,2},{7,3},{8,4},{9,5},{10,6},{11,7},{12,8},{13,9},{1... | collective-permute-start | bytes 1572872 | tf_op jit(solution)/shard_map/ppermute | solution.py:28
  28.1 0.8 collective-permute-start
  29.0 3.0 %collective-permute-start.10 = (bf16[520,128]{1,0:T(8,128)(2,1)S(1)}, bf16[520,128]{1,0:T(8,128)(2,1)S(1)}, u32[]{:S(2)}, u32[]{:S(2)}) collective-permute-start(bf16[520,128]{1,0:T(8,128)(2,1)S(1)} %get-tuple-element.27), channel_id=1, source_target_pairs={{2,0},{3,1},{4,2},{5,3},{6,4},{7,5},{8,6},{9,7},{10,8},{11,9},{12,... | collective-permute-start | bytes 399368 | tf_op jit(solution)/shard_map/ppermute | solution.py:28
  32.0 0.0 collective-permute-start.12
  32.0 19.1 %collective-permute-done.msg_ref = bf16[520,128]{1,0:T(8,128)(2,1)S(1)} collective-permute-done((bf16[520,128]{1,0:T(8,128)(2,1)S(1)}, bf16[520,128]{1,0:T(8,128)(2,1)S(1)}, u32[]{:S(2)}, u32[]{:S(2)}) %collective-permute-start) | collective-permute-done | bytes 133152 | tf_op jit(solution)/shard_map/ppermute | solution.py:28
  51.0 2.7 %advect.8 = bf16[256,1024]{1,0:T(8,128)(2,1)S(1)} custom-call(bf16[520,128]{1,0:T(8,128)(2,1)S(1)} %collective-permute-done.msg_ref, f32[8,69,24,128]{3,2,1,0:T(8,128)S(1)} %get-tuple-element.22.t_ref, f32[2,69,24,128]{3,2,1,0:T(8,128)S(1)} %get-tuple-element.23.e_ref, bf16[1024,1024]{1,0:T(8,128)(2,1)S(1)} %get-tuple-element.24.perm_ref), custom_call_target="tpu_custom_call" | custom-call | flops 16000000 | bytes 6000000 | tf_op jit(solution)/shard_map/advect/pallas_call | solution.py:554
  53.7 0.1 collective-permute-start.3
  53.8 0.0 collective-permute-done.10.msg_ref
  53.8 0.9 advect.13
  54.7 2.1 %collective-permute-start.11 = (bf16[256,1024]{1,0:T(8,128)(2,1)S(1)}, bf16[256,1024]{1,0:T(8,128)(2,1)S(1)}, u32[]{:S(2)}, u32[]{:S(2)}) collective-permute-start(bf16[256,1024]{1,0:T(8,128)(2,1)S(1)} %advect.13), channel_id=1, source_target_pairs={{14,0},{15,1},{0,2},{1,3},{2,4},{3,5},{4,6},{5,7},{6,8},{7,9},{8,1... | collective-permute-start | bytes 1572872 | tf_op jit(solution)/shard_map/ppermute | solution.py:28
  56.8 0.0 collective-permute-done.12.msg_ref
  56.8 1.5 %advect.14 = bf16[256,1024]{1,0:T(8,128)(2,1)S(1)} custom-call(bf16[520,128]{1,0:T(8,128)(2,1)S(1)} %collective-permute-done.12.msg_ref, f32[8,69,24,128]{3,2,1,0:T(8,128)S(1)} %get-tuple-element.22.t_ref, f32[2,69,24,128]{3,2,1,0:T(8,128)S(1)} %get-tuple-element.23.e_ref, bf16[1024,1024]{1,0:T(8,128)(2,1)S(1)} %get-tuple-element.24.perm_ref), custom_call_target="tpu_custom_call" | custom-call | flops 16000000 | bytes 6000000 | tf_op jit(solution)/shard_map/advect/pallas_call | solution.py:554
  58.3 1.6 %collective-permute-start.13 = (bf16[256,1024]{1,0:T(8,128)(2,1)S(1)}, bf16[256,1024]{1,0:T(8,128)(2,1)S(1)}, u32[]{:S(2)}, u32[]{:S(2)}) collective-permute-start(bf16[256,1024]{1,0:T(8,128)(2,1)S(1)} %advect.14), channel_id=1, source_target_pairs={{13,0},{14,1},{15,2},{0,3},{1,4},{2,5},{3,6},{4,7},{5,8},{6,9},{7,... | collective-permute-start | bytes 1572872 | tf_op jit(solution)/shard_map/ppermute | solution.py:28
  59.9 2.1 %advect.10 = bf16[256,1024]{1,0:T(8,128)(2,1)S(1)} custom-call(bf16[840,128]{1,0:T(8,128)(2,1)S(1)} %collective-permute-done.1.low_ref.msg_ref, f32[8,69,24,128]{3,2,1,0:T(8,128)S(1)} %get-tuple-element.22.t_ref, f32[2,69,24,128]{3,2,1,0:T(8,128)S(1)} %get-tuple-element.23.e_ref, bf16[1024,1024]{1,0:T(8,128)(2,1)S(1)} %get-tuple-element.24.perm_ref), custom_call_target="tpu_custom_call" | custom-call | flops 16000000 | bytes 6000000 | tf_op jit(solution)/shard_map/advect/pallas_call | solution.py:554
  62.0 1.5 %advect.9 = bf16[256,1024]{1,0:T(8,128)(2,1)S(1)} custom-call(bf16[840,128]{1,0:T(8,128)(2,1)S(1)} %collective-permute-done.2.high_ref.msg_ref, f32[8,69,24,128]{3,2,1,0:T(8,128)S(1)} %get-tuple-element.22.t_ref, f32[2,69,24,128]{3,2,1,0:T(8,128)S(1)} %get-tuple-element.23.e_ref, bf16[1024,1024]{1,0:T(8,128)(2,1)S(1)} %get-tuple-element.24.perm_ref), custom_call_target="tpu_custom_call" | custom-call | flops 16000000 | bytes 6000000 | tf_op jit(solution)/shard_map/advect/pallas_call | solution.py:554
  63.5 0.0 collective-permute-done.7.rest_0_
  63.6 2.0 %collective-permute-start.4 = (bf16[256,1024]{1,0:T(8,128)(2,1)S(1)}, bf16[256,1024]{1,0:T(8,128)(2,1)S(1)}, u32[]{:S(2)}, u32[]{:S(2)}) collective-permute-start(bf16[256,1024]{1,0:T(8,128)(2,1)S(1)} %advect.9), channel_id=1, source_target_pairs={{15,0},{0,1},{1,2},{2,3},{3,4},{4,5},{5,6},{6,7},{7,8},{8,9},{9,10... | collective-permute-start | bytes 1572872 | tf_op jit(solution)/shard_map/ppermute | solution.py:28
  65.6 0.0 collective-permute-done.9.rest_1_
  65.6 2.5 %collective-permute-start.5 = (bf16[256,1024]{1,0:T(8,128)(2,1)S(1)}, bf16[256,1024]{1,0:T(8,128)(2,1)S(1)}, u32[]{:S(2)}, u32[]{:S(2)}) collective-permute-start(bf16[256,1024]{1,0:T(8,128)(2,1)S(1)} %advect.10), channel_id=1, source_target_pairs={{1,0},{2,1},{3,2},{4,3},{5,4},{6,5},{7,6},{8,7},{9,8},{10,9},{11,1... | collective-permute-start | bytes 1572872 | tf_op jit(solution)/shard_map/ppermute | solution.py:28
  68.0 0.0 copy-start.2
  68.1 2.1 %advect.15.rest_4_ = bf16[256,1024]{1,0:T(8,128)(2,1)S(1)} custom-call(bf16[520,128]{1,0:T(8,128)(2,1)S(1)} %get-tuple-element.29.msg_ref, f32[8,69,24,128]{3,2,1,0:T(8,128)S(1)} %get-tuple-element.22.t_ref, f32[2,69,24,128]{3,2,1,0:T(8,128)S(1)} %get-tuple-element.23.e_ref, bf16[1024,1024]{1,0:T(8,128)(2,1)S(1)} %get-tuple-element.24.perm_ref), custom_call_target="tpu_custom_call" | custom-call | flops 16000000 | bytes 6000000 | tf_op jit(solution)/shard_map/advect/pallas_call | solution.py:554
  70.2 3.5 %collective-permute-done.11.rest_2_ = bf16[256,1024]{1,0:T(8,128)(2,1)S(1)} collective-permute-done((bf16[256,1024]{1,0:T(8,128)(2,1)S(1)}, bf16[256,1024]{1,0:T(8,128)(2,1)S(1)}, u32[]{:S(2)}, u32[]{:S(2)}) %collective-permute-start.11) | collective-permute-done | bytes 524320 | tf_op jit(solution)/shard_map/ppermute | solution.py:28
  73.6 14.7 %collective-permute-done.13.rest_3_ = bf16[256,1024]{1,0:T(8,128)(2,1)S(1)} collective-permute-done((bf16[256,1024]{1,0:T(8,128)(2,1)S(1)}, bf16[256,1024]{1,0:T(8,128)(2,1)S(1)}, u32[]{:S(2)}, u32[]{:S(2)}) %collective-permute-start.13) | collective-permute-done | bytes 524320 | tf_op jit(solution)/shard_map/ppermute | solution.py:28
  88.3 0.0 copy-done.2
  88.3 1.2 %early.1.rest_3_ = f32[2,4160,128]{2,1,0:T(8,128)S(1)} custom-call(s32[1,2,16]{2,1,0:T(2,128)S(1)} %bitcast.2, bf16[256,1024]{1,0:T(8,128)(2,1)S(1)} %collective-permute-done.7.rest_0_, bf16[256,1024]{1,0:T(8,128)(2,1)S(1)} %collective-permute-done.9.rest_1_, bf16[256,1024]{1,0:T(8,128)(2,1)S(1)} %collective-permute-done.11.rest_2_, ...), custom_call_target="tpu_custom_call" | custom-call | flops 2000000 | bytes 6000000 | tf_op jit(solution)/shard_map/early/pallas_call | solution.py:571
  89.6 0.0 collective-permute-done.3.rest_0_
  89.6 0.0 collective-permute-done.4.rest_1_
  89.6 0.0 collective-permute-done.5.rest_2_
  89.6 2.5 %late.1 = (bf16[64,64,256]{2,1,0:T(8,128)(2,1)}, f32[2,4160,128]{2,1,0:T(8,128)S(1)}) custom-call(s32[1,2,16]{2,1,0:T(2,128)S(1)} %bitcast.3, bf16[256,1024]{1,0:T(8,128)(2,1)S(1)} %collective-permute-done.3.rest_0_, bf16[256,1024]{1,0:T(8,128)(2,1)S(1)} %collective-permute-done.4.rest_1_, ...), custom_call_target="tpu_custom_call", output_to_operand_aliasing={{1}: (4, {})} | custom-call | flops 2000000 | bytes 6000000 | tf_op jit(solution)/shard_map/late/pallas_call | solution.py:584
Async XLA Ops:
  0.0 12.6 %copy-start.1 = (bf16[64,64,128]{2,1,0:T(8,128)(2,1)S(1)}, bf16[64,64,128]{2,1,0:T(8,128)(2,1)}, u32[]{:S(2)}) copy-start(bf16[64,64,128]{2,1,0:T(8,128)(2,1)} %wind_ref.1) | copy-start | bytes 3145732
  0.0 12.6 %copy-start = (bf16[64,64,256]{2,1,0:T(8,128)(2,1)S(1)}, bf16[64,64,256]{2,1,0:T(8,128)(2,1)}, u32[]{:S(2)}) copy-start(bf16[64,64,256]{2,1,0:T(8,128)(2,1)} %tracers_ref.3) | copy-start | bytes 6291460
  2.8 9.2 %collective-permute-start.1 = (bf16[840,128]{1,0:T(8,128)(2,1)S(1)}, bf16[840,128]{1,0:T(8,128)(2,1)S(1)}, u32[]{:S(2)}, u32[]{:S(2)}) collective-permute-start(bf16[840,128]{1,0:T(8,128)(2,1)S(1)} %get-tuple-element.19), channel_id=1, source_target_pairs={{15,0},{0,1},{1,2},{2,3},{3,4},{4,5},{5,6},{6,7},{7,8},{8,9},{9,10... | collective-permute-start | bytes 645128 | tf_op jit(solution)/shard_map/ppermute | solution.py:28
  3.3 9.3 %collective-permute-start.2 = (bf16[840,128]{1,0:T(8,128)(2,1)S(1)}, bf16[840,128]{1,0:T(8,128)(2,1)S(1)}, u32[]{:S(2)}, u32[]{:S(2)}) collective-permute-start(bf16[840,128]{1,0:T(8,128)(2,1)S(1)} %get-tuple-element.20), channel_id=1, source_target_pairs={{1,0},{2,1},{3,2},{4,3},{5,4},{6,5},{7,6},{8,7},{9,8},{10,9},{11,1... | collective-permute-start | bytes 645128 | tf_op jit(solution)/shard_map/ppermute | solution.py:28
  8.3 9.4 %collective-permute-start.6 = (bf16[520,128]{1,0:T(8,128)(2,1)S(1)}, bf16[520,128]{1,0:T(8,128)(2,1)S(1)}, u32[]{:S(2)}, u32[]{:S(2)}) collective-permute-start(bf16[520,128]{1,0:T(8,128)(2,1)S(1)} %get-tuple-element.25), channel_id=1, source_target_pairs={{14,0},{15,1},{0,2},{1,3},{2,4},{3,5},{4,6},{5,7},{6,8},{7,9},{8,1... | collective-permute-start | bytes 399368 | tf_op jit(solution)/shard_map/ppermute | solution.py:28
  8.4 16.5 %collective-permute-start.8 = (bf16[520,128]{1,0:T(8,128)(2,1)S(1)}, bf16[520,128]{1,0:T(8,128)(2,1)S(1)}, u32[]{:S(2)}, u32[]{:S(2)}) collective-permute-start(bf16[520,128]{1,0:T(8,128)(2,1)S(1)} %get-tuple-element.26), channel_id=1, source_target_pairs={{12,0},{13,1},{14,2},{15,3},{0,4},{1,5},{2,6},{3,7},{4,8},{5,9},{6... | collective-permute-start | bytes 399368 | tf_op jit(solution)/shard_map/ppermute | solution.py:28
  19.9 43.7 %collective-permute-start.7 = (bf16[256,1024]{1,0:T(8,128)(2,1)S(1)}, bf16[256,1024]{1,0:T(8,128)(2,1)S(1)}, u32[]{:S(2)}, u32[]{:S(2)}) collective-permute-start(bf16[256,1024]{1,0:T(8,128)(2,1)S(1)} %advect.11), channel_id=1, source_target_pairs={{2,0},{3,1},{4,2},{5,3},{6,4},{7,5},{8,6},{9,7},{10,8},{11,9},{12,... | collective-permute-start | bytes 1572872 | tf_op jit(solution)/shard_map/ppermute | solution.py:28
  26.4 39.2 %collective-permute-start.9 = (bf16[256,1024]{1,0:T(8,128)(2,1)S(1)}, bf16[256,1024]{1,0:T(8,128)(2,1)S(1)}, u32[]{:S(2)}, u32[]{:S(2)}) collective-permute-start(bf16[256,1024]{1,0:T(8,128)(2,1)S(1)} %advect.12), channel_id=1, source_target_pairs={{4,0},{5,1},{6,2},{7,3},{8,4},{9,5},{10,6},{11,7},{12,8},{13,9},{1... | collective-permute-start | bytes 1572872 | tf_op jit(solution)/shard_map/ppermute | solution.py:28
  28.1 22.9 %collective-permute-start = (bf16[520,128]{1,0:T(8,128)(2,1)S(1)}, bf16[520,128]{1,0:T(8,128)(2,1)S(1)}, u32[]{:S(2)}, u32[]{:S(2)}) collective-permute-start(bf16[520,128]{1,0:T(8,128)(2,1)S(1)} %get-tuple-element.18), channel_id=1, source_target_pairs={{13,0},{14,1},{15,2},{0,3},{1,4},{2,5},{3,6},{4,7},{5,8},{6,9},{7,... | collective-permute-start | bytes 399368 | tf_op jit(solution)/shard_map/ppermute | solution.py:28
  29.0 24.9 %collective-permute-start.10 = (bf16[520,128]{1,0:T(8,128)(2,1)S(1)}, bf16[520,128]{1,0:T(8,128)(2,1)S(1)}, u32[]{:S(2)}, u32[]{:S(2)}) collective-permute-start(bf16[520,128]{1,0:T(8,128)(2,1)S(1)} %get-tuple-element.27), channel_id=1, source_target_pairs={{2,0},{3,1},{4,2},{5,3},{6,4},{7,5},{8,6},{9,7},{10,8},{11,9},{12,... | collective-permute-start | bytes 399368 | tf_op jit(solution)/shard_map/ppermute | solution.py:28
  32.0 24.9 %collective-permute-start.12 = (bf16[520,128]{1,0:T(8,128)(2,1)S(1)}, bf16[520,128]{1,0:T(8,128)(2,1)S(1)}, u32[]{:S(2)}, u32[]{:S(2)}) collective-permute-start(bf16[520,128]{1,0:T(8,128)(2,1)S(1)} %get-tuple-element.28), channel_id=1, source_target_pairs={{3,0},{4,1},{5,2},{6,3},{7,4},{8,5},{9,6},{10,7},{11,8},{12,9},{13... | collective-permute-start | bytes 399368 | tf_op jit(solution)/shard_map/ppermute | solution.py:28
  53.7 35.8 %collective-permute-start.3 = (bf16[256,1024]{1,0:T(8,128)(2,1)S(1)}, bf16[256,1024]{1,0:T(8,128)(2,1)S(1)}, u32[]{:S(2)}, u32[]{:S(2)}) collective-permute-start(bf16[256,1024]{1,0:T(8,128)(2,1)S(1)} %advect.8), channel_id=1, source_target_pairs={{3,0},{4,1},{5,2},{6,3},{7,4},{8,5},{9,6},{10,7},{11,8},{12,9},{13... | collective-permute-start | bytes 1572872 | tf_op jit(solution)/shard_map/ppermute | solution.py:28
  54.7 18.9 %collective-permute-start.11 = (bf16[256,1024]{1,0:T(8,128)(2,1)S(1)}, bf16[256,1024]{1,0:T(8,128)(2,1)S(1)}, u32[]{:S(2)}, u32[]{:S(2)}) collective-permute-start(bf16[256,1024]{1,0:T(8,128)(2,1)S(1)} %advect.13), channel_id=1, source_target_pairs={{14,0},{15,1},{0,2},{1,3},{2,4},{3,5},{4,6},{5,7},{6,8},{7,9},{8,1... | collective-permute-start | bytes 1572872 | tf_op jit(solution)/shard_map/ppermute | solution.py:28
  58.3 30.0 %collective-permute-start.13 = (bf16[256,1024]{1,0:T(8,128)(2,1)S(1)}, bf16[256,1024]{1,0:T(8,128)(2,1)S(1)}, u32[]{:S(2)}, u32[]{:S(2)}) collective-permute-start(bf16[256,1024]{1,0:T(8,128)(2,1)S(1)} %advect.14), channel_id=1, source_target_pairs={{13,0},{14,1},{15,2},{0,3},{1,4},{2,5},{3,6},{4,7},{5,8},{6,9},{7,... | collective-permute-start | bytes 1572872 | tf_op jit(solution)/shard_map/ppermute | solution.py:28
  63.6 26.0 %collective-permute-start.4 = (bf16[256,1024]{1,0:T(8,128)(2,1)S(1)}, bf16[256,1024]{1,0:T(8,128)(2,1)S(1)}, u32[]{:S(2)}, u32[]{:S(2)}) collective-permute-start(bf16[256,1024]{1,0:T(8,128)(2,1)S(1)} %advect.9), channel_id=1, source_target_pairs={{15,0},{0,1},{1,2},{2,3},{3,4},{4,5},{5,6},{6,7},{7,8},{8,9},{9,10... | collective-permute-start | bytes 1572872 | tf_op jit(solution)/shard_map/ppermute | solution.py:28
  65.6 24.0 %collective-permute-start.5 = (bf16[256,1024]{1,0:T(8,128)(2,1)S(1)}, bf16[256,1024]{1,0:T(8,128)(2,1)S(1)}, u32[]{:S(2)}, u32[]{:S(2)}) collective-permute-start(bf16[256,1024]{1,0:T(8,128)(2,1)S(1)} %advect.10), channel_id=1, source_target_pairs={{1,0},{2,1},{3,2},{4,3},{5,4},{6,5},{7,6},{8,7},{9,8},{10,9},{11,1... | collective-permute-start | bytes 1572872 | tf_op jit(solution)/shard_map/ppermute | solution.py:28
  68.0 20.3 %copy-start.2 = (s32[1,16,2]{1,2,0:T(2,128)S(1)}, s32[1,16,2]{1,2,0:T(2,128)}, u32[]{:S(2)}) copy-start(s32[1,16,2]{1,2,0:T(2,128)} %param.5) | copy-start | bytes 388

commit v5 on v4

--- a/solution.py
+++ b/solution.py
@@ -425,11 +425,10 @@
     collect(sizes, slot_ref, zip(offsets, ins), wide_ref)
 
 
-def late_kernel(sizes, offsets, dep_ref, *rest):
+def late_kernel(sizes, offsets, slot_ref, *rest):
     columns, rows = sizes[:2]
     ins = rest[: len(offsets)]
-    _, out_ref, wide_ref, slot_ref, count_ref, stage_ref, sem_ref = rest[len(offsets) :]
-    fill_slots(dep_ref, slot_ref, count_ref, sizes[3])
+    _, out_ref, wide_ref, stage_ref, sem_ref = rest[len(offsets) :]
     collect(sizes, slot_ref, zip(offsets, ins), wide_ref)
     pitch = rows + 1
     halves = wide_ref.shape[0]
@@ -560,28 +559,30 @@
     late = ORDER[offsets - 1 - LATE : -1]
     first = pl.pallas_call(
         functools.partial(early_kernel, sizes, early),
-        out_shape=wide_shape,
+        out_shape=[wide_shape, jax.ShapeDtypeStruct((offsets * CAP,), jnp.int32)],
         in_specs=[smem] + [vmem] * len(early),
-        out_specs=vmem,
-        scratch_shapes=tables,
+        out_specs=[vmem, smem],
+        scratch_shapes=tables[1:],
         compiler_params=params(8),
         cost_estimate=pl.CostEstimate(flops=2_000_000, bytes_accessed=6_000_000, transcendentals=0),
         name="early",
     )
-    spread_out = first(table, *[received[n - FIRST] for n in early])
+    spread_out, slots = first(table, *[received[n - FIRST] for n in early])
     last = pl.pallas_call(
         functools.partial(late_kernel, sizes, late),
         out_shape=[jax.ShapeDtypeStruct((columns, rows, tracer_ch), BF16), wide_shape],
         in_specs=[smem] + [vmem] * (len(late) + 1),
         out_specs=[pl.BlockSpec(memory_space=pl.ANY), vmem],
-        scratch_shapes=tables
-        + [pltpu.VMEM((columns, rows, tracer_ch), BF16), pltpu.SemaphoreType.DMA((8,))],
+        scratch_shapes=[
+            pltpu.VMEM((columns, rows, tracer_ch), BF16),
+            pltpu.SemaphoreType.DMA((8,)),
+        ],
         input_output_aliases={len(late) + 1: 1},
         compiler_params=params(8),
         cost_estimate=pl.CostEstimate(flops=2_000_000, bytes_accessed=6_000_000, transcendentals=0),
         name="late",
     )
-    return last(table, *[received[n - FIRST] for n in late], spread_out)[0]
+    return last(slots, *[received[n - FIRST] for n in late], spread_out)[0]
 
 
 def solution(mesh):

time: 93.8 us -> 94.2 us (level)
  the two profiles are of different devices: /device:TPU:0 before, /device:TPU:3 now
where the time goes in v5:
time: 94.2 us; the launch traced here: 94.1 us
  waiting for transfers between devices  43.6 us (46%)
  Pallas kernels  28.8 us (31%)
  starting transfers between devices  21.6 us (23%)
    ppermute x14, waiting for transfers between devices, shifted(): return lax.ppermute(block, axis, route)  43.6 us
    ppermute x14, starting transfers between devices, shifted(): return lax.ppermute(block, axis, route)  21.6 us
    pallas_call x8, Pallas kernels, on_device(): result = advect(arrived[n], fields, extra, join)  16.9 us
    pallas_call x1, Pallas kernels, on_device(): prepare(tracers, wind_fields, arrived[-1], arrived[1], spread)  5.07 us
    pallas_call x1, Pallas kernels, on_device(): pl.pallas_call(functools.partial(wind_kernel, (columns, rows, inner, band...  2.74 us
    pallas_call x1, Pallas kernels, on_device(): return last(slots, *[received[n - FIRST] for n in late], spread_out)[0]  2.22 us
  transfers between devices with their start and end apart: 14, of which 6 were waited for; matrix products, arithmetic and copies ran while one was open for 0% of the time, Pallas kernels for 25%

profile of v5, /device:TPU:3, one launch (start us, length us, event | category | flops | bytes accessed | tf_op | source)
XLA Modules:
  0.0 94.1 jit_solution(16031681787672916914)
XLA Ops:
  0.0 0.0 copy-start.1
  0.0 0.0 copy-start
  0.0 2.7 %winds.1 = (bf16[520,128]{1,0:T(8,128)(2,1)S(1)}, bf16[520,128]{1,0:T(8,128)(2,1)S(1)}, bf16[520,128]{1,0:T(8,128)(2,1)S(1)}, bf16[840,128]{1,0:T(8,128)(2,1)S(1...) custom-call(s32[1,2,16]{2,1,0:T(2,128)} %bitcast.1, ...), custom_call_target="tpu_custom_call" | custom-call | flops 4000000 | bytes 3000000 | tf_op jit(solution)/shard_map/winds/pallas_call | solution.py:484
  2.8 1.9 %collective-permute-start.1 = (bf16[840,128]{1,0:T(8,128)(2,1)S(1)}, bf16[840,128]{1,0:T(8,128)(2,1)S(1)}, u32[]{:S(2)}, u32[]{:S(2)}) collective-permute-start(bf16[840,128]{1,0:T(8,128)(2,1)S(1)} %get-tuple-element.21), channel_id=1, source_target_pairs={{15,0},{0,1},{1,2},{2,3},{3,4},{4,5},{5,6},{6,7},{7,8},{8,9},{9,10... | collective-permute-start | bytes 645128 | tf_op jit(solution)/shard_map/ppermute | solution.py:28
  4.6 0.0 collective-permute-start.2
  4.6 1.2 %collective-permute-start = (bf16[520,128]{1,0:T(8,128)(2,1)S(1)}, bf16[520,128]{1,0:T(8,128)(2,1)S(1)}, u32[]{:S(2)}, u32[]{:S(2)}) collective-permute-start(bf16[520,128]{1,0:T(8,128)(2,1)S(1)} %get-tuple-element.20), channel_id=1, source_target_pairs={{14,0},{15,1},{0,2},{1,3},{2,4},{3,5},{4,6},{5,7},{6,8},{7,9},{8,1... | collective-permute-start | bytes 399368 | tf_op jit(solution)/shard_map/ppermute | solution.py:28
  5.9 1.3 %collective-permute-start.4 = (bf16[520,128]{1,0:T(8,128)(2,1)S(1)}, bf16[520,128]{1,0:T(8,128)(2,1)S(1)}, u32[]{:S(2)}, u32[]{:S(2)}) collective-permute-start(bf16[520,128]{1,0:T(8,128)(2,1)S(1)} %get-tuple-element.27), channel_id=1, source_target_pairs={{12,0},{13,1},{14,2},{15,3},{0,4},{1,5},{2,6},{3,7},{4,8},{5,9},{6... | collective-permute-start | bytes 399368 | tf_op jit(solution)/shard_map/ppermute | solution.py:28
  7.2 0.3 collective-permute-done.1.low_ref.msg_ref
  7.4 6.6 %collective-permute-done.2.high_ref.msg_ref = bf16[840,128]{1,0:T(8,128)(2,1)S(1)} collective-permute-done((bf16[840,128]{1,0:T(8,128)(2,1)S(1)}, bf16[840,128]{1,0:T(8,128)(2,1)S(1)}, u32[]{:S(2)}, u32[]{:S(2)}) %collective-permute-start.2) | collective-permute-done | bytes 215072 | tf_op jit(solution)/shard_map/ppermute | solution.py:28
  14.0 0.0 copy-done.1
  14.0 0.0 copy-done
  14.0 5.1 %prepare.1 = (f32[8,69,24,128]{3,2,1,0:T(8,128)S(1)}, f32[2,69,24,128]{3,2,1,0:T(8,128)S(1)}) custom-call(bf16[64,64,256]{2,1,0:T(8,128)(2,1)S(1)} %copy-done, bf16[64,64,128]{2,1,0:T(8,128)(2,1)S(1)} %copy-done.1, bf16[840,128]{1,0:T(8,128)(2,1)S(1)} %collective-permute-done.1.low_ref.msg_ref, bf16[840,128]{1,0:T(8,128)(2,1)S(1)} %collective-permute-done.2.high_ref.msg_ref, ...), custom_call_target="tpu_custom_call" | custom-call | flops 16000000 | bytes 12000000 | tf_op jit(solution)/shard_map/prepare/pallas_call | solution.py:534
  19.1 0.0 collective-permute-done.msg_ref
  19.1 2.1 %advect.8 = bf16[256,1024]{1,0:T(8,128)(2,1)S(1)} custom-call(bf16[520,128]{1,0:T(8,128)(2,1)S(1)} %collective-permute-done.msg_ref, f32[8,69,24,128]{3,2,1,0:T(8,128)S(1)} %get-tuple-element.24.t_ref, f32[2,69,24,128]{3,2,1,0:T(8,128)S(1)} %get-tuple-element.25.e_ref, bf16[1024,1024]{1,0:T(8,128)(2,1)S(1)} %get-tuple-element.26.perm_ref), custom_call_target="tpu_custom_call" | custom-call | flops 16000000 | bytes 6000000 | tf_op jit(solution)/shard_map/advect/pallas_call | solution.py:553
  21.2 3.4 %collective-permute-start.3 = (bf16[256,1024]{1,0:T(8,128)(2,1)S(1)}, bf16[256,1024]{1,0:T(8,128)(2,1)S(1)}, u32[]{:S(2)}, u32[]{:S(2)}) collective-permute-start(bf16[256,1024]{1,0:T(8,128)(2,1)S(1)} %advect.8), channel_id=1, source_target_pairs={{2,0},{3,1},{4,2},{5,3},{6,4},{7,5},{8,6},{9,7},{10,8},{11,9},{12,... | collective-permute-start | bytes 1572872 | tf_op jit(solution)/shard_map/ppermute | solution.py:28
  24.6 0.0 collective-permute-done.4.msg_ref
  24.6 1.5 %advect.9 = bf16[256,1024]{1,0:T(8,128)(2,1)S(1)} custom-call(bf16[520,128]{1,0:T(8,128)(2,1)S(1)} %collective-permute-done.4.msg_ref, f32[8,69,24,128]{3,2,1,0:T(8,128)S(1)} %get-tuple-element.24.t_ref, f32[2,69,24,128]{3,2,1,0:T(8,128)S(1)} %get-tuple-element.25.e_ref, bf16[1024,1024]{1,0:T(8,128)(2,1)S(1)} %get-tuple-element.26.perm_ref), custom_call_target="tpu_custom_call" | custom-call | flops 16000000 | bytes 6000000 | tf_op jit(solution)/shard_map/advect/pallas_call | solution.py:553
  26.1 1.4 %collective-permute-start.5 = (bf16[256,1024]{1,0:T(8,128)(2,1)S(1)}, bf16[256,1024]{1,0:T(8,128)(2,1)S(1)}, u32[]{:S(2)}, u32[]{:S(2)}) collective-permute-start(bf16[256,1024]{1,0:T(8,128)(2,1)S(1)} %advect.9), channel_id=1, source_target_pairs={{4,0},{5,1},{6,2},{7,3},{8,4},{9,5},{10,6},{11,7},{12,8},{13,9},{1... | collective-permute-start | bytes 1572872 | tf_op jit(solution)/shard_map/ppermute | solution.py:28
  27.6 1.3 %collective-permute-start.6 = (bf16[520,128]{1,0:T(8,128)(2,1)S(1)}, bf16[520,128]{1,0:T(8,128)(2,1)S(1)}, u32[]{:S(2)}, u32[]{:S(2)}) collective-permute-start(bf16[520,128]{1,0:T(8,128)(2,1)S(1)} %get-tuple-element.28), channel_id=1, source_target_pairs={{2,0},{3,1},{4,2},{5,3},{6,4},{7,5},{8,6},{9,7},{10,8},{11,9},{12,... | collective-permute-start | bytes 399368 | tf_op jit(solution)/shard_map/ppermute | solution.py:28
  28.9 0.6 collective-permute-start.8
  29.5 1.2 %collective-permute-start.10 = (bf16[520,128]{1,0:T(8,128)(2,1)S(1)}, bf16[520,128]{1,0:T(8,128)(2,1)S(1)}, u32[]{:S(2)}, u32[]{:S(2)}) collective-permute-start(bf16[520,128]{1,0:T(8,128)(2,1)S(1)} %get-tuple-element.32), channel_id=1, source_target_pairs={{13,0},{14,1},{15,2},{0,3},{1,4},{2,5},{3,6},{4,7},{5,8},{6,9},{7,... | collective-permute-start | bytes 399368 | tf_op jit(solution)/shard_map/ppermute | solution.py:28
  30.6 19.0 %collective-permute-done.6.msg_ref = bf16[520,128]{1,0:T(8,128)(2,1)S(1)} collective-permute-done((bf16[520,128]{1,0:T(8,128)(2,1)S(1)}, bf16[520,128]{1,0:T(8,128)(2,1)S(1)}, u32[]{:S(2)}, u32[]{:S(2)}) %collective-permute-start.6) | collective-permute-done | bytes 133152 | tf_op jit(solution)/shard_map/ppermute | solution.py:28
  49.6 3.3 %advect.10 = bf16[256,1024]{1,0:T(8,128)(2,1)S(1)} custom-call(bf16[520,128]{1,0:T(8,128)(2,1)S(1)} %collective-permute-done.6.msg_ref, f32[8,69,24,128]{3,2,1,0:T(8,128)S(1)} %get-tuple-element.24.t_ref, f32[2,69,24,128]{3,2,1,0:T(8,128)S(1)} %get-tuple-element.25.e_ref, bf16[1024,1024]{1,0:T(8,128)(2,1)S(1)} %get-tuple-element.26.perm_ref), custom_call_target="tpu_custom_call" | custom-call | flops 16000000 | bytes 6000000 | tf_op jit(solution)/shard_map/advect/pallas_call | solution.py:553
  53.0 0.1 collective-permute-start.7
  53.0 0.0 collective-permute-done.8.msg_ref
  53.0 1.5 %advect.11 = bf16[256,1024]{1,0:T(8,128)(2,1)S(1)} custom-call(bf16[520,128]{1,0:T(8,128)(2,1)S(1)} %collective-permute-done.8.msg_ref, f32[8,69,24,128]{3,2,1,0:T(8,128)S(1)} %get-tuple-element.24.t_ref, f32[2,69,24,128]{3,2,1,0:T(8,128)S(1)} %get-tuple-element.25.e_ref, bf16[1024,1024]{1,0:T(8,128)(2,1)S(1)} %get-tuple-element.26.perm_ref), custom_call_target="tpu_custom_call" | custom-call | flops 16000000 | bytes 6000000 | tf_op jit(solution)/shard_map/advect/pallas_call | solution.py:553
  54.6 1.5 %collective-permute-start.9 = (bf16[256,1024]{1,0:T(8,128)(2,1)S(1)}, bf16[256,1024]{1,0:T(8,128)(2,1)S(1)}, u32[]{:S(2)}, u32[]{:S(2)}) collective-permute-start(bf16[256,1024]{1,0:T(8,128)(2,1)S(1)} %advect.11), channel_id=1, source_target_pairs={{13,0},{14,1},{15,2},{0,3},{1,4},{2,5},{3,6},{4,7},{5,8},{6,9},{7,... | collective-permute-start | bytes 1572872 | tf_op jit(solution)/shard_map/ppermute | solution.py:28
  56.1 0.0 collective-permute-done.10.msg_ref
  56.1 1.5 %advect.13 = bf16[256,1024]{1,0:T(8,128)(2,1)S(1)} custom-call(bf16[520,128]{1,0:T(8,128)(2,1)S(1)} %collective-permute-done.10.msg_ref, f32[8,69,24,128]{3,2,1,0:T(8,128)S(1)} %get-tuple-element.24.t_ref, f32[2,69,24,128]{3,2,1,0:T(8,128)S(1)} %get-tuple-element.25.e_ref, bf16[1024,1024]{1,0:T(8,128)(2,1)S(1)} %get-tuple-element.26.perm_ref), custom_call_target="tpu_custom_call" | custom-call | flops 16000000 | bytes 6000000 | tf_op jit(solution)/shard_map/advect/pallas_call | solution.py:553
  57.6 5.7 %collective-permute-start.11 = (bf16[256,1024]{1,0:T(8,128)(2,1)S(1)}, bf16[256,1024]{1,0:T(8,128)(2,1)S(1)}, u32[]{:S(2)}, u32[]{:S(2)}) collective-permute-start(bf16[256,1024]{1,0:T(8,128)(2,1)S(1)} %advect.13), channel_id=1, source_target_pairs={{3,0},{4,1},{5,2},{6,3},{7,4},{8,5},{9,6},{10,7},{11,8},{12,9},{13... | collective-permute-start | bytes 1572872 | tf_op jit(solution)/shard_map/ppermute | solution.py:28
  63.3 2.1 %advect.15 = bf16[256,1024]{1,0:T(8,128)(2,1)S(1)} custom-call(bf16[840,128]{1,0:T(8,128)(2,1)S(1)} %collective-permute-done.1.low_ref.msg_ref, f32[8,69,24,128]{3,2,1,0:T(8,128)S(1)} %get-tuple-element.24.t_ref, f32[2,69,24,128]{3,2,1,0:T(8,128)S(1)} %get-tuple-element.25.e_ref, bf16[1024,1024]{1,0:T(8,128)(2,1)S(1)} %get-tuple-element.26.perm_ref), custom_call_target="tpu_custom_call" | custom-call | flops 16000000 | bytes 6000000 | tf_op jit(solution)/shard_map/advect/pallas_call | solution.py:553
  65.4 1.5 %advect.14 = bf16[256,1024]{1,0:T(8,128)(2,1)S(1)} custom-call(bf16[840,128]{1,0:T(8,128)(2,1)S(1)} %collective-permute-done.2.high_ref.msg_ref, f32[8,69,24,128]{3,2,1,0:T(8,128)S(1)} %get-tuple-element.24.t_ref, f32[2,69,24,128]{3,2,1,0:T(8,128)S(1)} %get-tuple-element.25.e_ref, bf16[1024,1024]{1,0:T(8,128)(2,1)S(1)} %get-tuple-element.26.perm_ref), custom_call_target="tpu_custom_call" | custom-call | flops 16000000 | bytes 6000000 | tf_op jit(solution)/shard_map/advect/pallas_call | solution.py:553
  66.9 0.0 collective-permute-done.3.rest_0_
  66.9 0.1 collective-permute-start.12
  67.0 0.0 collective-permute-done.5.rest_1_
  67.0 1.9 %collective-permute-start.13 = (bf16[256,1024]{1,0:T(8,128)(2,1)S(1)}, bf16[256,1024]{1,0:T(8,128)(2,1)S(1)}, u32[]{:S(2)}, u32[]{:S(2)}) collective-permute-start(bf16[256,1024]{1,0:T(8,128)(2,1)S(1)} %advect.15), channel_id=1, source_target_pairs={{1,0},{2,1},{3,2},{4,3},{5,4},{6,5},{7,6},{8,7},{9,8},{10,9},{11,1... | collective-permute-start | bytes 1572872 | tf_op jit(solution)/shard_map/ppermute | solution.py:28
  68.9 0.0 copy-start.2
  68.9 3.3 %advect.12.rest_4_ = bf16[256,1024]{1,0:T(8,128)(2,1)S(1)} custom-call(bf16[520,128]{1,0:T(8,128)(2,1)S(1)} %get-tuple-element.30.msg_ref, f32[8,69,24,128]{3,2,1,0:T(8,128)S(1)} %get-tuple-element.24.t_ref, f32[2,69,24,128]{3,2,1,0:T(8,128)S(1)} %get-tuple-element.25.e_ref, bf16[1024,1024]{1,0:T(8,128)(2,1)S(1)} %get-tuple-element.26.perm_ref), custom_call_target="tpu_custom_call" | custom-call | flops 16000000 | bytes 6000000 | tf_op jit(solution)/shard_map/advect/pallas_call | solution.py:553
  72.3 0.0 collective-permute-done.7.rest_2_
  72.3 10.7 %collective-permute-done.9.rest_3_ = bf16[256,1024]{1,0:T(8,128)(2,1)S(1)} collective-permute-done((bf16[256,1024]{1,0:T(8,128)(2,1)S(1)}, bf16[256,1024]{1,0:T(8,128)(2,1)S(1)}, u32[]{:S(2)}, u32[]{:S(2)}) %collective-permute-start.9) | collective-permute-done | bytes 524320 | tf_op jit(solution)/shard_map/ppermute | solution.py:28
  83.0 0.0 copy-done.2
  83.0 1.8 %early.1 = (f32[2,4160,128]{2,1,0:T(8,128)S(1)}, s32[32]{0:T(128)S(1)}) custom-call(s32[1,2,16]{2,1,0:T(2,128)S(1)} %bitcast.2, bf16[256,1024]{1,0:T(8,128)(2,1)S(1)} %collective-permute-done.3.rest_0_, bf16[256,1024]{1,0:T(8,128)(2,1)S(1)} %collective-permute-done.5.rest_1_, bf16[256,1024]{1,0:T(8,128)(2,1)S(1)} %collective-permute-done.7.rest_2_, ...), custom_call_target="tpu_custom_call" | custom-call | flops 2000000 | bytes 6000000 | tf_op jit(solution)/shard_map/early/pallas_call | solution.py:570
  84.9 0.0 collective-permute-done.11.rest_0_
  84.9 2.4 %collective-permute-done.12.rest_1_ = bf16[256,1024]{1,0:T(8,128)(2,1)S(1)} collective-permute-done((bf16[256,1024]{1,0:T(8,128)(2,1)S(1)}, bf16[256,1024]{1,0:T(8,128)(2,1)S(1)}, u32[]{:S(2)}, u32[]{:S(2)}) %collective-permute-start.12) | collective-permute-done | bytes 524320 | tf_op jit(solution)/shard_map/ppermute | solution.py:28
  87.2 4.6 %collective-permute-done.13.rest_2_ = bf16[256,1024]{1,0:T(8,128)(2,1)S(1)} collective-permute-done((bf16[256,1024]{1,0:T(8,128)(2,1)S(1)}, bf16[256,1024]{1,0:T(8,128)(2,1)S(1)}, u32[]{:S(2)}, u32[]{:S(2)}) %collective-permute-start.13) | collective-permute-done | bytes 524320 | tf_op jit(solution)/shard_map/ppermute | solution.py:28
  91.8 2.2 %late.1 = (bf16[64,64,256]{2,1,0:T(8,128)(2,1)}, f32[2,4160,128]{2,1,0:T(8,128)S(1)}) custom-call(s32[32]{0:T(128)S(1)} %get-tuple-element.31.slot_ref, bf16[256,1024]{1,0:T(8,128)(2,1)S(1)} %collective-permute-done.11.rest_0_, bf16[256,1024]{1,0:T(8,128)(2,1)S(1)} %collective-permute-done.12.rest_1_, ...), custom_call_target="tpu_custom_call", output_to_operand_aliasing={{1}: (4, {})} | custom-call | flops 2000000 | bytes 6000000 | tf_op jit(solution)/shard_map/late/pallas_call | solution.py:585
Async XLA Ops:
  0.0 14.0 %copy-start.1 = (bf16[64,64,128]{2,1,0:T(8,128)(2,1)S(1)}, bf16[64,64,128]{2,1,0:T(8,128)(2,1)}, u32[]{:S(2)}) copy-start(bf16[64,64,128]{2,1,0:T(8,128)(2,1)} %wind_ref.1) | copy-start | bytes 3145732
  0.0 14.0 %copy-start = (bf16[64,64,256]{2,1,0:T(8,128)(2,1)S(1)}, bf16[64,64,256]{2,1,0:T(8,128)(2,1)}, u32[]{:S(2)}) copy-start(bf16[64,64,256]{2,1,0:T(8,128)(2,1)} %tracers_ref.3) | copy-start | bytes 6291460
  2.8 4.7 %collective-permute-start.1 = (bf16[840,128]{1,0:T(8,128)(2,1)S(1)}, bf16[840,128]{1,0:T(8,128)(2,1)S(1)}, u32[]{:S(2)}, u32[]{:S(2)}) collective-permute-start(bf16[840,128]{1,0:T(8,128)(2,1)S(1)} %get-tuple-element.21), channel_id=1, source_target_pairs={{15,0},{0,1},{1,2},{2,3},{3,4},{4,5},{5,6},{6,7},{7,8},{8,9},{9,10... | collective-permute-start | bytes 645128 | tf_op jit(solution)/shard_map/ppermute | solution.py:28
  4.6 9.4 %collective-permute-start.2 = (bf16[840,128]{1,0:T(8,128)(2,1)S(1)}, bf16[840,128]{1,0:T(8,128)(2,1)S(1)}, u32[]{:S(2)}, u32[]{:S(2)}) collective-permute-start(bf16[840,128]{1,0:T(8,128)(2,1)S(1)} %get-tuple-element.22), channel_id=1, source_target_pairs={{1,0},{2,1},{3,2},{4,3},{5,4},{6,5},{7,6},{8,7},{9,8},{10,9},{11,1... | collective-permute-start | bytes 645128 | tf_op jit(solution)/shard_map/ppermute | solution.py:28
  4.6 14.5 %collective-permute-start = (bf16[520,128]{1,0:T(8,128)(2,1)S(1)}, bf16[520,128]{1,0:T(8,128)(2,1)S(1)}, u32[]{:S(2)}, u32[]{:S(2)}) collective-permute-start(bf16[520,128]{1,0:T(8,128)(2,1)S(1)} %get-tuple-element.20), channel_id=1, source_target_pairs={{14,0},{15,1},{0,2},{1,3},{2,4},{3,5},{4,6},{5,7},{6,8},{7,9},{8,1... | collective-permute-start | bytes 399368 | tf_op jit(solution)/shard_map/ppermute | solution.py:28
  5.9 18.7 %collective-permute-start.4 = (bf16[520,128]{1,0:T(8,128)(2,1)S(1)}, bf16[520,128]{1,0:T(8,128)(2,1)S(1)}, u32[]{:S(2)}, u32[]{:S(2)}) collective-permute-start(bf16[520,128]{1,0:T(8,128)(2,1)S(1)} %get-tuple-element.27), channel_id=1, source_target_pairs={{12,0},{13,1},{14,2},{15,3},{0,4},{1,5},{2,6},{3,7},{4,8},{5,9},{6... | collective-permute-start | bytes 399368 | tf_op jit(solution)/shard_map/ppermute | solution.py:28
  21.2 45.7 %collective-permute-start.3 = (bf16[256,1024]{1,0:T(8,128)(2,1)S(1)}, bf16[256,1024]{1,0:T(8,128)(2,1)S(1)}, u32[]{:S(2)}, u32[]{:S(2)}) collective-permute-start(bf16[256,1024]{1,0:T(8,128)(2,1)S(1)} %advect.8), channel_id=1, source_target_pairs={{2,0},{3,1},{4,2},{5,3},{6,4},{7,5},{8,6},{9,7},{10,8},{11,9},{12,... | collective-permute-start | bytes 1572872 | tf_op jit(solution)/shard_map/ppermute | solution.py:28
  26.1 40.9 %collective-permute-start.5 = (bf16[256,1024]{1,0:T(8,128)(2,1)S(1)}, bf16[256,1024]{1,0:T(8,128)(2,1)S(1)}, u32[]{:S(2)}, u32[]{:S(2)}) collective-permute-start(bf16[256,1024]{1,0:T(8,128)(2,1)S(1)} %advect.9), channel_id=1, source_target_pairs={{4,0},{5,1},{6,2},{7,3},{8,4},{9,5},{10,6},{11,7},{12,8},{13,9},{1... | collective-permute-start | bytes 1572872 | tf_op jit(solution)/shard_map/ppermute | solution.py:28
  27.6 22.1 %collective-permute-start.6 = (bf16[520,128]{1,0:T(8,128)(2,1)S(1)}, bf16[520,128]{1,0:T(8,128)(2,1)S(1)}, u32[]{:S(2)}, u32[]{:S(2)}) collective-permute-start(bf16[520,128]{1,0:T(8,128)(2,1)S(1)} %get-tuple-element.28), channel_id=1, source_target_pairs={{2,0},{3,1},{4,2},{5,3},{6,4},{7,5},{8,6},{9,7},{10,8},{11,9},{12,... | collective-permute-start | bytes 399368 | tf_op jit(solution)/shard_map/ppermute | solution.py:28
  28.9 24.2 %collective-permute-start.8 = (bf16[520,128]{1,0:T(8,128)(2,1)S(1)}, bf16[520,128]{1,0:T(8,128)(2,1)S(1)}, u32[]{:S(2)}, u32[]{:S(2)}) collective-permute-start(bf16[520,128]{1,0:T(8,128)(2,1)S(1)} %get-tuple-element.29), channel_id=1, source_target_pairs={{3,0},{4,1},{5,2},{6,3},{7,4},{8,5},{9,6},{10,7},{11,8},{12,9},{13... | collective-permute-start | bytes 399368 | tf_op jit(solution)/shard_map/ppermute | solution.py:28
  29.5 26.6 %collective-permute-start.10 = (bf16[520,128]{1,0:T(8,128)(2,1)S(1)}, bf16[520,128]{1,0:T(8,128)(2,1)S(1)}, u32[]{:S(2)}, u32[]{:S(2)}) collective-permute-start(bf16[520,128]{1,0:T(8,128)(2,1)S(1)} %get-tuple-element.32), channel_id=1, source_target_pairs={{13,0},{14,1},{15,2},{0,3},{1,4},{2,5},{3,6},{4,7},{5,8},{6,9},{7,... | collective-permute-start | bytes 399368 | tf_op jit(solution)/shard_map/ppermute | solution.py:28
  53.0 19.3 %collective-permute-start.7 = (bf16[256,1024]{1,0:T(8,128)(2,1)S(1)}, bf16[256,1024]{1,0:T(8,128)(2,1)S(1)}, u32[]{:S(2)}, u32[]{:S(2)}) collective-permute-start(bf16[256,1024]{1,0:T(8,128)(2,1)S(1)} %advect.10), channel_id=1, source_target_pairs={{14,0},{15,1},{0,2},{1,3},{2,4},{3,5},{4,6},{5,7},{6,8},{7,9},{8,1... | collective-permute-start | bytes 1572872 | tf_op jit(solution)/shard_map/ppermute | solution.py:28
  54.6 28.5 %collective-permute-start.9 = (bf16[256,1024]{1,0:T(8,128)(2,1)S(1)}, bf16[256,1024]{1,0:T(8,128)(2,1)S(1)}, u32[]{:S(2)}, u32[]{:S(2)}) collective-permute-start(bf16[256,1024]{1,0:T(8,128)(2,1)S(1)} %advect.11), channel_id=1, source_target_pairs={{13,0},{14,1},{15,2},{0,3},{1,4},{2,5},{3,6},{4,7},{5,8},{6,9},{7,... | collective-permute-start | bytes 1572872 | tf_op jit(solution)/shard_map/ppermute | solution.py:28
  57.6 27.3 %collective-permute-start.11 = (bf16[256,1024]{1,0:T(8,128)(2,1)S(1)}, bf16[256,1024]{1,0:T(8,128)(2,1)S(1)}, u32[]{:S(2)}, u32[]{:S(2)}) collective-permute-start(bf16[256,1024]{1,0:T(8,128)(2,1)S(1)} %advect.13), channel_id=1, source_target_pairs={{3,0},{4,1},{5,2},{6,3},{7,4},{8,5},{9,6},{10,7},{11,8},{12,9},{13... | collective-permute-start | bytes 1572872 | tf_op jit(solution)/shard_map/ppermute | solution.py:28
  66.9 20.3 %collective-permute-start.12 = (bf16[256,1024]{1,0:T(8,128)(2,1)S(1)}, bf16[256,1024]{1,0:T(8,128)(2,1)S(1)}, u32[]{:S(2)}, u32[]{:S(2)}) collective-permute-start(bf16[256,1024]{1,0:T(8,128)(2,1)S(1)} %advect.14), channel_id=1, source_target_pairs={{15,0},{0,1},{1,2},{2,3},{3,4},{4,5},{5,6},{6,7},{7,8},{8,9},{9,10... | collective-permute-start | bytes 1572872 | tf_op jit(solution)/shard_map/ppermute | solution.py:28
  67.0 24.8 %collective-permute-start.13 = (bf16[256,1024]{1,0:T(8,128)(2,1)S(1)}, bf16[256,1024]{1,0:T(8,128)(2,1)S(1)}, u32[]{:S(2)}, u32[]{:S(2)}) collective-permute-start(bf16[256,1024]{1,0:T(8,128)(2,1)S(1)} %advect.15), channel_id=1, source_target_pairs={{1,0},{2,1},{3,2},{4,3},{5,4},{6,5},{7,6},{8,7},{9,8},{10,9},{11,1... | collective-permute-start | bytes 1572872 | tf_op jit(solution)/shard_map/ppermute | solution.py:28
  68.9 14.1 %copy-start.2 = (s32[1,16,2]{1,2,0:T(2,128)S(1)}, s32[1,16,2]{1,2,0:T(2,128)}, u32[]{:S(2)}) copy-start(s32[1,16,2]{1,2,0:T(2,128)} %param.5) | copy-start | bytes 388
